TPU v7x, 128 devices: a whole 4x4x4 slice. The times are simulated.
128 devices in a mesh: field: 4 (over x_hi, core), slab: 32 (over x_lo, z, y).
Axes of the slice: x: 4 (x_hi: 2, x_lo: 2; x = x_hi * 2 + x_lo), y: 4, z: 4, core: 2. Of those that a mesh axis runs over, the one named last changes fastest.
Arguments:
- velocity_u: float32 [512, 512, 512], P('field', 'slab'), may hold values from -6 to 6
- velocity_v: float32 [512, 512, 512], P('field', 'slab'), may hold values from -6 to 6
- scalar_theta: float32 [512, 512, 512], P('field', 'slab'), may hold values from -6 to 6
Outputs:
- spectrum: float32 [4, 320, 320, 320], P('field', 'slab')
All inputs are finite; a program needn't handle non-finite values.
Results may differ from a plain program's by a relative error of at most 0.00029.
Values sent between devices are 32-bit elements; how exact they have to be, the bound alone decides.
No kernel may reach another device: no remote copies, remote signals or barrier semaphores. Data moves between devices by JAX's collectives and lax.ppermute only.
A program may use at most 128 MiB of HBM per device.

v0:
```python
import functools

import jax
import jax.numpy as jnp
import ml_dtypes
import numpy as np
from jax import lax
from jax.experimental import pallas as pl
from jax.experimental.pallas import tpu as pltpu
from jax.sharding import Mesh
from jax.sharding import PartitionSpec as P


N = 512
KEEP = 160
LANES = 128
XB = 128
YC = 8
DESTS = 16
PAIRS = 5
LAST = (3, 2)
VMEM_LIMIT = 50 * 1024 * 1024


def split_table(table):
    high = table.astype(ml_dtypes.bfloat16)
    low = (table - high.astype(np.float64)).astype(ml_dtypes.bfloat16)
    return np.stack([high, low])


def angles(places, waves):
    return (places * waves % N) * (2.0 * np.pi / N)


def depth_table():
    angle = angles(np.arange(N)[:, None], np.arange(KEEP)[None, :])
    re, im = np.cos(angle), -np.sin(angle)
    zeros = np.zeros((N, 64))
    table = np.concatenate([re[:, :128], im[:, :128], re[:, 128:], im[:, 128:], zeros], axis=1)
    return split_table(table / np.sqrt(N))


def first_table():
    half, e, pair, dest = np.meshgrid(np.arange(2), np.arange(2), np.arange(5), np.arange(16), indexing="ij")
    waves = (half * 160 + dest * 10 + 2 * pair + e - KEEP).reshape(2, KEEP)
    angle = angles(np.arange(2 * XB)[None, None, :], waves[:, :, None]).reshape(2, KEEP, 2, XB)
    table = np.stack([np.cos(angle), np.sin(angle)], axis=1).transpose(0, 1, 3, 2, 4)
    return split_table(table / np.sqrt(N))


def second_table(chunk):
    source, y = np.meshgrid(np.arange(16), np.arange(YC), indexing="ij")
    places = (source * 16 + chunk * YC + y).reshape(-1)
    places = places[None, :] + np.array([[0], [256]])
    waves = np.arange(2 * KEEP) - KEEP
    angle = angles(places[:, None, :], waves[None, :, None])
    table = np.concatenate([np.cos(angle), np.sin(angle)], axis=2)
    return split_table(table / np.sqrt(N))


def halves(value):
    high = value.astype(jnp.bfloat16)
    return high, (value - high.astype(jnp.float32)).astype(jnp.bfloat16)


def dot(a, b):
    return jnp.dot(a, b, preferred_element_type=jnp.float32)


def turn_tail(tail):
    lane = lax.broadcasted_iota(jnp.int32, tail.shape, 1)
    return jnp.where(lane % 64 < 32, pltpu.roll(tail, 96, 1), -pltpu.roll(tail, 32, 1))


def params():
    return pltpu.CompilerParams(vmem_limit_bytes=VMEM_LIMIT)


def depth_kernel(group, keeps, place_ref, u_ref, v_ref, t_ref, table_ref, *out_refs):
    first = place_ref[0] == 0
    squares = place_ref[1] == group
    rows = YC * u_ref.shape[0]

    def load(ref):
        return jnp.concatenate([ref[:, y, :] for y in range(YC)], axis=0)

    u, v, t = load(u_ref), load(v_ref), load(t_ref)
    highs, lows = [], []
    for keep in keeps:
        swap = first if keep == 0 else ~first
        a = jnp.where(squares & swap, v, u)
        high, low = halves(a * jnp.where(squares, a, jnp.where(swap, t, v)))
        highs.append(high)
        lows.append(low)
    high, low = jnp.concatenate(highs, axis=0), jnp.concatenate(lows, axis=0)
    out = dot(jnp.concatenate([high, low, high], axis=1), table_ref[...])
    for i, ref in enumerate(out_refs):
        ref[...] = out[i * rows : (i + 1) * rows].reshape(YC, rows // YC, 384)


def depth_stage(place, u, v, t, table, chunk, group, keeps):
    xb = 32
    block = pl.BlockSpec((xb, YC, N), lambda i: (i, chunk, 0))
    out = pl.BlockSpec((YC, xb, 384), lambda i: (0, i, 0))
    shape = jax.ShapeDtypeStruct((YC, XB, 384), jnp.float32)
    return pl.pallas_call(
        functools.partial(depth_kernel, group, keeps),
        grid=(XB // xb,),
        in_specs=[
            pl.BlockSpec(memory_space=pltpu.SMEM),
            block,
            block,
            block,
            pl.BlockSpec((3 * N, 384), lambda i: (0, 0)),
        ],
        out_specs=[out] * len(keeps),
        out_shape=[shape] * len(keeps),
        compiler_params=params(),
        cost_estimate=pl.CostEstimate(
            flops=len(keeps) * XB * YC * N * 384 * 6, bytes_accessed=9_000_000, transcendentals=0
        ),
    )(place, u, v, t, table)


def first_kernel(blocks, splits, place_ref, own_ref, recv_ref, table_ref, *refs):
    core, high_half, low_half = place_ref[0], place_ref[1], place_ref[3]
    step = pl.program_id(0)
    sides = []
    for y in range(2):
        values = jnp.concatenate([own_ref[y], recv_ref[y]], axis=0)
        re, im, tail = values[:, :128], values[:, 128:256], values[:, 256:]
        sides.append(jnp.concatenate([values, jnp.concatenate([im, -re, turn_tail(tail)], axis=1)], axis=0))
    high, low = halves(jnp.concatenate(sides, axis=1))
    data = jnp.concatenate([high, low, high], axis=0)

    def rows_of(half):
        parts = [[table_ref[part, half, cs, core ^ j] for cs in range(2) for j in range(2)] for part in range(2)]
        return jnp.concatenate(parts[0] + parts[0] + parts[1], axis=1)

    out = dot(jnp.concatenate([rows_of(low_half ^ b) for b in blocks], axis=0), data)
    sign = jnp.where(high_half == 1, -1.0, 1.0)
    index = 0
    for b in range(len(blocks)):
        base = 0
        for pairs in splits:
            ref = refs[index]
            index += 1
            stride = 5 * pairs * YC
            for y in range(2):
                for p in range(pairs):
                    row = b * 160 + (base + p) * DESTS
                    even = out[row : row + DESTS, 384 * y : 384 * (y + 1)]
                    odd = out[row + 80 : row + 80 + DESTS, 384 * y : 384 * (y + 1)] * sign
                    tiles = [even[:, :128], even[:, 128:256], odd[:, :128], odd[:, 128:256]]
                    tiles.append(even[:, 256:] + pltpu.roll(odd[:, 256:], 64, 1))
                    for i, tile in enumerate(tiles):
                        start = (i * pairs + p) * YC + 2 * step + y
                        ref[pl.ds(start, DESTS, stride=stride), :] = tile
            base += pairs


def first_stage(place, own, recv, table, blocks, splits):
    block = pl.BlockSpec((2, XB, 384), lambda i: (i, 0, 0))
    sizes = list(splits) * len(blocks)
    outs = [(DESTS * 5 * pairs * YC, LANES) for pairs in sizes]
    results = pl.pallas_call(
        functools.partial(first_kernel, blocks, splits),
        grid=(YC // 2,),
        in_specs=[
            pl.BlockSpec(memory_space=pltpu.SMEM),
            block,
            block,
            pl.BlockSpec(table.shape, lambda i: (0,) * 6),
        ],
        out_specs=[pl.BlockSpec(shape, lambda i: (0, 0)) for shape in outs],
        out_shape=[jax.ShapeDtypeStruct(shape, jnp.float32) for shape in outs],
        compiler_params=params(),
        cost_estimate=pl.CostEstimate(flops=YC * len(blocks) * 160 * 512 * 384 * 6, bytes_accessed=7_000_000, transcendentals=0),
    )(place, own, recv, table)
    return [r.reshape(DESTS, 5, pairs, YC, LANES) for r, pairs in zip(results, sizes)]


def second_kernel(count, fresh, base, place_ref, table_ref, *refs):
    out_ref = refs[-1]
    left, right = [], []
    for side in range(count):
        t = [refs[side][:, i, 0].reshape(DESTS * YC, LANES) for i in range(5)]
        values = jnp.concatenate(t, axis=1)
        turned = jnp.concatenate([t[1], -t[0], t[3], -t[2], turn_tail(t[4])], axis=1)
        high, low = halves(jnp.concatenate([values, turned], axis=0))
        half = place_ref[3] ^ fresh[side]
        left += [table_ref[0, half], table_ref[0, half], table_ref[1, half]]
        right += [high, low, high]
    out = dot(jnp.concatenate(left, axis=1), jnp.concatenate(right, axis=0))
    tail = out[:, 512:]
    lane = lax.broadcasted_iota(jnp.int32, tail.shape, 1)
    for e in range(2):
        re, im = out[:, 256 * e : 256 * e + 128], out[:, 256 * e + 128 : 256 * e + 256]
        moved = pltpu.roll(im, 32, 1)
        ends = tail if e == 0 else pltpu.roll(tail, 64, 1)
        pieces = [re, jnp.where(lane < 32, ends, moved), jnp.where(lane < 32, moved, ends)[:, :64]]
        for i, piece in enumerate(pieces):
            span = slice(128 * i, min(128 * (i + 1), 320))
            if len(refs) > count + 1:
                piece = piece + refs[count][e, :, span]
            out_ref[e, :, span] = piece

    @pl.when((place_ref[2] == 1) & (pl.program_id(0) + base == 0))
    def _():
        row = out_ref[0, KEEP : KEEP + 1, 0:128]
        first = lax.broadcasted_iota(jnp.int32, row.shape, 1) == 0
        out_ref[0, KEEP : KEEP + 1, 0:128] = jnp.where(first, 0.0, row)


def second_stage(place, table, sides, base, before):
    pairs = sides[0][1].shape[2]
    block = pl.BlockSpec((DESTS, 5, 1, YC, LANES), lambda k: (0, 0, k, 0, 0))
    out = pl.BlockSpec((2, 2 * KEEP, 2 * KEEP), lambda k: (k + base, 0, 0))
    extra = [] if before is None else [before]
    count = len(sides)
    return pl.pallas_call(
        functools.partial(second_kernel, count, [s[0] for s in sides], base),
        grid=(pairs,),
        in_specs=[pl.BlockSpec(memory_space=pltpu.SMEM), pl.BlockSpec(table.shape, lambda k: (0,) * 4)]
        + [block] * count
        + [out] * len(extra),
        out_specs=out,
        out_shape=jax.ShapeDtypeStruct((2 * PAIRS, 2 * KEEP, 2 * KEEP), jnp.float32),
        input_output_aliases={2 + count: 0} if extra else {},
        compiler_params=params(),
        cost_estimate=pl.CostEstimate(
            flops=pairs * count * 320 * 256 * 640 * 6, bytes_accessed=3_000_000 * pairs, transcendentals=0
        ),
    )(place, table, *[s[1] for s in sides], *extra)


def ring(value, flip_high, flip_low):
    moves = [(2 * h + l, 2 * (h ^ flip_high) + (l ^ flip_low)) for h in range(2) for l in range(2)]
    return lax.ppermute(value, ("xh", "xl"), moves)


def spread(value):
    return lax.all_to_all(value, ("z", "y"), split_axis=0, concat_axis=0, tiled=True)


def transform(velocity_u, velocity_v, scalar_theta):
    high, core, low = lax.axis_index("xh"), lax.axis_index("core"), lax.axis_index("xl")
    owns_mean = (low == 1) & (lax.axis_index("z") == 0) & (lax.axis_index("y") == 0)
    place = jnp.stack([core, high, owns_mean.astype(jnp.int32), low]).astype(jnp.int32)

    rows = jnp.asarray(first_table())
    split = depth_table()
    columns = jnp.asarray(np.concatenate([split[0], split[0], split[1]], axis=0))
    fields = (velocity_u, velocity_v, scalar_theta)

    def depth(unit, keeps):
        return depth_stage(place, *fields, columns, int(unit[0]), int(unit[1]), keeps)

    def swap(send):
        return lax.ppermute(send, "core", [(0, 1), (1, 0)])

    def first(own, recv, blocks, splits):
        return first_stage(place, own, recv, rows, blocks, splits)

    def near_ring(values):
        return [ring(value, 1, 0) for value in values]

    def far_ring(unit, values):
        return [ring(value, int(unit[1]), 1) for value in values]

    def gather(a, b):
        return spread(jnp.add(a, b))

    def second(chunk, sides, base, result):
        return second_stage(place, jnp.asarray(second_table(chunk)), sides, base, result)

    (send,) = depth("01", (0,))
    recv = swap(send)
    (own,) = depth("01", (1,))
    near = near_ring(first(own, recv, (0,), (PAIRS,)))
    far = far_ring("01", first(own, recv, (1,), (PAIRS,)))

    send, own = depth("00", (0, 1))
    kept, across = first(own, swap(send), (0, 1), (PAIRS,))
    across = far_ring("00", [across])

    send, own = depth("11", (0, 1))
    parts = first(own, swap(send), (0, 1), LAST)
    near_last = near_ring(parts[:2])
    far_last = far_ring("11", parts[2:])

    send, own = depth("10", (0, 1))
    parts = first(own, swap(send), (0, 1), LAST)
    kept_last = parts[:2]
    across_last = far_ring("10", parts[2:])

    mine = gather(kept, near[0])
    other = gather(across[0], far[0])
    mine_last = [gather(a, b) for a, b in zip(kept_last, near_last)]
    other_last = [gather(a, b) for a, b in zip(across_last, far_last)]

    result = second(0, [(0, mine), (1, other)], 0, None)
    result = second(1, [(0, mine_last[0])], 0, result)
    result = second(1, [(0, mine_last[1])], LAST[0], result)
    result = second(1, [(1, other_last[0])], 0, result)
    result = second(1, [(1, other_last[1])], LAST[0], result)
    return result[None]


def solution(mesh):
    fine = Mesh(mesh.devices.reshape(2, 2, 2, 4, 4), ("xh", "core", "xl", "z", "y"))
    spec = P(("xh", "core"), ("xl", "z", "y"), None)
    out_specs = P(("xh", "core"), ("xl", "z", "y"), None, None)
    return jax.shard_map(transform, mesh=fine, in_specs=(spec,) * 3, out_specs=out_specs, check_vma=False)
```

profile of v0, /device:TPU:22, one launch (start us, length us, event | category | flops | bytes accessed | tf_op | source)
XLA Modules:
  0.0 237.4 jit_solution(12598660549053524782)
XLA Ops:
  0.1 1.3 copy-done
  1.4 7.8 %shard_map.102 = (f32[8,128,384]{2,1,0:T(8,128)S(1)}, f32[8,128,384]{2,1,0:T(8,128)}) custom-call(s32[4]{0:T(128)S(1)} %pad_add_fusion.place_ref, f32[128,16,512]{2,1,0:T(8,128)} %u_ref.9, f32[128,16,512]{2,1,0:T(8,128)} %v_ref.9, f32[128,16,512]{2,1,0:T(8,128)} %t_ref.9, bf16[1536,384]{1,0:T(8,128)(2,1)S(1)} %copy-done), custom_call_target="tpu_custom_call" | custom-call | flops 2415919104 | bytes 9000000 | tf_op jit(solution)/shard_map/pallas_call | solution.py:106
  9.2 7.8 %shard_map.100 = (f32[8,128,384]{2,1,0:T(8,128)S(1)}, f32[8,128,384]{2,1,0:T(8,128)}) custom-call(s32[4]{0:T(128)S(1)} %pad_add_fusion.place_ref, f32[128,16,512]{2,1,0:T(8,128)} %u_ref.9, f32[128,16,512]{2,1,0:T(8,128)} %v_ref.9, f32[128,16,512]{2,1,0:T(8,128)} %t_ref.9, bf16[1536,384]{1,0:T(8,128)(2,1)S(1)} %copy-done), custom_call_target="tpu_custom_call" | custom-call | flops 2415919104 | bytes 9000000 | tf_op jit(solution)/shard_map/pallas_call | solution.py:106
  17.5 6.7 %shard_map.107 = f32[8,128,384]{2,1,0:T(8,128)} custom-call(s32[4]{0:T(128)S(1)} %pad_add_fusion.place_ref, f32[128,16,512]{2,1,0:T(8,128)} %u_ref.9, f32[128,16,512]{2,1,0:T(8,128)} %v_ref.9, f32[128,16,512]{2,1,0:T(8,128)} %t_ref.9, bf16[1536,384]{1,0:T(8,128)(2,1)S(1)} %copy-done), custom_call_target="tpu_custom_call" | custom-call | flops 1207959552 | bytes 9000000 | tf_op jit(solution)/shard_map/pallas_call | solution.py:106
  24.3 1.2 copy-done.18
  25.5 7.0 %shard_map.103 = (f32[1920,128]{1,0:T(8,128)}, f32[1280,128]{1,0:T(8,128)S(1)}, f32[1920,128]{1,0:T(8,128)}, f32[1280,128]{1,0:T(8,128)S(1)}) custom-call(s32[4]{0:T(128)S(1)} %pad_add_fusion.place_ref, f32[8,128,384]{2,1,0:T(8,128)} %get-tuple-element.24.own_ref, f32[8,128,384]{2,1,0:T(8,128)} %copy-done.18, bf16[2,2,2,2,160,128]{5,4,3,2,1,0:T(8,128)(2,1)S(1)} %copy-done.13), custom_call_target="tpu_custom_call" | custom-call | flops 3019898880 | bytes 7000000 | tf_op jit(solution)/shard_map/pallas_call | solution.py:166
  33.3 1.4 collective-permute-start.6
  34.7 1.2 copy-done.17
  35.9 6.7 %shard_map.101 = (f32[1920,128]{1,0:T(8,128)S(1)}, f32[1280,128]{1,0:T(8,128)S(1)}, f32[1920,128]{1,0:T(8,128)}, f32[1280,128]{1,0:T(8,128)S(1)}) custom-call(s32[4]{0:T(128)S(1)} %pad_add_fusion.place_ref, f32[8,128,384]{2,1,0:T(8,128)} %get-tuple-element.21.own_ref, f32[8,128,384]{2,1,0:T(8,128)} %copy-done.17, bf16[2,2,2,2,160,128]{5,4,3,2,1,0:T(8,128)(2,1)S(1)} %copy-done.13), custom_call_target="tpu_custom_call" | custom-call | flops 3019898880 | bytes 7000000 | tf_op jit(solution)/shard_map/pallas_call | solution.py:166
  42.6 0.9 copy-done.10
  43.5 2.7 %collective-permute-start.5 = (f32[16,5,3,8,128]{4,3,2,1,0:T(8,128)}, f32[16,5,3,8,128]{4,3,2,1,0:T(8,128)}, u32[]{:S(2)}, u32[]{:S(2)}) collective-permute-start(f32[16,5,3,8,128]{4,3,2,1,0:T(8,128)} %bitcast.7), channel_id=1, source_target_pairs={{0,80},{16,64},{64,16},{80,0},{1,81},{17,65},{65,17},{81,1},{2,82}... | collective-permute-start | bytes 2949128 | tf_op jit(solution)/shard_map/ppermute | solution.py:239
  46.2 6.3 %collective-permute-done.6 = f32[16,5,2,8,128]{4,3,2,1,0:T(8,128)S(1)} collective-permute-done((f32[16,5,2,8,128]{4,3,2,1,0:T(8,128)S(1)}, f32[16,5,2,8,128]{4,3,2,1,0:T(8,128)S(1)}, u32[]{:S(2)}, u32[]{:S(2)}) %collective-permute-start.6) | collective-permute-done | bytes 655392 | tf_op jit(solution)/shard_map/ppermute | solution.py:239
  52.5 0.9 add.20
  53.4 8.3 %all-to-all-start.2 = ((f32[16,5,2,8,128]{4,3,2,1,0:T(8,128)}), f32[16,5,2,8,128]{4,3,2,1,0:T(8,128)S(1)}, u32[]{:S(2)}, u32[]{:S(2)}) async-start(f32[16,5,2,8,128]{4,3,2,1,0:T(8,128)} %add.20), calls=%async_computation.2 | async-start | bytes 1310720 | tf_op jit(solution)/shard_map/all_to_all | solution.py:243
  61.7 8.2 %shard_map.104 = (f32[8,128,384]{2,1,0:T(8,128)}, f32[8,128,384]{2,1,0:T(8,128)}) custom-call(s32[4]{0:T(128)S(1)} %pad_add_fusion.place_ref, f32[128,16,512]{2,1,0:T(8,128)} %u_ref.9, f32[128,16,512]{2,1,0:T(8,128)} %v_ref.9, f32[128,16,512]{2,1,0:T(8,128)} %t_ref.9, bf16[1536,384]{1,0:T(8,128)(2,1)S(1)} %copy-done.1), custom_call_target="tpu_custom_call" | custom-call | flops 2415919104 | bytes 9000000 | tf_op jit(solution)/shard_map/pallas_call | solution.py:106
  69.9 1.4 collective-permute-start.7
  71.3 1.7 collective-permute-done.5
  73.0 2.6 %add.19 = f32[16,5,3,8,128]{4,3,2,1,0:T(8,128)} add(f32[16,5,3,8,128]{4,3,2,1,0:T(8,128)} %collective-permute-done.4, f32[16,5,3,8,128]{4,3,2,1,0:T(8,128)} %collective-permute-done.5) | non-fusion elementwise | flops 245760 | bytes 2949120 | tf_op jit(solution)/shard_map/add | solution.py:272
  76.5 8.3 %all-to-all-start.1 = ((f32[16,5,3,8,128]{4,3,2,1,0:T(8,128)}), f32[16,5,3,8,128]{4,3,2,1,0:T(8,128)S(1)}, u32[]{:S(2)}, u32[]{:S(2)}) async-start(f32[16,5,3,8,128]{4,3,2,1,0:T(8,128)} %add.19), calls=%async_computation.1 | async-start | bytes 1966080 | tf_op jit(solution)/shard_map/all_to_all | solution.py:243
  84.8 5.9 %shard_map.106.own_ref = f32[8,128,384]{2,1,0:T(8,128)S(1)} custom-call(s32[4]{0:T(128)S(1)} %pad_add_fusion.place_ref, f32[128,16,512]{2,1,0:T(8,128)} %u_ref.9, f32[128,16,512]{2,1,0:T(8,128)} %v_ref.9, f32[128,16,512]{2,1,0:T(8,128)} %t_ref.9, bf16[1536,384]{1,0:T(8,128)(2,1)S(1)} %copy-done.1), custom_call_target="tpu_custom_call" | custom-call | flops 1207959552 | bytes 9000000 | tf_op jit(solution)/shard_map/pallas_call | solution.py:106
  90.7 5.6 %shard_map.108 = f32[3200,128]{1,0:T(8,128)} custom-call(s32[4]{0:T(128)S(1)} %pad_add_fusion.place_ref, f32[8,128,384]{2,1,0:T(8,128)S(1)} %shard_map.106.own_ref, f32[8,128,384]{2,1,0:T(8,128)} %collective-permute-done.9.recv_ref, bf16[2,2,2,2,160,128]{5,4,3,2,1,0:T(8,128)(2,1)S(1)} %copy-done.14), custom_call_target="tpu_custom_call" | custom-call | flops 1509949440 | bytes 7000000 | tf_op jit(solution)/shard_map/pallas_call | solution.py:166
  96.3 1.5 collective-permute-start.10
  97.7 2.4 %add.21 = f32[16,5,3,8,128]{4,3,2,1,0:T(8,128)} add(f32[16,5,3,8,128]{4,3,2,1,0:T(8,128)S(1)} %bitcast.17, f32[16,5,3,8,128]{4,3,2,1,0:T(8,128)} %collective-permute-done.7) | non-fusion elementwise | flops 245760 | bytes 2949120 | tf_op jit(solution)/shard_map/add | solution.py:272
  100.1 7.4 %all-to-all-start.3 = ((f32[16,5,3,8,128]{4,3,2,1,0:T(8,128)}), f32[16,5,3,8,128]{4,3,2,1,0:T(8,128)S(1)}, u32[]{:S(2)}, u32[]{:S(2)}) async-start(f32[16,5,3,8,128]{4,3,2,1,0:T(8,128)} %add.21), calls=%async_computation.3 | async-start | bytes 1966080 | tf_op jit(solution)/shard_map/all_to_all | solution.py:243
  107.5 1.4 copy-done.7
  108.9 7.2 %shard_map.105 = (f32[3200,128]{1,0:T(8,128)}, f32[3200,128]{1,0:T(8,128)}) custom-call(s32[4]{0:T(128)S(1)} %pad_add_fusion.place_ref, f32[8,128,384]{2,1,0:T(8,128)S(1)} %copy-done.7, f32[8,128,384]{2,1,0:T(8,128)} %collective-permute-done.8.recv_ref, bf16[2,2,2,2,160,128]{5,4,3,2,1,0:T(8,128)(2,1)S(1)} %copy-done.15), custom_call_target="tpu_custom_call" | custom-call | flops 3019898880 | bytes 7000000 | tf_op jit(solution)/shard_map/pallas_call | solution.py:166
  116.1 5.4 %shard_map.109 = f32[3200,128]{1,0:T(8,128)} custom-call(s32[4]{0:T(128)S(1)} %pad_add_fusion.place_ref, f32[8,128,384]{2,1,0:T(8,128)S(1)} %copy-done.6, f32[8,128,384]{2,1,0:T(8,128)} %collective-permute-done.9.recv_ref, bf16[2,2,2,2,160,128]{5,4,3,2,1,0:T(8,128)(2,1)S(1)} %copy-done.15), custom_call_target="tpu_custom_call" | custom-call | flops 1509949440 | bytes 7000000 | tf_op jit(solution)/shard_map/pallas_call | solution.py:166
  121.6 2.5 %collective-permute-start.12 = (f32[16,5,5,8,128]{4,3,2,1,0:T(8,128)}, f32[16,5,5,8,128]{4,3,2,1,0:T(8,128)}, u32[]{:S(2)}, u32[]{:S(2)}) collective-permute-start(f32[16,5,5,8,128]{4,3,2,1,0:T(8,128)} %bitcast.25), channel_id=1, source_target_pairs={{0,80},{16,64},{64,16},{80,0},{1,81},{17,65},{65,17},{81,1},{2,82}... | collective-permute-start | bytes 4915208 | tf_op jit(solution)/shard_map/ppermute | solution.py:239
  124.0 12.7 %collective-permute-done.10 = f32[16,5,5,8,128]{4,3,2,1,0:T(8,128)} collective-permute-done((f32[16,5,5,8,128]{4,3,2,1,0:T(8,128)}, f32[16,5,5,8,128]{4,3,2,1,0:T(8,128)}, u32[]{:S(2)}, u32[]{:S(2)}) %collective-permute-start.10) | collective-permute-done | bytes 1638432 | tf_op jit(solution)/shard_map/ppermute | solution.py:239
  136.8 2.8 %add.22 = f32[16,5,5,8,128]{4,3,2,1,0:T(8,128)} add(f32[16,5,5,8,128]{4,3,2,1,0:T(8,128)S(1)} %bitcast.22, f32[16,5,5,8,128]{4,3,2,1,0:T(8,128)} %collective-permute-done.10) | non-fusion elementwise | flops 409600 | bytes 4915200 | tf_op jit(solution)/shard_map/add | solution.py:272
  139.6 7.2 %all-to-all-start.4 = ((f32[16,5,5,8,128]{4,3,2,1,0:T(8,128)}), f32[16,5,5,8,128]{4,3,2,1,0:T(8,128)}, u32[]{:S(2)}, u32[]{:S(2)}) async-start(f32[16,5,5,8,128]{4,3,2,1,0:T(8,128)} %add.22), calls=%async_computation.4 | async-start | bytes 3276800 | tf_op jit(solution)/shard_map/all_to_all | solution.py:243
  146.9 21.3 %collective-permute-done.11 = f32[16,5,5,8,128]{4,3,2,1,0:T(8,128)} collective-permute-done((f32[16,5,5,8,128]{4,3,2,1,0:T(8,128)}, f32[16,5,5,8,128]{4,3,2,1,0:T(8,128)}, u32[]{:S(2)}, u32[]{:S(2)}) %collective-permute-start.11) | collective-permute-done | bytes 1638432 | tf_op jit(solution)/shard_map/ppermute | solution.py:239
  168.2 2.2 collective-permute-done.12
  170.4 3.3 %add.23 = f32[16,5,5,8,128]{4,3,2,1,0:T(8,128)} add(f32[16,5,5,8,128]{4,3,2,1,0:T(8,128)} %collective-permute-done.11, f32[16,5,5,8,128]{4,3,2,1,0:T(8,128)} %collective-permute-done.12) | non-fusion elementwise | flops 409600 | bytes 4915200 | tf_op jit(solution)/shard_map/add | solution.py:272
  173.7 7.4 %all-to-all-start.5 = ((f32[16,5,5,8,128]{4,3,2,1,0:T(8,128)}), f32[16,5,5,8,128]{4,3,2,1,0:T(8,128)}, u32[]{:S(2)}, u32[]{:S(2)}) async-start(f32[16,5,5,8,128]{4,3,2,1,0:T(8,128)} %add.23), calls=%async_computation.5 | async-start | bytes 3276800 | tf_op jit(solution)/shard_map/all_to_all | solution.py:243
  181.1 0.9 collective-permute-start.1
  181.9 1.2 collective-permute-start.3
  183.2 14.1 %collective-permute-done.1 = f32[16,5,2,8,128]{4,3,2,1,0:T(8,128)S(1)} collective-permute-done((f32[16,5,2,8,128]{4,3,2,1,0:T(8,128)S(1)}, f32[16,5,2,8,128]{4,3,2,1,0:T(8,128)S(1)}, u32[]{:S(2)}, u32[]{:S(2)}) %collective-permute-start.1) | collective-permute-done | bytes 655392 | tf_op jit(solution)/shard_map/ppermute | solution.py:239
  197.2 1.7 collective-permute-done.3
  199.0 0.9 add.18
  199.9 3.1 %all-to-all-done.5.refs_1_ = f32[16,5,5,8,128]{4,3,2,1,0:T(8,128)} async-done(((f32[16,5,5,8,128]{4,3,2,1,0:T(8,128)}), f32[16,5,5,8,128]{4,3,2,1,0:T(8,128)}, u32[]{:S(2)}, u32[]{:S(2)}) %all-to-all-start.5) | async-done | bytes 1638432 | tf_op jit(solution)/shard_map/all_to_all | solution.py:243
  203.0 8.0 %all-to-all-start = ((f32[16,5,2,8,128]{4,3,2,1,0:T(8,128)}), f32[16,5,2,8,128]{4,3,2,1,0:T(8,128)}, u32[]{:S(2)}, u32[]{:S(2)}) async-start(f32[16,5,2,8,128]{4,3,2,1,0:T(8,128)} %add.18), calls=%async_computation | async-start | bytes 1310720 | tf_op jit(solution)/shard_map/all_to_all | solution.py:243
  211.0 1.1 copy-done.12
  212.1 8.1 %shard_map.110.refs_1_ = f32[10,320,320]{2,1,0:T(8,128)} custom-call(s32[4]{0:T(128)S(1)} %pad_add_fusion.place_ref, bf16[2,2,320,256]{3,2,1,0:T(8,128)(2,1)S(1)} %copy-done.12, f32[16,5,5,8,128]{4,3,2,1,0:T(8,128)} %all-to-all-done.4.refs_0_, f32[16,5,5,8,128]{4,3,2,1,0:T(8,128)} %all-to-all-done.5.refs_1_), custom_call_target="tpu_custom_call" | custom-call | flops 3145728000 | bytes 15000000 | tf_op jit(solution)/shard_map/pallas_call | solution.py:221
  220.2 5.1 %shard_map.111.refs_1_ = f32[10,320,320]{2,1,0:T(8,128)} custom-call(s32[4]{0:T(128)S(1)} %pad_add_fusion.place_ref, bf16[2,2,320,256]{3,2,1,0:T(8,128)(2,1)S(1)} %copy-done.2, f32[16,5,3,8,128]{4,3,2,1,0:T(8,128)S(1)} %all-to-all-done.3.refs_0_, f32[10,320,320]{2,1,0:T(8,128)} %shard_map.110.refs_1_), custom_call_target="tpu_custom_call", output_to_operand_aliasing={{}: (3, {})} | custom-call | flops 943718400 | bytes 9000000 | tf_op jit(solution)/shard_map/pallas_call | solution.py:221
  225.3 3.5 %shard_map.112.refs_1_ = f32[10,320,320]{2,1,0:T(8,128)} custom-call(s32[4]{0:T(128)S(1)} %pad_add_fusion.place_ref, bf16[2,2,320,256]{3,2,1,0:T(8,128)(2,1)S(1)} %copy-done.2, f32[16,5,2,8,128]{4,3,2,1,0:T(8,128)S(1)} %copy-done.4, f32[10,320,320]{2,1,0:T(8,128)} %shard_map.111.refs_1_), custom_call_target="tpu_custom_call", output_to_operand_aliasing={{}: (3, {})} | custom-call | flops 629145600 | bytes 6000000 | tf_op jit(solution)/shard_map/pallas_call | solution.py:221
  228.7 5.0 %shard_map.113.refs_1_ = f32[10,320,320]{2,1,0:T(8,128)} custom-call(s32[4]{0:T(128)S(1)} %pad_add_fusion.place_ref, bf16[2,2,320,256]{3,2,1,0:T(8,128)(2,1)S(1)} %copy-done.2, f32[16,5,3,8,128]{4,3,2,1,0:T(8,128)S(1)} %all-to-all-done.1.refs_0_, f32[10,320,320]{2,1,0:T(8,128)} %shard_map.112.refs_1_), custom_call_target="tpu_custom_call", output_to_operand_aliasing={{}: (3, {})} | custom-call | flops 943718400 | bytes 9000000 | tf_op jit(solution)/shard_map/pallas_call | solution.py:221
  233.8 3.6 %shard_map.114 = f32[10,320,320]{2,1,0:T(8,128)} custom-call(s32[4]{0:T(128)S(1)} %pad_add_fusion.place_ref, bf16[2,2,320,256]{3,2,1,0:T(8,128)(2,1)S(1)} %copy-done.2, f32[16,5,2,8,128]{4,3,2,1,0:T(8,128)} %all-to-all-done.refs_0_, f32[10,320,320]{2,1,0:T(8,128)} %shard_map.113.refs_1_), custom_call_target="tpu_custom_call", output_to_operand_aliasing={{}: (3, {})} | custom-call | flops 629145600 | bytes 6000000 | tf_op jit(solution)/shard_map/pallas_call | solution.py:221
  (50 shorter events, 2.5 us)
Async XLA Ops:
  0.1 1.3 copy-start
  9.2 15.1 %collective-permute-start.2 = (f32[8,128,384]{2,1,0:T(8,128)S(1)}, f32[8,128,384]{2,1,0:T(8,128)S(1)}, u32[]{:S(2)}, u32[]{:S(2)}) collective-permute-start(f32[8,128,384]{2,1,0:T(8,128)S(1)} %get-tuple-element.25), channel_id=1, source_target_pairs={{0,32},{32,0},{1,33},{33,1},{2,34},{34,2},{3,35},{35,3},{4,36},{36... | collective-permute-start | bytes 4718600 | tf_op jit(solution)/shard_map/ppermute | solution.py:260
  17.0 8.5 %copy-start.13 = (bf16[2,2,2,2,160,128]{5,4,3,2,1,0:T(8,128)(2,1)S(1)}, bf16[2,2,2,2,160,128]{5,4,3,2,1,0:T(8,128)(2,1)}, u32[]{:S(2)}) copy-start(bf16[2,2,2,2,160,128]{5,4,3,2,1,0:T(8,128)(2,1)} %constant.33.clone.table_ref) | copy-start | bytes 1966084
  17.0 17.7 %collective-permute-start = (f32[8,128,384]{2,1,0:T(8,128)S(1)}, f32[8,128,384]{2,1,0:T(8,128)S(1)}, u32[]{:S(2)}, u32[]{:S(2)}) collective-permute-start(f32[8,128,384]{2,1,0:T(8,128)S(1)} %get-tuple-element.22), channel_id=1, source_target_pairs={{0,32},{32,0},{1,33},{33,1},{2,34},{34,2},{3,35},{35,3},{4,36},{36... | collective-permute-start | bytes 4718600 | tf_op jit(solution)/shard_map/ppermute | solution.py:260
  24.2 66.4 %collective-permute-start.9 = (f32[8,128,384]{2,1,0:T(8,128)}, f32[8,128,384]{2,1,0:T(8,128)}, u32[]{:S(2)}, u32[]{:S(2)}) collective-permute-start(f32[8,128,384]{2,1,0:T(8,128)} %shard_map.107), channel_id=1, source_target_pairs={{0,32},{32,0},{1,33},{33,1},{2,34},{34,2},{3,35},{35,3},{4,36},{36... | collective-permute-start | bytes 4718600 | tf_op jit(solution)/shard_map/ppermute | solution.py:260
  24.3 1.2 copy-start.18
  32.5 0.8 copy-start.8
  33.3 19.2 %collective-permute-start.6 = (f32[16,5,2,8,128]{4,3,2,1,0:T(8,128)S(1)}, f32[16,5,2,8,128]{4,3,2,1,0:T(8,128)S(1)}, u32[]{:S(2)}, u32[]{:S(2)}) collective-permute-start(f32[16,5,2,8,128]{4,3,2,1,0:T(8,128)S(1)} %bitcast.21), channel_id=1, source_target_pairs={{0,64},{16,80},{64,0},{80,16},{1,65},{17,81},{65,1},{81,17},{2,66}... | collective-permute-start | bytes 1966088 | tf_op jit(solution)/shard_map/ppermute | solution.py:239
  34.7 1.2 copy-start.17
  42.6 0.9 copy-start.10
  43.5 27.8 %collective-permute-start.4 = (f32[16,5,3,8,128]{4,3,2,1,0:T(8,128)}, f32[16,5,3,8,128]{4,3,2,1,0:T(8,128)}, u32[]{:S(2)}, u32[]{:S(2)}) collective-permute-start(f32[16,5,3,8,128]{4,3,2,1,0:T(8,128)} %bitcast.6), channel_id=1, source_target_pairs={{0,16},{16,0},{64,80},{80,64},{1,17},{17,1},{65,81},{81,65},{2,18}... | collective-permute-start | bytes 2949128 | tf_op jit(solution)/shard_map/ppermute | solution.py:239
  43.5 29.6 %collective-permute-start.5 = (f32[16,5,3,8,128]{4,3,2,1,0:T(8,128)}, f32[16,5,3,8,128]{4,3,2,1,0:T(8,128)}, u32[]{:S(2)}, u32[]{:S(2)}) collective-permute-start(f32[16,5,3,8,128]{4,3,2,1,0:T(8,128)} %bitcast.7), channel_id=1, source_target_pairs={{0,80},{16,64},{64,16},{80,0},{1,81},{17,65},{65,17},{81,1},{2,82}... | collective-permute-start | bytes 2949128 | tf_op jit(solution)/shard_map/ppermute | solution.py:239
  52.5 9.2 %copy-start.1 = (bf16[1536,384]{1,0:T(8,128)(2,1)S(1)}, bf16[1536,384]{1,0:T(8,128)(2,1)}, u32[]{:S(2)}) copy-start(bf16[1536,384]{1,0:T(8,128)(2,1)} %constant.34.clone.table_ref) | copy-start | bytes 3538948
  53.4 22.2 %all-to-all-start.2 = ((f32[16,5,2,8,128]{4,3,2,1,0:T(8,128)}), f32[16,5,2,8,128]{4,3,2,1,0:T(8,128)S(1)}, u32[]{:S(2)}, u32[]{:S(2)}) async-start(f32[16,5,2,8,128]{4,3,2,1,0:T(8,128)} %add.20), calls=%async_computation.2 | async-start | bytes 1310720 | tf_op jit(solution)/shard_map/all_to_all | solution.py:243
  69.9 37.6 %collective-permute-start.8 = (f32[8,128,384]{2,1,0:T(8,128)}, f32[8,128,384]{2,1,0:T(8,128)}, u32[]{:S(2)}, u32[]{:S(2)}) collective-permute-start(f32[8,128,384]{2,1,0:T(8,128)} %get-tuple-element.34), channel_id=1, source_target_pairs={{0,32},{32,0},{1,33},{33,1},{2,34},{34,2},{3,35},{35,3},{4,36},{36... | collective-permute-start | bytes 4718600 | tf_op jit(solution)/shard_map/ppermute | solution.py:260
  69.9 27.9 %collective-permute-start.7 = (f32[16,5,3,8,128]{4,3,2,1,0:T(8,128)}, f32[16,5,3,8,128]{4,3,2,1,0:T(8,128)}, u32[]{:S(2)}, u32[]{:S(2)}) collective-permute-start(f32[16,5,3,8,128]{4,3,2,1,0:T(8,128)} %bitcast.11), channel_id=1, source_target_pairs={{0,64},{16,80},{64,0},{80,16},{1,65},{17,81},{65,1},{81,17},{2,66}... | collective-permute-start | bytes 2949128 | tf_op jit(solution)/shard_map/ppermute | solution.py:239
  75.6 0.9 copy-start.3
  76.5 23.7 %all-to-all-start.1 = ((f32[16,5,3,8,128]{4,3,2,1,0:T(8,128)}), f32[16,5,3,8,128]{4,3,2,1,0:T(8,128)S(1)}, u32[]{:S(2)}, u32[]{:S(2)}) async-start(f32[16,5,3,8,128]{4,3,2,1,0:T(8,128)} %add.19), calls=%async_computation.1 | async-start | bytes 1966080 | tf_op jit(solution)/shard_map/all_to_all | solution.py:243
  84.8 5.9 %copy-start.14 = (bf16[2,2,2,2,160,128]{5,4,3,2,1,0:T(8,128)(2,1)S(1)}, bf16[2,2,2,2,160,128]{5,4,3,2,1,0:T(8,128)(2,1)}, u32[]{:S(2)}) copy-start(bf16[2,2,2,2,160,128]{5,4,3,2,1,0:T(8,128)(2,1)} %constant.33.clone.table_ref) | copy-start | bytes 1966084
  90.6 5.6 %copy-start.5 = (f32[8,128,384]{2,1,0:T(8,128)}, f32[8,128,384]{2,1,0:T(8,128)S(1)}, u32[]{:S(2)}) copy-start(f32[8,128,384]{2,1,0:T(8,128)S(1)} %shard_map.106.own_ref) | copy-start | bytes 4718596
  96.3 40.5 %collective-permute-start.10 = (f32[16,5,5,8,128]{4,3,2,1,0:T(8,128)}, f32[16,5,5,8,128]{4,3,2,1,0:T(8,128)}, u32[]{:S(2)}, u32[]{:S(2)}) collective-permute-start(f32[16,5,5,8,128]{4,3,2,1,0:T(8,128)} %bitcast.23), channel_id=1, source_target_pairs={{0,64},{16,80},{64,0},{80,16},{1,65},{17,81},{65,1},{81,17},{2,66}... | collective-permute-start | bytes 4915208 | tf_op jit(solution)/shard_map/ppermute | solution.py:239
  100.1 7.4 %copy-start.15 = (bf16[2,2,2,2,160,128]{5,4,3,2,1,0:T(8,128)(2,1)S(1)}, bf16[2,2,2,2,160,128]{5,4,3,2,1,0:T(8,128)(2,1)}, u32[]{:S(2)}) copy-start(bf16[2,2,2,2,160,128]{5,4,3,2,1,0:T(8,128)(2,1)} %constant.33.clone.table_ref) | copy-start | bytes 1966084
  100.1 39.5 %all-to-all-start.3 = ((f32[16,5,3,8,128]{4,3,2,1,0:T(8,128)}), f32[16,5,3,8,128]{4,3,2,1,0:T(8,128)S(1)}, u32[]{:S(2)}, u32[]{:S(2)}) async-start(f32[16,5,3,8,128]{4,3,2,1,0:T(8,128)} %add.21), calls=%async_computation.3 | async-start | bytes 1966080 | tf_op jit(solution)/shard_map/all_to_all | solution.py:243
  107.5 1.4 copy-start.7
  108.9 7.2 %copy-start.6 = (f32[8,128,384]{2,1,0:T(8,128)S(1)}, f32[8,128,384]{2,1,0:T(8,128)}, u32[]{:S(2)}) copy-start(f32[8,128,384]{2,1,0:T(8,128)} %copy-done.5) | copy-start | bytes 4718596
  116.1 20.7 %copy-start.16 = (f32[3200,128]{1,0:T(8,128)S(1)}, f32[3200,128]{1,0:T(8,128)}, u32[]{:S(2)}) copy-start(f32[3200,128]{1,0:T(8,128)} %get-tuple-element.35) | copy-start | bytes 4915204
  116.1 52.1 %collective-permute-start.11 = (f32[16,5,5,8,128]{4,3,2,1,0:T(8,128)}, f32[16,5,5,8,128]{4,3,2,1,0:T(8,128)}, u32[]{:S(2)}, u32[]{:S(2)}) collective-permute-start(f32[16,5,5,8,128]{4,3,2,1,0:T(8,128)} %bitcast.24), channel_id=1, source_target_pairs={{0,16},{16,0},{64,80},{80,64},{1,17},{17,1},{65,81},{81,65},{2,18}... | collective-permute-start | bytes 4915208 | tf_op jit(solution)/shard_map/ppermute | solution.py:239
  121.6 48.8 %collective-permute-start.12 = (f32[16,5,5,8,128]{4,3,2,1,0:T(8,128)}, f32[16,5,5,8,128]{4,3,2,1,0:T(8,128)}, u32[]{:S(2)}, u32[]{:S(2)}) collective-permute-start(f32[16,5,5,8,128]{4,3,2,1,0:T(8,128)} %bitcast.25), channel_id=1, source_target_pairs={{0,80},{16,64},{64,16},{80,0},{1,81},{17,65},{65,17},{81,1},{2,82}... | collective-permute-start | bytes 4915208 | tf_op jit(solution)/shard_map/ppermute | solution.py:239
  139.6 34.0 %all-to-all-start.4 = ((f32[16,5,5,8,128]{4,3,2,1,0:T(8,128)}), f32[16,5,5,8,128]{4,3,2,1,0:T(8,128)}, u32[]{:S(2)}, u32[]{:S(2)}) async-start(f32[16,5,5,8,128]{4,3,2,1,0:T(8,128)} %add.22), calls=%async_computation.4 | async-start | bytes 3276800 | tf_op jit(solution)/shard_map/all_to_all | solution.py:243
  173.7 7.4 %copy-start.11 = (f32[1280,128]{1,0:T(8,128)S(1)}, f32[1280,128]{1,0:T(8,128)}, u32[]{:S(2)}) copy-start(f32[1280,128]{1,0:T(8,128)} %copy-done.10) | copy-start | bytes 1966084
  173.7 8.3 %copy-start.9 = (f32[1280,128]{1,0:T(8,128)S(1)}, f32[1280,128]{1,0:T(8,128)}, u32[]{:S(2)}) copy-start(f32[1280,128]{1,0:T(8,128)} %copy-done.8) | copy-start | bytes 1966084
  173.7 29.3 %all-to-all-start.5 = ((f32[16,5,5,8,128]{4,3,2,1,0:T(8,128)}), f32[16,5,5,8,128]{4,3,2,1,0:T(8,128)}, u32[]{:S(2)}, u32[]{:S(2)}) async-start(f32[16,5,5,8,128]{4,3,2,1,0:T(8,128)} %add.23), calls=%async_computation.5 | async-start | bytes 3276800 | tf_op jit(solution)/shard_map/all_to_all | solution.py:243
  181.1 16.2 %collective-permute-start.1 = (f32[16,5,2,8,128]{4,3,2,1,0:T(8,128)S(1)}, f32[16,5,2,8,128]{4,3,2,1,0:T(8,128)S(1)}, u32[]{:S(2)}, u32[]{:S(2)}) collective-permute-start(f32[16,5,2,8,128]{4,3,2,1,0:T(8,128)S(1)} %bitcast.20), channel_id=1, source_target_pairs={{0,16},{16,0},{64,80},{80,64},{1,17},{17,1},{65,81},{81,65},{2,18}... | collective-permute-start | bytes 1966088 | tf_op jit(solution)/shard_map/ppermute | solution.py:239
  181.9 17.0 %collective-permute-start.3 = (f32[16,5,2,8,128]{4,3,2,1,0:T(8,128)S(1)}, f32[16,5,2,8,128]{4,3,2,1,0:T(8,128)S(1)}, u32[]{:S(2)}, u32[]{:S(2)}) collective-permute-start(f32[16,5,2,8,128]{4,3,2,1,0:T(8,128)S(1)} %bitcast.19), channel_id=1, source_target_pairs={{0,80},{16,64},{64,16},{80,0},{1,81},{17,65},{65,17},{81,1},{2,82}... | collective-permute-start | bytes 1966088 | tf_op jit(solution)/shard_map/ppermute | solution.py:239
  203.0 30.8 %all-to-all-start = ((f32[16,5,2,8,128]{4,3,2,1,0:T(8,128)}), f32[16,5,2,8,128]{4,3,2,1,0:T(8,128)}, u32[]{:S(2)}, u32[]{:S(2)}) async-start(f32[16,5,2,8,128]{4,3,2,1,0:T(8,128)} %add.18), calls=%async_computation | async-start | bytes 1310720 | tf_op jit(solution)/shard_map/all_to_all | solution.py:243
  211.0 1.1 copy-start.12
  212.1 8.1 %copy-start.2 = (bf16[2,2,320,256]{3,2,1,0:T(8,128)(2,1)S(1)}, bf16[2,2,320,256]{3,2,1,0:T(8,128)(2,1)}, u32[]{:S(2)}) copy-start(bf16[2,2,320,256]{3,2,1,0:T(8,128)(2,1)} %constant.36.clone.table_ref) | copy-start | bytes 1966084
  220.2 5.1 %copy-start.4 = (f32[16,5,2,8,128]{4,3,2,1,0:T(8,128)S(1)}, f32[16,5,2,8,128]{4,3,2,1,0:T(8,128)}, u32[]{:S(2)}) copy-start(f32[16,5,2,8,128]{4,3,2,1,0:T(8,128)} %copy-done.3) | copy-start | bytes 1966084
where the time goes:
time: 239 us; the launch traced here: 237 us
  Pallas kernels  93.6 us (39%)
  waiting for transfers between devices  63.3 us (26%)
  starting transfers between devices  58.7 us (25%)
  other arithmetic  13 us (5%)
  local copies, waits for them, and re-layouts  8.67 us (4%)
    ppermute x9, waiting for transfers between devices, ring(): return lax.ppermute(value, ('xh', 'xl'), moves)  60.1 us
    all_to_all x6, starting transfers between devices, spread(): lax.all_to_all(value, ('z', 'y'), split_axis=0, concat_axis=0, tiled=True)  46.5 us
    pallas_call x5, Pallas kernels, depth_stage(): pl.pallas_call(functools.partial(depth_kernel, group, keeps), grid=(XB //...  36.4 us
    pallas_call x5, Pallas kernels, first_stage(): pl.pallas_call(functools.partial(first_kernel, blocks, splits), grid=(YC...  32 us
    pallas_call x5, Pallas kernels, second_stage(): pl.pallas_call(functools.partial(second_kernel, count, [s[0] for s in sid...  25.3 us
    add x6, other arithmetic, gather(): return spread(jnp.add(a, b))  12.9 us
    ppermute x9, starting transfers between devices, ring(): return lax.ppermute(value, ('xh', 'xl'), moves)  11.6 us
    unnamed x38, local copies, waits for them, and re-layouts  8.67 us
  transfers between devices with their start and end apart: 19, of which 8 were waited for; matrix products, arithmetic and copies ran while one was open for 5% of the time, Pallas kernels for 35%

commit v1 on v0

--- a/solution.py
+++ b/solution.py
@@ -184,7 +184,11 @@
     out_ref = refs[-1]
     left, right = [], []
     for side in range(count):
-        t = [refs[side][:, i, 0].reshape(DESTS * YC, LANES) for i in range(5)]
+        if len(refs[side].shape) == 5:
+            t = [refs[side][:, i, 0].reshape(DESTS * YC, LANES) for i in range(5)]
+        else:
+            steps = [((place_ref[4] - z) & 3, (place_ref[5] - y) & 3) for z in range(4) for y in range(4)]
+            t = [jnp.concatenate([refs[side][e, d, i, 0] for e, d in steps], axis=0) for i in range(5)]
         values = jnp.concatenate(t, axis=1)
         turned = jnp.concatenate([t[1], -t[0], t[3], -t[2], turn_tail(t[4])], axis=1)
         high, low = halves(jnp.concatenate([values, turned], axis=0))
@@ -215,6 +219,7 @@
 def second_stage(place, table, sides, base, before):
     pairs = sides[0][1].shape[2]
     block = pl.BlockSpec((DESTS, 5, 1, YC, LANES), lambda k: (0, 0, k, 0, 0))
+    stepped = pl.BlockSpec((4, 4, 5, 1, YC, LANES), lambda k: (0, 0, 0, k, 0, 0))
     out = pl.BlockSpec((2, 2 * KEEP, 2 * KEEP), lambda k: (k + base, 0, 0))
     extra = [] if before is None else [before]
     count = len(sides)
@@ -222,7 +227,7 @@
         functools.partial(second_kernel, count, [s[0] for s in sides], base),
         grid=(pairs,),
         in_specs=[pl.BlockSpec(memory_space=pltpu.SMEM), pl.BlockSpec(table.shape, lambda k: (0,) * 4)]
-        + [block] * count
+        + [block if s[1].ndim == 5 else stepped for s in sides]
         + [out] * len(extra),
         out_specs=out,
         out_shape=jax.ShapeDtypeStruct((2 * PAIRS, 2 * KEEP, 2 * KEEP), jnp.float32),
@@ -246,7 +251,8 @@
 def transform(velocity_u, velocity_v, scalar_theta):
     high, core, low = lax.axis_index("xh"), lax.axis_index("core"), lax.axis_index("xl")
     owns_mean = (low == 1) & (lax.axis_index("z") == 0) & (lax.axis_index("y") == 0)
-    place = jnp.stack([core, high, owns_mean.astype(jnp.int32), low]).astype(jnp.int32)
+    z_at, y_at = lax.axis_index("z"), lax.axis_index("y")
+    place = jnp.stack([core, high, owns_mean.astype(jnp.int32), low, z_at, y_at]).astype(jnp.int32)
 
     rows = jnp.asarray(first_table())
     split = depth_table()
@@ -270,6 +276,20 @@
 
     def gather(a, b):
         return spread(jnp.add(a, b))
+
+    def pick(value, at, axis):
+        return lax.dynamic_index_in_dim(value, at & 3, axis, keepdims=False)
+
+    def shift(value, axis, step):
+        return lax.ppermute(value, axis, [(i, (i + step) % 4) for i in range(4)])
+
+    def stepwise(a, b):
+        a, b = (value.reshape(4, 4, *value.shape[1:]) for value in (a, b))
+        blocks = [pick(a, y_at + d, 1) + pick(b, y_at + d, 1) for d in range(4)]
+        blocks = [block if d == 0 else shift(block, "y", d) for d, block in enumerate(blocks)]
+        groups = [jnp.stack([pick(block, z_at + e, 0) for block in blocks]) for e in range(4)]
+        groups = [group if e == 0 else shift(group, "z", e) for e, group in enumerate(groups)]
+        return jnp.stack(groups)
 
     def second(chunk, sides, base, result):
         return second_stage(place, jnp.asarray(second_table(chunk)), sides, base, result)
@@ -295,7 +315,7 @@
     across_last = far_ring("10", parts[2:])
 
     mine = gather(kept, near[0])
-    other = gather(across[0], far[0])
+    other = stepwise(across[0], far[0])
     mine_last = [gather(a, b) for a, b in zip(kept_last, near_last)]
     other_last = [gather(a, b) for a, b in zip(across_last, far_last)]
 

time: 239 us -> 281 us (1.18)
  the two profiles are of different devices: /device:TPU:22 before, /device:TPU:1 now
where the time goes in v1:
time: 281 us; the launch traced here: 280 us
  waiting for transfers between devices  104 us (37%)
  Pallas kernels  92.5 us (33%)
  starting transfers between devices  57 us (20%)
  other arithmetic  17.4 us (6%)
  local copies, waits for them, and re-layouts  8.19 us (3%)
    ppermute x9, waiting for transfers between devices, ring(): return lax.ppermute(value, ('xh', 'xl'), moves)  54.2 us
    ppermute x6, waiting for transfers between devices, shift(): return lax.ppermute(value, axis, [(i, (i + step) % 4) for i in range(4)])  50.2 us
    pallas_call x5, Pallas kernels, depth_stage(): pl.pallas_call(functools.partial(depth_kernel, group, keeps), grid=(XB //...  36.3 us
    all_to_all x5, starting transfers between devices, spread(): lax.all_to_all(value, ('z', 'y'), split_axis=0, concat_axis=0, tiled=True)  32.4 us
    pallas_call x5, Pallas kernels, first_stage(): pl.pallas_call(functools.partial(first_kernel, blocks, splits), grid=(YC...  31.5 us
    pallas_call x5, Pallas kernels, second_stage(): pl.pallas_call(functools.partial(second_kernel, count, [s[0] for s in sid...  24.6 us
    ppermute x9, starting transfers between devices, ring(): return lax.ppermute(value, ('xh', 'xl'), moves)  12.8 us
    ppermute x6, starting transfers between devices, shift(): return lax.ppermute(value, axis, [(i, (i + step) % 4) for i in range(4)])  9.85 us
  transfers between devices with their start and end apart: 24, of which 7 were waited for; matrix products, arithmetic and copies ran while one was open for 7% of the time, Pallas kernels for 29%

profile of v1, /device:TPU:1, one launch (start us, length us, event | category | flops | bytes accessed | tf_op | source)
XLA Modules:
  0.0 279.8 jit_solution(2644278190430001655)
XLA Ops:
  0.1 1.3 copy-done
  1.4 7.9 %shard_map.102 = (f32[8,128,384]{2,1,0:T(8,128)S(1)}, f32[8,128,384]{2,1,0:T(8,128)}) custom-call(s32[6]{0:T(128)S(1)} %stack.74.place_ref, f32[128,16,512]{2,1,0:T(8,128)} %u_ref.9, f32[128,16,512]{2,1,0:T(8,128)} %v_ref.9, f32[128,16,512]{2,1,0:T(8,128)} %t_ref.9, bf16[1536,384]{1,0:T(8,128)(2,1)S(1)} %copy-done), custom_call_target="tpu_custom_call" | custom-call | flops 2415919104 | bytes 9000000 | tf_op jit(solution)/shard_map/pallas_call | solution.py:106
  9.2 1.4 collective-permute-start.2
  10.6 7.8 %shard_map.100 = (f32[8,128,384]{2,1,0:T(8,128)S(1)}, f32[8,128,384]{2,1,0:T(8,128)}) custom-call(s32[6]{0:T(128)S(1)} %stack.74.place_ref, f32[128,16,512]{2,1,0:T(8,128)} %u_ref.9, f32[128,16,512]{2,1,0:T(8,128)} %v_ref.9, f32[128,16,512]{2,1,0:T(8,128)} %t_ref.9, bf16[1536,384]{1,0:T(8,128)(2,1)S(1)} %copy-done), custom_call_target="tpu_custom_call" | custom-call | flops 2415919104 | bytes 9000000 | tf_op jit(solution)/shard_map/pallas_call | solution.py:106
  18.5 6.7 %shard_map.107 = f32[8,128,384]{2,1,0:T(8,128)} custom-call(s32[6]{0:T(128)S(1)} %stack.74.place_ref, f32[128,16,512]{2,1,0:T(8,128)} %u_ref.9, f32[128,16,512]{2,1,0:T(8,128)} %v_ref.9, f32[128,16,512]{2,1,0:T(8,128)} %t_ref.9, bf16[1536,384]{1,0:T(8,128)(2,1)S(1)} %copy-done), custom_call_target="tpu_custom_call" | custom-call | flops 1207959552 | bytes 9000000 | tf_op jit(solution)/shard_map/pallas_call | solution.py:106
  25.6 8.2 %shard_map.104 = (f32[8,128,384]{2,1,0:T(8,128)}, f32[8,128,384]{2,1,0:T(8,128)}) custom-call(s32[6]{0:T(128)S(1)} %stack.74.place_ref, f32[128,16,512]{2,1,0:T(8,128)} %u_ref.9, f32[128,16,512]{2,1,0:T(8,128)} %v_ref.9, f32[128,16,512]{2,1,0:T(8,128)} %t_ref.9, bf16[1536,384]{1,0:T(8,128)(2,1)S(1)} %copy-done), custom_call_target="tpu_custom_call" | custom-call | flops 2415919104 | bytes 9000000 | tf_op jit(solution)/shard_map/pallas_call | solution.py:106
  33.9 1.2 copy-done.15
  35.1 7.0 %shard_map.103 = (f32[1920,128]{1,0:T(8,128)}, f32[1280,128]{1,0:T(8,128)S(1)}, f32[1920,128]{1,0:T(8,128)}, f32[1280,128]{1,0:T(8,128)S(1)}) custom-call(s32[6]{0:T(128)S(1)} %stack.74.place_ref, f32[8,128,384]{2,1,0:T(8,128)} %get-tuple-element.24.own_ref, f32[8,128,384]{2,1,0:T(8,128)} %copy-done.15, bf16[2,2,2,2,160,128]{5,4,3,2,1,0:T(8,128)(2,1)S(1)} %copy-done.10), custom_call_target="tpu_custom_call" | custom-call | flops 3019898880 | bytes 7000000 | tf_op jit(solution)/shard_map/pallas_call | solution.py:166
  42.9 2.9 %collective-permute-start.6 = (f32[16,5,2,8,128]{4,3,2,1,0:T(8,128)S(1)}, f32[16,5,2,8,128]{4,3,2,1,0:T(8,128)S(1)}, u32[]{:S(2)}, u32[]{:S(2)}) collective-permute-start(f32[16,5,2,8,128]{4,3,2,1,0:T(8,128)S(1)} %bitcast.62), channel_id=1, source_target_pairs={{0,64},{16,80},{64,0},{80,16},{1,65},{17,81},{65,1},{81,17},{2,66}... | collective-permute-start | bytes 1966088 | tf_op jit(solution)/shard_map/ppermute | solution.py:244
  45.7 1.1 copy-done.14
  46.9 6.7 %shard_map.101 = (f32[1920,128]{1,0:T(8,128)S(1)}, f32[1280,128]{1,0:T(8,128)S(1)}, f32[1920,128]{1,0:T(8,128)}, f32[1280,128]{1,0:T(8,128)S(1)}) custom-call(s32[6]{0:T(128)S(1)} %stack.74.place_ref, f32[8,128,384]{2,1,0:T(8,128)} %get-tuple-element.21.own_ref, f32[8,128,384]{2,1,0:T(8,128)} %copy-done.14, bf16[2,2,2,2,160,128]{5,4,3,2,1,0:T(8,128)(2,1)S(1)} %copy-done.10), custom_call_target="tpu_custom_call" | custom-call | flops 3019898880 | bytes 7000000 | tf_op jit(solution)/shard_map/pallas_call | solution.py:166
  54.5 5.8 %collective-permute-done.6 = f32[16,5,2,8,128]{4,3,2,1,0:T(8,128)S(1)} collective-permute-done((f32[16,5,2,8,128]{4,3,2,1,0:T(8,128)S(1)}, f32[16,5,2,8,128]{4,3,2,1,0:T(8,128)S(1)}, u32[]{:S(2)}, u32[]{:S(2)}) %collective-permute-start.6) | collective-permute-done | bytes 655392 | tf_op jit(solution)/shard_map/ppermute | solution.py:244
  61.2 7.9 %all-to-all-start.2 = ((f32[16,5,2,8,128]{4,3,2,1,0:T(8,128)}), f32[16,5,2,8,128]{4,3,2,1,0:T(8,128)S(1)}, u32[]{:S(2)}, u32[]{:S(2)}) async-start(f32[16,5,2,8,128]{4,3,2,1,0:T(8,128)} %add.111), calls=%async_computation.2 | async-start | bytes 1310720 | tf_op jit(solution)/shard_map/all_to_all | solution.py:248
  69.1 5.8 %shard_map.106.own_ref = f32[8,128,384]{2,1,0:T(8,128)S(1)} custom-call(s32[6]{0:T(128)S(1)} %stack.74.place_ref, f32[128,16,512]{2,1,0:T(8,128)} %u_ref.9, f32[128,16,512]{2,1,0:T(8,128)} %v_ref.9, f32[128,16,512]{2,1,0:T(8,128)} %t_ref.9, bf16[1536,384]{1,0:T(8,128)(2,1)S(1)} %copy-done.1), custom_call_target="tpu_custom_call" | custom-call | flops 1207959552 | bytes 9000000 | tf_op jit(solution)/shard_map/pallas_call | solution.py:106
  74.9 2.8 %collective-permute-start.7 = (f32[16,5,3,8,128]{4,3,2,1,0:T(8,128)}, f32[16,5,3,8,128]{4,3,2,1,0:T(8,128)}, u32[]{:S(2)}, u32[]{:S(2)}) collective-permute-start(f32[16,5,3,8,128]{4,3,2,1,0:T(8,128)} %bitcast.13), channel_id=1, source_target_pairs={{0,64},{16,80},{64,0},{80,16},{1,65},{17,81},{65,1},{81,17},{2,66}... | collective-permute-start | bytes 2949128 | tf_op jit(solution)/shard_map/ppermute | solution.py:244
  77.8 5.3 %shard_map.109 = f32[3200,128]{1,0:T(8,128)} custom-call(s32[6]{0:T(128)S(1)} %stack.74.place_ref, f32[8,128,384]{2,1,0:T(8,128)S(1)} %shard_map.106.own_ref, f32[8,128,384]{2,1,0:T(8,128)} %collective-permute-done.9.recv_ref, bf16[2,2,2,2,160,128]{5,4,3,2,1,0:T(8,128)(2,1)S(1)} %copy-done.11), custom_call_target="tpu_custom_call" | custom-call | flops 1509949440 | bytes 7000000 | tf_op jit(solution)/shard_map/pallas_call | solution.py:166
  83.9 2.6 add.110
  86.5 7.1 %all-to-all-start.1 = ((f32[16,5,3,8,128]{4,3,2,1,0:T(8,128)}), f32[16,5,3,8,128]{4,3,2,1,0:T(8,128)S(1)}, u32[]{:S(2)}, u32[]{:S(2)}) async-start(f32[16,5,3,8,128]{4,3,2,1,0:T(8,128)} %add.110), calls=%async_computation.1 | async-start | bytes 1966080 | tf_op jit(solution)/shard_map/all_to_all | solution.py:248
  93.6 1.4 copy-done.5
  95.0 7.3 %shard_map.105 = (f32[3200,128]{1,0:T(8,128)}, f32[3200,128]{1,0:T(8,128)}) custom-call(s32[6]{0:T(128)S(1)} %stack.74.place_ref, f32[8,128,384]{2,1,0:T(8,128)S(1)} %copy-done.5, f32[8,128,384]{2,1,0:T(8,128)} %collective-permute-done.8.recv_ref, bf16[2,2,2,2,160,128]{5,4,3,2,1,0:T(8,128)(2,1)S(1)} %copy-done.12), custom_call_target="tpu_custom_call" | custom-call | flops 3019898880 | bytes 7000000 | tf_op jit(solution)/shard_map/pallas_call | solution.py:166
  102.2 1.2 collective-permute-start.11
  103.4 5.3 %shard_map.108 = f32[3200,128]{1,0:T(8,128)} custom-call(s32[6]{0:T(128)S(1)} %stack.74.place_ref, f32[8,128,384]{2,1,0:T(8,128)S(1)} %copy-done.4, f32[8,128,384]{2,1,0:T(8,128)} %collective-permute-done.9.recv_ref, bf16[2,2,2,2,160,128]{5,4,3,2,1,0:T(8,128)(2,1)S(1)} %copy-done.12), custom_call_target="tpu_custom_call" | custom-call | flops 1509949440 | bytes 7000000 | tf_op jit(solution)/shard_map/pallas_call | solution.py:166
  108.7 2.5 collective-permute-start.10
  111.2 2.3 add.112
  113.5 6.6 %all-to-all-start.3 = ((f32[16,5,3,8,128]{4,3,2,1,0:T(8,128)}), f32[16,5,3,8,128]{4,3,2,1,0:T(8,128)S(1)}, u32[]{:S(2)}, u32[]{:S(2)}) async-start(f32[16,5,3,8,128]{4,3,2,1,0:T(8,128)} %add.112), calls=%async_computation.3 | async-start | bytes 1966080 | tf_op jit(solution)/shard_map/all_to_all | solution.py:248
  120.1 18.9 %collective-permute-done.12 = f32[16,5,5,8,128]{4,3,2,1,0:T(8,128)} collective-permute-done((f32[16,5,5,8,128]{4,3,2,1,0:T(8,128)}, f32[16,5,5,8,128]{4,3,2,1,0:T(8,128)}, u32[]{:S(2)}, u32[]{:S(2)}) %collective-permute-start.12) | collective-permute-done | bytes 1638432 | tf_op jit(solution)/shard_map/ppermute | solution.py:244
  139.1 2.9 %fusion.2 = (f32[4,5,5,8,128]{4,3,2,1,0:T(8,128)}, f32[4,5,5,8,128]{4,3,2,1,0:T(8,128)}, f32[4,5,5,8,128]{4,3,2,1,0:T(8,128)}) fusion(f32[4,4,5,5,8,128]{5,4,3,2,1,0:T(8,128)} %bitcast.19, s32[]{:T(128)S(6)} %select_n.44, f32[4,4,5,5,8,128]{5,4,3,2,1,0:T(8,128)} %bitcast.17, s32[]{:T(128)S(6)} %select_n.45, s32[]{:T(128)S(6)} %select_n.46), kind=kLoop, calls=%fused_computation.10 | loop fusion | flops 307200 | bytes 3686412 | tf_op jit(solution)/shard_map/add | solution.py:288
  141.9 3.2 %collective-permute-start.15 = (f32[4,5,5,8,128]{4,3,2,1,0:T(8,128)}, f32[4,5,5,8,128]{4,3,2,1,0:T(8,128)}, u32[]{:S(2)}, u32[]{:S(2)}) collective-permute-start(f32[4,5,5,8,128]{4,3,2,1,0:T(8,128)} %get-tuple-element.39), channel_id=1, source_target_pairs={{0,3},{1,0},{2,1},{3,2},{4,7},{5,4},{6,5},{7,6},{8,11},{9,8},{10,9... | collective-permute-start | bytes 1228808 | tf_op jit(solution)/shard_map/ppermute | solution.py:284
  145.1 29.5 %collective-permute-done.10 = f32[16,5,5,8,128]{4,3,2,1,0:T(8,128)} collective-permute-done((f32[16,5,5,8,128]{4,3,2,1,0:T(8,128)}, f32[16,5,5,8,128]{4,3,2,1,0:T(8,128)}, u32[]{:S(2)}, u32[]{:S(2)}) %collective-permute-start.10) | collective-permute-done | bytes 1638432 | tf_op jit(solution)/shard_map/ppermute | solution.py:244
  174.6 2.8 %add.113 = f32[16,5,5,8,128]{4,3,2,1,0:T(8,128)} add(f32[16,5,5,8,128]{4,3,2,1,0:T(8,128)S(1)} %bitcast.63, f32[16,5,5,8,128]{4,3,2,1,0:T(8,128)} %collective-permute-done.10) | non-fusion elementwise | flops 409600 | bytes 4915200 | tf_op jit(solution)/shard_map/add | solution.py:278
  177.4 6.6 %all-to-all-start.4 = ((f32[16,5,5,8,128]{4,3,2,1,0:T(8,128)}), f32[16,5,5,8,128]{4,3,2,1,0:T(8,128)}, u32[]{:S(2)}, u32[]{:S(2)}) async-start(f32[16,5,5,8,128]{4,3,2,1,0:T(8,128)} %add.113), calls=%async_computation.4 | async-start | bytes 3276800 | tf_op jit(solution)/shard_map/all_to_all | solution.py:248
  184.0 2.8 %collective-permute-start.14 = (f32[4,5,5,8,128]{4,3,2,1,0:T(8,128)}, f32[4,5,5,8,128]{4,3,2,1,0:T(8,128)}, u32[]{:S(2)}, u32[]{:S(2)}) collective-permute-start(f32[4,5,5,8,128]{4,3,2,1,0:T(8,128)} %get-tuple-element.38), channel_id=1, source_target_pairs={{0,2},{1,3},{2,0},{3,1},{4,6},{5,7},{6,4},{7,5},{8,10},{9,11},{10,... | collective-permute-start | bytes 1228808 | tf_op jit(solution)/shard_map/ppermute | solution.py:284
  188.7 1.2 dynamic-slice_add_fusion
  190.0 1.1 constant_dynamic-slice_fusion.6
  191.1 19.3 %collective-permute-done.14 = f32[4,5,5,8,128]{4,3,2,1,0:T(8,128)} collective-permute-done((f32[4,5,5,8,128]{4,3,2,1,0:T(8,128)}, f32[4,5,5,8,128]{4,3,2,1,0:T(8,128)}, u32[]{:S(2)}, u32[]{:S(2)}) %collective-permute-start.14) | collective-permute-done | bytes 409632 | tf_op jit(solution)/shard_map/ppermute | solution.py:284
  210.3 1.1 constant_dynamic-slice_fusion.8
  211.4 10.8 %collective-permute-done.13 = f32[4,5,5,8,128]{4,3,2,1,0:T(8,128)S(1)} collective-permute-done((f32[4,5,5,8,128]{4,3,2,1,0:T(8,128)}, f32[4,5,5,8,128]{4,3,2,1,0:T(8,128)S(1)}, u32[]{:S(2)}, u32[]{:S(2)}) %collective-permute-start.13) | collective-permute-done | bytes 409632 | tf_op jit(solution)/shard_map/ppermute | solution.py:284
  223.1 2.1 collective-permute-start.18
  228.3 0.9 add.109
  229.2 4.3 %all-to-all-start = ((f32[16,5,2,8,128]{4,3,2,1,0:T(8,128)}), f32[16,5,2,8,128]{4,3,2,1,0:T(8,128)}, u32[]{:S(2)}, u32[]{:S(2)}) async-start(f32[16,5,2,8,128]{4,3,2,1,0:T(8,128)} %add.109), calls=%async_computation | async-start | bytes 1310720 | tf_op jit(solution)/shard_map/all_to_all | solution.py:248
  233.5 3.5 %collective-permute-done.17 = f32[4,5,5,8,128]{4,3,2,1,0:T(8,128)} collective-permute-done((f32[4,5,5,8,128]{4,3,2,1,0:T(8,128)}, f32[4,5,5,8,128]{4,3,2,1,0:T(8,128)}, u32[]{:S(2)}, u32[]{:S(2)}) %collective-permute-start.17) | collective-permute-done | bytes 409632 | tf_op jit(solution)/shard_map/ppermute | solution.py:284
  237.0 16.6 %collective-permute-done.16 = f32[4,5,5,8,128]{4,3,2,1,0:T(8,128)} collective-permute-done((f32[4,5,5,8,128]{4,3,2,1,0:T(8,128)}, f32[4,5,5,8,128]{4,3,2,1,0:T(8,128)}, u32[]{:S(2)}, u32[]{:S(2)}) %collective-permute-start.16) | collective-permute-done | bytes 409632 | tf_op jit(solution)/shard_map/ppermute | solution.py:284
  253.7 1.4 pad_maximum_fusion.refs_1_
  255.1 7.6 %shard_map.110.refs_1_ = f32[10,320,320]{2,1,0:T(8,128)} custom-call(s32[6]{0:T(128)S(1)} %stack.74.place_ref, bf16[2,2,320,256]{3,2,1,0:T(8,128)(2,1)S(1)} %copy-done.9, f32[16,5,5,8,128]{4,3,2,1,0:T(8,128)} %all-to-all-done.4.refs_0_, f32[4,4,5,5,8,128]{5,4,3,2,1,0:T(8,128)S(1)} %pad_maximum_fusion.refs_1_), custom_call_target="tpu_custom_call" | custom-call | flops 3145728000 | bytes 15000000 | tf_op jit(solution)/shard_map/pallas_call | solution.py:226
  262.7 5.0 %shard_map.111.refs_1_ = f32[10,320,320]{2,1,0:T(8,128)} custom-call(s32[6]{0:T(128)S(1)} %stack.74.place_ref, bf16[2,2,320,256]{3,2,1,0:T(8,128)(2,1)S(1)} %copy-done.2, f32[16,5,3,8,128]{4,3,2,1,0:T(8,128)S(1)} %all-to-all-done.3.refs_0_, f32[10,320,320]{2,1,0:T(8,128)} %shard_map.110.refs_1_), custom_call_target="tpu_custom_call", output_to_operand_aliasing={{}: (3, {})} | custom-call | flops 943718400 | bytes 9000000 | tf_op jit(solution)/shard_map/pallas_call | solution.py:226
  267.7 3.5 %shard_map.112.refs_1_ = f32[10,320,320]{2,1,0:T(8,128)} custom-call(s32[6]{0:T(128)S(1)} %stack.74.place_ref, bf16[2,2,320,256]{3,2,1,0:T(8,128)(2,1)S(1)} %copy-done.2, f32[16,5,2,8,128]{4,3,2,1,0:T(8,128)S(1)} %all-to-all-done.2.refs_0_, f32[10,320,320]{2,1,0:T(8,128)} %shard_map.111.refs_1_), custom_call_target="tpu_custom_call", output_to_operand_aliasing={{}: (3, {})} | custom-call | flops 629145600 | bytes 6000000 | tf_op jit(solution)/shard_map/pallas_call | solution.py:226
  271.2 5.0 %shard_map.113.refs_1_ = f32[10,320,320]{2,1,0:T(8,128)} custom-call(s32[6]{0:T(128)S(1)} %stack.74.place_ref, bf16[2,2,320,256]{3,2,1,0:T(8,128)(2,1)S(1)} %copy-done.2, f32[16,5,3,8,128]{4,3,2,1,0:T(8,128)S(1)} %all-to-all-done.1.refs_0_, f32[10,320,320]{2,1,0:T(8,128)} %shard_map.112.refs_1_), custom_call_target="tpu_custom_call", output_to_operand_aliasing={{}: (3, {})} | custom-call | flops 943718400 | bytes 9000000 | tf_op jit(solution)/shard_map/pallas_call | solution.py:226
  276.2 3.6 %shard_map.114 = f32[10,320,320]{2,1,0:T(8,128)} custom-call(s32[6]{0:T(128)S(1)} %stack.74.place_ref, bf16[2,2,320,256]{3,2,1,0:T(8,128)(2,1)S(1)} %copy-done.2, f32[16,5,2,8,128]{4,3,2,1,0:T(8,128)} %all-to-all-done.refs_0_, f32[10,320,320]{2,1,0:T(8,128)} %shard_map.113.refs_1_), custom_call_target="tpu_custom_call", output_to_operand_aliasing={{}: (3, {})} | custom-call | flops 629145600 | bytes 6000000 | tf_op jit(solution)/shard_map/pallas_call | solution.py:226
  (64 shorter events, 10.2 us)
Async XLA Ops:
  0.1 1.3 copy-start
  9.2 24.7 %collective-permute-start.2 = (f32[8,128,384]{2,1,0:T(8,128)S(1)}, f32[8,128,384]{2,1,0:T(8,128)S(1)}, u32[]{:S(2)}, u32[]{:S(2)}) collective-permute-start(f32[8,128,384]{2,1,0:T(8,128)S(1)} %get-tuple-element.25), channel_id=1, source_target_pairs={{0,32},{32,0},{1,33},{33,1},{2,34},{34,2},{3,35},{35,3},{4,36},{36... | collective-permute-start | bytes 4718600 | tf_op jit(solution)/shard_map/ppermute | solution.py:266
  18.5 27.3 %collective-permute-start = (f32[8,128,384]{2,1,0:T(8,128)S(1)}, f32[8,128,384]{2,1,0:T(8,128)S(1)}, u32[]{:S(2)}, u32[]{:S(2)}) collective-permute-start(f32[8,128,384]{2,1,0:T(8,128)S(1)} %get-tuple-element.22), channel_id=1, source_target_pairs={{0,32},{32,0},{1,33},{33,1},{2,34},{34,2},{3,35},{35,3},{4,36},{36... | collective-permute-start | bytes 4718600 | tf_op jit(solution)/shard_map/ppermute | solution.py:266
  25.1 9.9 %copy-start.10 = (bf16[2,2,2,2,160,128]{5,4,3,2,1,0:T(8,128)(2,1)S(1)}, bf16[2,2,2,2,160,128]{5,4,3,2,1,0:T(8,128)(2,1)}, u32[]{:S(2)}) copy-start(bf16[2,2,2,2,160,128]{5,4,3,2,1,0:T(8,128)(2,1)} %constant.94.clone.table_ref) | copy-start | bytes 1966084
  25.1 52.6 %collective-permute-start.9 = (f32[8,128,384]{2,1,0:T(8,128)}, f32[8,128,384]{2,1,0:T(8,128)}, u32[]{:S(2)}, u32[]{:S(2)}) collective-permute-start(f32[8,128,384]{2,1,0:T(8,128)} %shard_map.107), channel_id=1, source_target_pairs={{0,32},{32,0},{1,33},{33,1},{2,34},{34,2},{3,35},{35,3},{4,36},{36... | collective-permute-start | bytes 4718600 | tf_op jit(solution)/shard_map/ppermute | solution.py:266
  33.8 59.7 %collective-permute-start.8 = (f32[8,128,384]{2,1,0:T(8,128)}, f32[8,128,384]{2,1,0:T(8,128)}, u32[]{:S(2)}, u32[]{:S(2)}) collective-permute-start(f32[8,128,384]{2,1,0:T(8,128)} %get-tuple-element.34), channel_id=1, source_target_pairs={{0,32},{32,0},{1,33},{33,1},{2,34},{34,2},{3,35},{35,3},{4,36},{36... | collective-permute-start | bytes 4718600 | tf_op jit(solution)/shard_map/ppermute | solution.py:266
  33.9 1.2 copy-start.15
  42.0 0.8 copy-start.6
  42.9 17.4 %collective-permute-start.6 = (f32[16,5,2,8,128]{4,3,2,1,0:T(8,128)S(1)}, f32[16,5,2,8,128]{4,3,2,1,0:T(8,128)S(1)}, u32[]{:S(2)}, u32[]{:S(2)}) collective-permute-start(f32[16,5,2,8,128]{4,3,2,1,0:T(8,128)S(1)} %bitcast.62), channel_id=1, source_target_pairs={{0,64},{16,80},{64,0},{80,16},{1,65},{17,81},{65,1},{81,17},{2,66}... | collective-permute-start | bytes 1966088 | tf_op jit(solution)/shard_map/ppermute | solution.py:244
  45.7 1.1 copy-start.14
  53.6 7.6 %copy-start.8 = (f32[1280,128]{1,0:T(8,128)}, f32[1280,128]{1,0:T(8,128)S(1)}, u32[]{:S(2)}) copy-start(f32[1280,128]{1,0:T(8,128)S(1)} %get-tuple-element.23) | copy-start | bytes 1966084
  53.6 30.3 %collective-permute-start.4 = (f32[16,5,3,8,128]{4,3,2,1,0:T(8,128)}, f32[16,5,3,8,128]{4,3,2,1,0:T(8,128)}, u32[]{:S(2)}, u32[]{:S(2)}) collective-permute-start(f32[16,5,3,8,128]{4,3,2,1,0:T(8,128)} %bitcast.8), channel_id=1, source_target_pairs={{0,16},{16,0},{64,80},{80,64},{1,17},{17,1},{65,81},{81,65},{2,18}... | collective-permute-start | bytes 2949128 | tf_op jit(solution)/shard_map/ppermute | solution.py:244
  53.9 30.0 %collective-permute-start.5 = (f32[16,5,3,8,128]{4,3,2,1,0:T(8,128)}, f32[16,5,3,8,128]{4,3,2,1,0:T(8,128)}, u32[]{:S(2)}, u32[]{:S(2)}) collective-permute-start(f32[16,5,3,8,128]{4,3,2,1,0:T(8,128)} %bitcast.9), channel_id=1, source_target_pairs={{0,80},{16,64},{64,16},{80,0},{1,81},{17,65},{65,17},{81,1},{2,82}... | collective-permute-start | bytes 2949128 | tf_op jit(solution)/shard_map/ppermute | solution.py:244
  60.3 8.8 %copy-start.1 = (bf16[1536,384]{1,0:T(8,128)(2,1)S(1)}, bf16[1536,384]{1,0:T(8,128)(2,1)}, u32[]{:S(2)}) copy-start(bf16[1536,384]{1,0:T(8,128)(2,1)} %constant.95.clone.table_ref) | copy-start | bytes 3538948
  61.2 25.3 %all-to-all-start.2 = ((f32[16,5,2,8,128]{4,3,2,1,0:T(8,128)}), f32[16,5,2,8,128]{4,3,2,1,0:T(8,128)S(1)}, u32[]{:S(2)}, u32[]{:S(2)}) async-start(f32[16,5,2,8,128]{4,3,2,1,0:T(8,128)} %add.111), calls=%async_computation.2 | async-start | bytes 1310720 | tf_op jit(solution)/shard_map/all_to_all | solution.py:248
  69.1 8.7 %copy-start.11 = (bf16[2,2,2,2,160,128]{5,4,3,2,1,0:T(8,128)(2,1)S(1)}, bf16[2,2,2,2,160,128]{5,4,3,2,1,0:T(8,128)(2,1)}, u32[]{:S(2)}) copy-start(bf16[2,2,2,2,160,128]{5,4,3,2,1,0:T(8,128)(2,1)} %constant.94.clone.table_ref) | copy-start | bytes 1966084
  74.9 8.1 %copy-start.3 = (f32[8,128,384]{2,1,0:T(8,128)}, f32[8,128,384]{2,1,0:T(8,128)S(1)}, u32[]{:S(2)}) copy-start(f32[8,128,384]{2,1,0:T(8,128)S(1)} %shard_map.106.own_ref) | copy-start | bytes 4718596
  74.9 36.3 %collective-permute-start.7 = (f32[16,5,3,8,128]{4,3,2,1,0:T(8,128)}, f32[16,5,3,8,128]{4,3,2,1,0:T(8,128)}, u32[]{:S(2)}, u32[]{:S(2)}) collective-permute-start(f32[16,5,3,8,128]{4,3,2,1,0:T(8,128)} %bitcast.13), channel_id=1, source_target_pairs={{0,64},{16,80},{64,0},{80,16},{1,65},{17,81},{65,1},{81,17},{2,66}... | collective-permute-start | bytes 2949128 | tf_op jit(solution)/shard_map/ppermute | solution.py:244
  83.0 56.0 %collective-permute-start.12 = (f32[16,5,5,8,128]{4,3,2,1,0:T(8,128)}, f32[16,5,5,8,128]{4,3,2,1,0:T(8,128)}, u32[]{:S(2)}, u32[]{:S(2)}) collective-permute-start(f32[16,5,5,8,128]{4,3,2,1,0:T(8,128)} %bitcast.64), channel_id=1, source_target_pairs={{0,80},{16,64},{64,16},{80,0},{1,81},{17,65},{65,17},{81,1},{2,82}... | collective-permute-start | bytes 4915208 | tf_op jit(solution)/shard_map/ppermute | solution.py:244
  86.5 7.1 %copy-start.12 = (bf16[2,2,2,2,160,128]{5,4,3,2,1,0:T(8,128)(2,1)S(1)}, bf16[2,2,2,2,160,128]{5,4,3,2,1,0:T(8,128)(2,1)}, u32[]{:S(2)}) copy-start(bf16[2,2,2,2,160,128]{5,4,3,2,1,0:T(8,128)(2,1)} %constant.94.clone.table_ref) | copy-start | bytes 1966084
  86.5 27.0 %all-to-all-start.1 = ((f32[16,5,3,8,128]{4,3,2,1,0:T(8,128)}), f32[16,5,3,8,128]{4,3,2,1,0:T(8,128)S(1)}, u32[]{:S(2)}, u32[]{:S(2)}) async-start(f32[16,5,3,8,128]{4,3,2,1,0:T(8,128)} %add.110), calls=%async_computation.1 | async-start | bytes 1966080 | tf_op jit(solution)/shard_map/all_to_all | solution.py:248
  93.6 1.4 copy-start.5
  95.0 8.5 %copy-start.4 = (f32[8,128,384]{2,1,0:T(8,128)S(1)}, f32[8,128,384]{2,1,0:T(8,128)}, u32[]{:S(2)}) copy-start(f32[8,128,384]{2,1,0:T(8,128)} %copy-done.3) | copy-start | bytes 4718596
  102.2 36.8 %collective-permute-start.11 = (f32[16,5,5,8,128]{4,3,2,1,0:T(8,128)}, f32[16,5,5,8,128]{4,3,2,1,0:T(8,128)}, u32[]{:S(2)}, u32[]{:S(2)}) collective-permute-start(f32[16,5,5,8,128]{4,3,2,1,0:T(8,128)} %bitcast.66), channel_id=1, source_target_pairs={{0,16},{16,0},{64,80},{80,64},{1,17},{17,1},{65,81},{81,65},{2,18}... | collective-permute-start | bytes 4915208 | tf_op jit(solution)/shard_map/ppermute | solution.py:244
  108.7 65.9 %collective-permute-start.10 = (f32[16,5,5,8,128]{4,3,2,1,0:T(8,128)}, f32[16,5,5,8,128]{4,3,2,1,0:T(8,128)}, u32[]{:S(2)}, u32[]{:S(2)}) collective-permute-start(f32[16,5,5,8,128]{4,3,2,1,0:T(8,128)} %bitcast.65), channel_id=1, source_target_pairs={{0,64},{16,80},{64,0},{80,16},{1,65},{17,81},{65,1},{81,17},{2,66}... | collective-permute-start | bytes 4915208 | tf_op jit(solution)/shard_map/ppermute | solution.py:244
  113.5 64.0 %all-to-all-start.3 = ((f32[16,5,3,8,128]{4,3,2,1,0:T(8,128)}), f32[16,5,3,8,128]{4,3,2,1,0:T(8,128)S(1)}, u32[]{:S(2)}, u32[]{:S(2)}) async-start(f32[16,5,3,8,128]{4,3,2,1,0:T(8,128)} %add.112), calls=%async_computation.3 | async-start | bytes 1966080 | tf_op jit(solution)/shard_map/all_to_all | solution.py:248
  139.1 35.6 %copy-start.13 = (f32[3200,128]{1,0:T(8,128)S(1)}, f32[3200,128]{1,0:T(8,128)}, u32[]{:S(2)}) copy-start(f32[3200,128]{1,0:T(8,128)} %get-tuple-element.35) | copy-start | bytes 4915204
  141.9 48.0 %collective-permute-start.15 = (f32[4,5,5,8,128]{4,3,2,1,0:T(8,128)}, f32[4,5,5,8,128]{4,3,2,1,0:T(8,128)}, u32[]{:S(2)}, u32[]{:S(2)}) collective-permute-start(f32[4,5,5,8,128]{4,3,2,1,0:T(8,128)} %get-tuple-element.39), channel_id=1, source_target_pairs={{0,3},{1,0},{2,1},{3,2},{4,7},{5,4},{6,5},{7,6},{8,11},{9,8},{10,9... | collective-permute-start | bytes 1228808 | tf_op jit(solution)/shard_map/ppermute | solution.py:284
  177.4 10.2 %copy-start.7 = (f32[1280,128]{1,0:T(8,128)S(1)}, f32[1280,128]{1,0:T(8,128)}, u32[]{:S(2)}) copy-start(f32[1280,128]{1,0:T(8,128)} %copy-done.6) | copy-start | bytes 1966084
  177.4 51.8 %all-to-all-start.4 = ((f32[16,5,5,8,128]{4,3,2,1,0:T(8,128)}), f32[16,5,5,8,128]{4,3,2,1,0:T(8,128)}, u32[]{:S(2)}, u32[]{:S(2)}) async-start(f32[16,5,5,8,128]{4,3,2,1,0:T(8,128)} %add.113), calls=%async_computation.4 | async-start | bytes 3276800 | tf_op jit(solution)/shard_map/all_to_all | solution.py:248
  184.0 26.3 %collective-permute-start.14 = (f32[4,5,5,8,128]{4,3,2,1,0:T(8,128)}, f32[4,5,5,8,128]{4,3,2,1,0:T(8,128)}, u32[]{:S(2)}, u32[]{:S(2)}) collective-permute-start(f32[4,5,5,8,128]{4,3,2,1,0:T(8,128)} %get-tuple-element.38), channel_id=1, source_target_pairs={{0,2},{1,3},{2,0},{3,1},{4,6},{5,7},{6,4},{7,5},{8,10},{9,11},{10,... | collective-permute-start | bytes 1228808 | tf_op jit(solution)/shard_map/ppermute | solution.py:284
  186.8 41.4 %collective-permute-start.1 = (f32[16,5,2,8,128]{4,3,2,1,0:T(8,128)}, f32[16,5,2,8,128]{4,3,2,1,0:T(8,128)S(1)}, u32[]{:S(2)}, u32[]{:S(2)}) collective-permute-start(f32[16,5,2,8,128]{4,3,2,1,0:T(8,128)} %bitcast.61), channel_id=1, source_target_pairs={{0,16},{16,0},{64,80},{80,64},{1,17},{17,1},{65,81},{81,65},{2,18}... | collective-permute-start | bytes 1966088 | tf_op jit(solution)/shard_map/ppermute | solution.py:244
  187.6 40.7 %collective-permute-start.3 = (f32[16,5,2,8,128]{4,3,2,1,0:T(8,128)S(1)}, f32[16,5,2,8,128]{4,3,2,1,0:T(8,128)S(1)}, u32[]{:S(2)}, u32[]{:S(2)}) collective-permute-start(f32[16,5,2,8,128]{4,3,2,1,0:T(8,128)S(1)} %bitcast.60), channel_id=1, source_target_pairs={{0,80},{16,64},{64,16},{80,0},{1,81},{17,65},{65,17},{81,1},{2,82}... | collective-permute-start | bytes 1966088 | tf_op jit(solution)/shard_map/ppermute | solution.py:244
  188.5 33.8 %collective-permute-start.13 = (f32[4,5,5,8,128]{4,3,2,1,0:T(8,128)}, f32[4,5,5,8,128]{4,3,2,1,0:T(8,128)S(1)}, u32[]{:S(2)}, u32[]{:S(2)}) collective-permute-start(f32[4,5,5,8,128]{4,3,2,1,0:T(8,128)} %get-tuple-element.37), channel_id=1, source_target_pairs={{0,1},{1,2},{2,3},{3,0},{4,5},{5,6},{6,7},{7,4},{8,9},{9,10},{10,1... | collective-permute-start | bytes 1228808 | tf_op jit(solution)/shard_map/ppermute | solution.py:284
  223.1 10.4 %collective-permute-start.18 = (f32[4,5,5,8,128]{4,3,2,1,0:T(8,128)}, f32[4,5,5,8,128]{4,3,2,1,0:T(8,128)}, u32[]{:S(2)}, u32[]{:S(2)}) collective-permute-start(f32[4,5,5,8,128]{4,3,2,1,0:T(8,128)} %pad_maximum_fusion.3), channel_id=1, source_target_pairs={{0,12},{4,0},{8,4},{12,8},{1,13},{5,1},{9,5},{13,9},{2,14},{6,2},{... | collective-permute-start | bytes 1228808 | tf_op jit(solution)/shard_map/ppermute | solution.py:284
  226.0 11.1 %collective-permute-start.17 = (f32[4,5,5,8,128]{4,3,2,1,0:T(8,128)}, f32[4,5,5,8,128]{4,3,2,1,0:T(8,128)}, u32[]{:S(2)}, u32[]{:S(2)}) collective-permute-start(f32[4,5,5,8,128]{4,3,2,1,0:T(8,128)} %pad_maximum_fusion.2), channel_id=1, source_target_pairs={{0,8},{4,12},{8,0},{12,4},{1,9},{5,13},{9,1},{13,5},{2,10},{6,14},... | collective-permute-start | bytes 1228808 | tf_op jit(solution)/shard_map/ppermute | solution.py:284
  227.4 26.3 %collective-permute-start.16 = (f32[4,5,5,8,128]{4,3,2,1,0:T(8,128)}, f32[4,5,5,8,128]{4,3,2,1,0:T(8,128)}, u32[]{:S(2)}, u32[]{:S(2)}) collective-permute-start(f32[4,5,5,8,128]{4,3,2,1,0:T(8,128)} %pad_maximum_fusion.1), channel_id=1, source_target_pairs={{0,4},{4,8},{8,12},{12,0},{1,5},{5,9},{9,13},{13,1},{2,6},{6,10},{... | collective-permute-start | bytes 1228808 | tf_op jit(solution)/shard_map/ppermute | solution.py:284
  229.2 47.0 %all-to-all-start = ((f32[16,5,2,8,128]{4,3,2,1,0:T(8,128)}), f32[16,5,2,8,128]{4,3,2,1,0:T(8,128)}, u32[]{:S(2)}, u32[]{:S(2)}) async-start(f32[16,5,2,8,128]{4,3,2,1,0:T(8,128)} %add.109), calls=%async_computation | async-start | bytes 1310720 | tf_op jit(solution)/shard_map/all_to_all | solution.py:248
  253.7 1.5 copy-start.9
  255.1 7.6 %copy-start.2 = (bf16[2,2,320,256]{3,2,1,0:T(8,128)(2,1)S(1)}, bf16[2,2,320,256]{3,2,1,0:T(8,128)(2,1)}, u32[]{:S(2)}) copy-start(bf16[2,2,320,256]{3,2,1,0:T(8,128)(2,1)} %constant.97.clone.table_ref) | copy-start | bytes 1966084

commit v2 on v0

--- a/solution.py
+++ b/solution.py
@@ -51,10 +51,9 @@
 def second_table(chunk):
     source, y = np.meshgrid(np.arange(16), np.arange(YC), indexing="ij")
     places = (source * 16 + chunk * YC + y).reshape(-1)
-    places = places[None, :] + np.array([[0], [256]])
     waves = np.arange(2 * KEEP) - KEEP
-    angle = angles(places[:, None, :], waves[None, :, None])
-    table = np.concatenate([np.cos(angle), np.sin(angle)], axis=2)
+    angle = angles(places[None, :], waves[:, None])
+    table = np.concatenate([np.cos(angle), np.sin(angle)], axis=1)
     return split_table(table / np.sqrt(N))
 
 
@@ -79,21 +78,19 @@
 def depth_kernel(group, keeps, place_ref, u_ref, v_ref, t_ref, table_ref, *out_refs):
     first = place_ref[0] == 0
     squares = place_ref[1] == group
-    rows = YC * u_ref.shape[0]
-
-    def load(ref):
-        return jnp.concatenate([ref[:, y, :] for y in range(YC)], axis=0)
-
-    u, v, t = load(u_ref), load(v_ref), load(t_ref)
+    u, v, t = u_ref[...], v_ref[...], t_ref[...]
+    rows = YC * u.shape[0]
     highs, lows = [], []
     for keep in keeps:
         swap = first if keep == 0 else ~first
         a = jnp.where(squares & swap, v, u)
-        high, low = halves(a * jnp.where(squares, a, jnp.where(swap, t, v)))
+        product = a * jnp.where(squares, a, jnp.where(swap, t, v))
+        high, low = halves(jnp.swapaxes(product, 0, 1).reshape(rows, N))
         highs.append(high)
         lows.append(low)
     high, low = jnp.concatenate(highs, axis=0), jnp.concatenate(lows, axis=0)
-    out = dot(jnp.concatenate([high, low, high], axis=1), table_ref[...])
+    table = jnp.concatenate([table_ref[0], table_ref[0], table_ref[1]], axis=0)
+    out = dot(jnp.concatenate([high, low, high], axis=1), table)
     for i, ref in enumerate(out_refs):
         ref[...] = out[i * rows : (i + 1) * rows].reshape(YC, rows // YC, 384)
 
@@ -111,7 +108,7 @@
             block,
             block,
             block,
-            pl.BlockSpec((3 * N, 384), lambda i: (0, 0)),
+            pl.BlockSpec((2, N, 384), lambda i: (0, 0, 0)),
         ],
         out_specs=[out] * len(keeps),
         out_shape=[shape] * len(keeps),
@@ -142,7 +139,7 @@
     index = 0
     for b in range(len(blocks)):
         base = 0
-        for pairs in splits:
+        for pairs in splits[b]:
             ref = refs[index]
             index += 1
             stride = 5 * pairs * YC
@@ -161,7 +158,7 @@
 
 def first_stage(place, own, recv, table, blocks, splits):
     block = pl.BlockSpec((2, XB, 384), lambda i: (i, 0, 0))
-    sizes = list(splits) * len(blocks)
+    sizes = [pairs for split in splits for pairs in split]
     outs = [(DESTS * 5 * pairs * YC, LANES) for pairs in sizes]
     results = pl.pallas_call(
         functools.partial(first_kernel, blocks, splits),
@@ -188,8 +185,10 @@
         values = jnp.concatenate(t, axis=1)
         turned = jnp.concatenate([t[1], -t[0], t[3], -t[2], turn_tail(t[4])], axis=1)
         high, low = halves(jnp.concatenate([values, turned], axis=0))
-        half = place_ref[3] ^ fresh[side]
-        left += [table_ref[0, half], table_ref[0, half], table_ref[1, half]]
+        odd = lax.broadcasted_iota(jnp.int32, (2 * KEEP, 1), 0) % 2 == 1
+        flip = odd & ((place_ref[3] ^ fresh[side]) == 1)
+        sign = jnp.where(flip, -1.0, 1.0).astype(jnp.bfloat16)
+        left += [table_ref[0] * sign, table_ref[0] * sign, table_ref[1] * sign]
         right += [high, low, high]
     out = dot(jnp.concatenate(left, axis=1), jnp.concatenate(right, axis=0))
     tail = out[:, 512:]
@@ -221,7 +220,7 @@
     return pl.pallas_call(
         functools.partial(second_kernel, count, [s[0] for s in sides], base),
         grid=(pairs,),
-        in_specs=[pl.BlockSpec(memory_space=pltpu.SMEM), pl.BlockSpec(table.shape, lambda k: (0,) * 4)]
+        in_specs=[pl.BlockSpec(memory_space=pltpu.SMEM), pl.BlockSpec(table.shape, lambda k: (0,) * 3)]
         + [block] * count
         + [out] * len(extra),
         out_specs=out,
@@ -249,8 +248,7 @@
     place = jnp.stack([core, high, owns_mean.astype(jnp.int32), low]).astype(jnp.int32)
 
     rows = jnp.asarray(first_table())
-    split = depth_table()
-    columns = jnp.asarray(np.concatenate([split[0], split[0], split[1]], axis=0))
+    columns = jnp.asarray(depth_table())
     fields = (velocity_u, velocity_v, scalar_theta)
 
     def depth(unit, keeps):
@@ -277,31 +275,29 @@
     (send,) = depth("01", (0,))
     recv = swap(send)
     (own,) = depth("01", (1,))
-    near = near_ring(first(own, recv, (0,), (PAIRS,)))
-    far = far_ring("01", first(own, recv, (1,), (PAIRS,)))
+    near = near_ring(first(own, recv, (0,), ((PAIRS,),)))
+    far = far_ring("01", first(own, recv, (1,), ((PAIRS,),)))
 
     send, own = depth("00", (0, 1))
-    kept, across = first(own, swap(send), (0, 1), (PAIRS,))
+    kept, across = first(own, swap(send), (0, 1), ((PAIRS,), (PAIRS,)))
     across = far_ring("00", [across])
 
     send, own = depth("11", (0, 1))
-    parts = first(own, swap(send), (0, 1), LAST)
-    near_last = near_ring(parts[:2])
-    far_last = far_ring("11", parts[2:])
+    near_last, *far_last = first(own, swap(send), (0, 1), ((PAIRS,), LAST))
+    near_last = near_ring([near_last])
+    far_last = far_ring("11", far_last)
 
     send, own = depth("10", (0, 1))
-    parts = first(own, swap(send), (0, 1), LAST)
-    kept_last = parts[:2]
-    across_last = far_ring("10", parts[2:])
+    kept_last, *across_last = first(own, swap(send), (0, 1), ((PAIRS,), LAST))
+    across_last = far_ring("10", across_last)
 
     mine = gather(kept, near[0])
     other = gather(across[0], far[0])
-    mine_last = [gather(a, b) for a, b in zip(kept_last, near_last)]
+    mine_last = gather(kept_last, near_last[0])
     other_last = [gather(a, b) for a, b in zip(across_last, far_last)]
 
     result = second(0, [(0, mine), (1, other)], 0, None)
-    result = second(1, [(0, mine_last[0])], 0, result)
-    result = second(1, [(0, mine_last[1])], LAST[0], result)
+    result = second(1, [(0, mine_last)], 0, result)
     result = second(1, [(1, other_last[0])], 0, result)
     result = second(1, [(1, other_last[1])], LAST[0], result)
     return result[None]

time: 239 us -> 263 us (1.10)
  waiting for transfers between devices: 63.3 us -> 106 us
  starting transfers between devices: 58.7 us -> 48 us
  Pallas kernels: 93.6 us -> 89.3 us
    ppermute x9 -> x8, waiting for transfers between devices: 60.1 us -> 102 us  [ring(): return lax.ppermute(value, ('xh', 'xl'), moves)]
    all_to_all x6 -> x5, starting transfers between devices: 46.5 us -> 37.9 us  [spread(): lax.all_to_all(value, ('z', 'y'), split_axis=0, concat_axis=0, tiled=True)]
    ppermute x9 -> x8, starting transfers between devices: 11.6 us -> 9.5 us  [ring(): return lax.ppermute(value, ('xh', 'xl'), moves)]
    add x6 -> x5, other arithmetic: 12.9 us -> 11 us  [gather(): return spread(jnp.add(a, b))]
    unnamed x38 -> x30, local copies, waits for them, and re-layouts: 8.67 us -> 6.98 us
    pallas_call x5 -> x4, Pallas kernels: 25.3 us -> 23.9 us  [second_stage(): pl.pallas_call(functools.partial(second_kernel, count, [s[0] for s in sid...]
  transfers between devices with their start and end apart: 19 -> 17, of which waited for: 8 -> 8; matrix products, arithmetic and copies ran while one was open for 5% -> 4% of each run, Pallas kernels for 35% -> 30%
where the time goes in v2:
time: 263 us; the launch traced here: 261 us
  waiting for transfers between devices  106 us (40%)
  Pallas kernels  89.3 us (34%)
  starting transfers between devices  48 us (18%)
  other arithmetic  11.1 us (4%)
  local copies, waits for them, and re-layouts  6.98 us (3%)
    ppermute x8, waiting for transfers between devices, ring(): return lax.ppermute(value, ('xh', 'xl'), moves)  102 us
    all_to_all x5, starting transfers between devices, spread(): lax.all_to_all(value, ('z', 'y'), split_axis=0, concat_axis=0, tiled=True)  37.9 us
    pallas_call x5, Pallas kernels, depth_stage(): pl.pallas_call(functools.partial(depth_kernel, group, keeps), grid=(XB //...  33.8 us
    pallas_call x5, Pallas kernels, first_stage(): pl.pallas_call(functools.partial(first_kernel, blocks, splits), grid=(YC...  31.6 us
    pallas_call x4, Pallas kernels, second_stage(): pl.pallas_call(functools.partial(second_kernel, count, [s[0] for s in sid...  23.9 us
    add x5, other arithmetic, gather(): return spread(jnp.add(a, b))  11 us
    ppermute x8, starting transfers between devices, ring(): return lax.ppermute(value, ('xh', 'xl'), moves)  9.5 us
    unnamed x30, local copies, waits for them, and re-layouts  6.98 us
  transfers between devices with their start and end apart: 17, of which 8 were waited for; matrix products, arithmetic and copies ran while one was open for 4% of the time, Pallas kernels for 30%

profile of v2, /device:TPU:22, one launch (start us, length us, event | category | flops | bytes accessed | tf_op | source)
XLA Modules:
  0.0 261.1 jit_solution(11940929966953093974)
XLA Ops:
  0.0 0.1 pad_add_fusion.place_ref
  0.1 1.1 copy-done
  1.2 7.0 %shard_map.91 = (f32[8,128,384]{2,1,0:T(8,128)S(1)}, f32[8,128,384]{2,1,0:T(8,128)S(1)}) custom-call(s32[4]{0:T(128)S(1)} %pad_add_fusion.place_ref, f32[128,16,512]{2,1,0:T(8,128)} %u_ref.9, f32[128,16,512]{2,1,0:T(8,128)} %v_ref.9, f32[128,16,512]{2,1,0:T(8,128)} %t_ref.9, bf16[2,512,384]{2,1,0:T(8,128)(2,1)S(1)} %copy-done), custom_call_target="tpu_custom_call" | custom-call | flops 2415919104 | bytes 9000000 | tf_op jit(solution)/shard_map/pallas_call | solution.py:103
  8.3 0.1 collective-permute-start
  8.4 7.1 %shard_map.93 = (f32[8,128,384]{2,1,0:T(8,128)S(1)}, f32[8,128,384]{2,1,0:T(8,128)S(1)}) custom-call(s32[4]{0:T(128)S(1)} %pad_add_fusion.place_ref, f32[128,16,512]{2,1,0:T(8,128)} %u_ref.9, f32[128,16,512]{2,1,0:T(8,128)} %v_ref.9, f32[128,16,512]{2,1,0:T(8,128)} %t_ref.9, bf16[2,512,384]{2,1,0:T(8,128)(2,1)S(1)} %copy-done), custom_call_target="tpu_custom_call" | custom-call | flops 2415919104 | bytes 9000000 | tf_op jit(solution)/shard_map/pallas_call | solution.py:103
  15.5 0.5 collective-permute-start.2
  16.0 1.2 copy-done.14
  17.2 6.6 %shard_map.92 = (f32[3200,128]{1,0:T(8,128)}, f32[1920,128]{1,0:T(8,128)S(1)}, f32[1280,128]{1,0:T(8,128)S(1)}) custom-call(s32[4]{0:T(128)S(1)} %pad_add_fusion.place_ref, f32[8,128,384]{2,1,0:T(8,128)S(1)} %get-tuple-element.19.own_ref, f32[8,128,384]{2,1,0:T(8,128)} %copy-done.14, bf16[2,2,2,2,160,128]{5,4,3,2,1,0:T(8,128)(2,1)S(1)} %copy-done.8), custom_call_target="tpu_custom_call" | custom-call | flops 3019898880 | bytes 7000000 | tf_op jit(solution)/shard_map/pallas_call | solution.py:163
  23.8 0.8 collective-permute-start.4
  24.7 1.2 copy-done.13
  25.8 6.7 %shard_map.94 = (f32[3200,128]{1,0:T(8,128)}, f32[1920,128]{1,0:T(8,128)S(1)}, f32[1280,128]{1,0:T(8,128)S(1)}) custom-call(s32[4]{0:T(128)S(1)} %pad_add_fusion.place_ref, f32[8,128,384]{2,1,0:T(8,128)S(1)} %get-tuple-element.22.own_ref, f32[8,128,384]{2,1,0:T(8,128)} %copy-done.13, bf16[2,2,2,2,160,128]{5,4,3,2,1,0:T(8,128)(2,1)S(1)} %copy-done.8), custom_call_target="tpu_custom_call" | custom-call | flops 3019898880 | bytes 7000000 | tf_op jit(solution)/shard_map/pallas_call | solution.py:163
  32.6 1.1 collective-permute-start.5
  33.7 6.0 %shard_map.98 = f32[8,128,384]{2,1,0:T(8,128)} custom-call(s32[4]{0:T(128)S(1)} %pad_add_fusion.place_ref, f32[128,16,512]{2,1,0:T(8,128)} %u_ref.9, f32[128,16,512]{2,1,0:T(8,128)} %v_ref.9, f32[128,16,512]{2,1,0:T(8,128)} %t_ref.9, bf16[2,512,384]{2,1,0:T(8,128)(2,1)S(1)} %copy-done.1), custom_call_target="tpu_custom_call" | custom-call | flops 1207959552 | bytes 9000000 | tf_op jit(solution)/shard_map/pallas_call | solution.py:103
  39.8 2.2 collective-permute-start.6
  42.0 6.5 %collective-permute-done.4 = f32[16,5,3,8,128]{4,3,2,1,0:T(8,128)S(1)} collective-permute-done((f32[16,5,3,8,128]{4,3,2,1,0:T(8,128)S(1)}, f32[16,5,3,8,128]{4,3,2,1,0:T(8,128)S(1)}, u32[]{:S(2)}, u32[]{:S(2)}) %collective-permute-start.4) | collective-permute-done | bytes 983072 | tf_op jit(solution)/shard_map/ppermute | solution.py:238
  48.4 44.0 %collective-permute-done.5 = f32[16,5,3,8,128]{4,3,2,1,0:T(8,128)S(1)} collective-permute-done((f32[16,5,3,8,128]{4,3,2,1,0:T(8,128)S(1)}, f32[16,5,3,8,128]{4,3,2,1,0:T(8,128)S(1)}, u32[]{:S(2)}, u32[]{:S(2)}) %collective-permute-start.5) | collective-permute-done | bytes 983072 | tf_op jit(solution)/shard_map/ppermute | solution.py:238
  92.4 1.1 add.16
  93.5 8.3 %all-to-all-start.1 = ((f32[16,5,3,8,128]{4,3,2,1,0:T(8,128)}), f32[16,5,3,8,128]{4,3,2,1,0:T(8,128)S(1)}, u32[]{:S(2)}, u32[]{:S(2)}) async-start(f32[16,5,3,8,128]{4,3,2,1,0:T(8,128)} %add.16), calls=%async_computation.1 | async-start | bytes 1966080 | tf_op jit(solution)/shard_map/all_to_all | solution.py:242
  101.8 7.8 %shard_map.95 = (f32[8,128,384]{2,1,0:T(8,128)}, f32[8,128,384]{2,1,0:T(8,128)S(1)}) custom-call(s32[4]{0:T(128)S(1)} %pad_add_fusion.place_ref, f32[128,16,512]{2,1,0:T(8,128)} %u_ref.9, f32[128,16,512]{2,1,0:T(8,128)} %v_ref.9, f32[128,16,512]{2,1,0:T(8,128)} %t_ref.9, bf16[2,512,384]{2,1,0:T(8,128)(2,1)S(1)} %copy-done.1), custom_call_target="tpu_custom_call" | custom-call | flops 2415919104 | bytes 9000000 | tf_op jit(solution)/shard_map/pallas_call | solution.py:103
  109.6 5.8 %shard_map.97.own_ref = f32[8,128,384]{2,1,0:T(8,128)S(1)} custom-call(s32[4]{0:T(128)S(1)} %pad_add_fusion.place_ref, f32[128,16,512]{2,1,0:T(8,128)} %u_ref.9, f32[128,16,512]{2,1,0:T(8,128)} %v_ref.9, f32[128,16,512]{2,1,0:T(8,128)} %t_ref.9, bf16[2,512,384]{2,1,0:T(8,128)(2,1)S(1)} %copy-done.1), custom_call_target="tpu_custom_call" | custom-call | flops 1207959552 | bytes 9000000 | tf_op jit(solution)/shard_map/pallas_call | solution.py:103
  115.5 5.8 %shard_map.99 = f32[3200,128]{1,0:T(8,128)} custom-call(s32[4]{0:T(128)S(1)} %pad_add_fusion.place_ref, f32[8,128,384]{2,1,0:T(8,128)S(1)} %shard_map.97.own_ref, f32[8,128,384]{2,1,0:T(8,128)} %collective-permute-done.8.recv_ref, bf16[2,2,2,2,160,128]{5,4,3,2,1,0:T(8,128)(2,1)S(1)} %copy-done.8), custom_call_target="tpu_custom_call" | custom-call | flops 1509949440 | bytes 7000000 | tf_op jit(solution)/shard_map/pallas_call | solution.py:163
  121.2 0.3 collective-permute-start.9
  121.6 2.8 %add.17 = f32[16,5,5,8,128]{4,3,2,1,0:T(8,128)} add(f32[16,5,5,8,128]{4,3,2,1,0:T(8,128)S(1)} %bitcast.19, f32[16,5,5,8,128]{4,3,2,1,0:T(8,128)} %collective-permute-done.6) | non-fusion elementwise | flops 409600 | bytes 4915200 | tf_op jit(solution)/shard_map/add | solution.py:270
  124.4 7.2 %all-to-all-start.2 = ((f32[16,5,5,8,128]{4,3,2,1,0:T(8,128)}), f32[16,5,5,8,128]{4,3,2,1,0:T(8,128)S(1)}, u32[]{:S(2)}, u32[]{:S(2)}) async-start(f32[16,5,5,8,128]{4,3,2,1,0:T(8,128)} %add.17), calls=%async_computation.2 | async-start | bytes 3276800 | tf_op jit(solution)/shard_map/all_to_all | solution.py:242
  131.6 1.4 copy-done.6
  133.0 1.1 copy-done.9
  134.1 7.2 %shard_map.96 = (f32[3200,128]{1,0:T(8,128)}, f32[3200,128]{1,0:T(8,128)}) custom-call(s32[4]{0:T(128)S(1)} %pad_add_fusion.place_ref, f32[8,128,384]{2,1,0:T(8,128)S(1)} %copy-done.6, f32[8,128,384]{2,1,0:T(8,128)} %collective-permute-done.7.recv_ref, bf16[2,2,2,2,160,128]{5,4,3,2,1,0:T(8,128)(2,1)S(1)} %copy-done.9), custom_call_target="tpu_custom_call" | custom-call | flops 3019898880 | bytes 7000000 | tf_op jit(solution)/shard_map/pallas_call | solution.py:163
  141.3 1.7 collective-permute-start.10
  143.0 5.3 %shard_map.100 = f32[3200,128]{1,0:T(8,128)} custom-call(s32[4]{0:T(128)S(1)} %pad_add_fusion.place_ref, f32[8,128,384]{2,1,0:T(8,128)S(1)} %copy-done.4, f32[8,128,384]{2,1,0:T(8,128)} %collective-permute-done.8.recv_ref, bf16[2,2,2,2,160,128]{5,4,3,2,1,0:T(8,128)(2,1)S(1)} %copy-done.9), custom_call_target="tpu_custom_call" | custom-call | flops 1509949440 | bytes 7000000 | tf_op jit(solution)/shard_map/pallas_call | solution.py:163
  148.3 2.1 collective-permute-start.11
  150.4 11.4 %collective-permute-done.9 = f32[16,5,5,8,128]{4,3,2,1,0:T(8,128)} collective-permute-done((f32[16,5,5,8,128]{4,3,2,1,0:T(8,128)}, f32[16,5,5,8,128]{4,3,2,1,0:T(8,128)}, u32[]{:S(2)}, u32[]{:S(2)}) %collective-permute-start.9) | collective-permute-done | bytes 1638432 | tf_op jit(solution)/shard_map/ppermute | solution.py:238
  161.8 2.9 %add.18 = f32[16,5,5,8,128]{4,3,2,1,0:T(8,128)} add(f32[16,5,5,8,128]{4,3,2,1,0:T(8,128)S(1)} %bitcast.20, f32[16,5,5,8,128]{4,3,2,1,0:T(8,128)} %collective-permute-done.9) | non-fusion elementwise | flops 409600 | bytes 4915200 | tf_op jit(solution)/shard_map/add | solution.py:270
  164.7 7.2 %all-to-all-start.3 = ((f32[16,5,5,8,128]{4,3,2,1,0:T(8,128)}), f32[16,5,5,8,128]{4,3,2,1,0:T(8,128)}, u32[]{:S(2)}, u32[]{:S(2)}) async-start(f32[16,5,5,8,128]{4,3,2,1,0:T(8,128)} %add.18), calls=%async_computation.3 | async-start | bytes 3276800 | tf_op jit(solution)/shard_map/all_to_all | solution.py:242
  171.9 22.4 %collective-permute-done.10 = f32[16,5,5,8,128]{4,3,2,1,0:T(8,128)} collective-permute-done((f32[16,5,5,8,128]{4,3,2,1,0:T(8,128)}, f32[16,5,5,8,128]{4,3,2,1,0:T(8,128)}, u32[]{:S(2)}, u32[]{:S(2)}) %collective-permute-start.10) | collective-permute-done | bytes 1638432 | tf_op jit(solution)/shard_map/ppermute | solution.py:238
  194.3 1.5 collective-permute-done.11
  195.8 3.3 %add.19 = f32[16,5,5,8,128]{4,3,2,1,0:T(8,128)} add(f32[16,5,5,8,128]{4,3,2,1,0:T(8,128)} %collective-permute-done.10, f32[16,5,5,8,128]{4,3,2,1,0:T(8,128)} %collective-permute-done.11) | non-fusion elementwise | flops 409600 | bytes 4915200 | tf_op jit(solution)/shard_map/add | solution.py:270
  199.1 7.2 %all-to-all-start.4 = ((f32[16,5,5,8,128]{4,3,2,1,0:T(8,128)}), f32[16,5,5,8,128]{4,3,2,1,0:T(8,128)}, u32[]{:S(2)}, u32[]{:S(2)}) async-start(f32[16,5,5,8,128]{4,3,2,1,0:T(8,128)} %add.19), calls=%async_computation.4 | async-start | bytes 3276800 | tf_op jit(solution)/shard_map/all_to_all | solution.py:242
  206.3 1.2 collective-permute-start.3
  207.5 14.9 %collective-permute-done.1 = f32[16,5,2,8,128]{4,3,2,1,0:T(8,128)S(1)} collective-permute-done((f32[16,5,2,8,128]{4,3,2,1,0:T(8,128)S(1)}, f32[16,5,2,8,128]{4,3,2,1,0:T(8,128)S(1)}, u32[]{:S(2)}, u32[]{:S(2)}) %collective-permute-start.1) | collective-permute-done | bytes 655392 | tf_op jit(solution)/shard_map/ppermute | solution.py:238
  222.4 1.5 collective-permute-done.3
  223.9 0.9 add.15
  224.8 3.4 %all-to-all-done.4.refs_1_ = f32[16,5,5,8,128]{4,3,2,1,0:T(8,128)} async-done(((f32[16,5,5,8,128]{4,3,2,1,0:T(8,128)}), f32[16,5,5,8,128]{4,3,2,1,0:T(8,128)}, u32[]{:S(2)}, u32[]{:S(2)}) %all-to-all-start.4) | async-done | bytes 1638432 | tf_op jit(solution)/shard_map/all_to_all | solution.py:242
  228.2 8.0 %all-to-all-start = ((f32[16,5,2,8,128]{4,3,2,1,0:T(8,128)}), f32[16,5,2,8,128]{4,3,2,1,0:T(8,128)}, u32[]{:S(2)}, u32[]{:S(2)}) async-start(f32[16,5,2,8,128]{4,3,2,1,0:T(8,128)} %add.15), calls=%async_computation | async-start | bytes 1310720 | tf_op jit(solution)/shard_map/all_to_all | solution.py:242
  236.2 1.0 copy-done.10
  237.2 8.1 %shard_map.101.refs_1_ = f32[10,320,320]{2,1,0:T(8,128)} custom-call(s32[4]{0:T(128)S(1)} %pad_add_fusion.place_ref, bf16[2,320,256]{2,1,0:T(8,128)(2,1)S(1)} %copy-done.10, f32[16,5,5,8,128]{4,3,2,1,0:T(8,128)} %all-to-all-done.3.refs_0_, f32[16,5,5,8,128]{4,3,2,1,0:T(8,128)} %all-to-all-done.4.refs_1_), custom_call_target="tpu_custom_call" | custom-call | flops 3145728000 | bytes 15000000 | tf_op jit(solution)/shard_map/pallas_call | solution.py:220
  245.3 7.2 %shard_map.102.refs_1_ = f32[10,320,320]{2,1,0:T(8,128)} custom-call(s32[4]{0:T(128)S(1)} %pad_add_fusion.place_ref, bf16[2,320,256]{2,1,0:T(8,128)(2,1)S(1)} %copy-done.2, f32[16,5,5,8,128]{4,3,2,1,0:T(8,128)S(1)} %all-to-all-done.2.refs_0_, f32[10,320,320]{2,1,0:T(8,128)} %shard_map.101.refs_1_), custom_call_target="tpu_custom_call", output_to_operand_aliasing={{}: (3, {})} | custom-call | flops 1572864000 | bytes 15000000 | tf_op jit(solution)/shard_map/pallas_call | solution.py:220
  252.5 5.0 %shard_map.103.refs_1_ = f32[10,320,320]{2,1,0:T(8,128)} custom-call(s32[4]{0:T(128)S(1)} %pad_add_fusion.place_ref, bf16[2,320,256]{2,1,0:T(8,128)(2,1)S(1)} %copy-done.2, f32[16,5,3,8,128]{4,3,2,1,0:T(8,128)S(1)} %all-to-all-done.1.refs_0_, f32[10,320,320]{2,1,0:T(8,128)} %shard_map.102.refs_1_), custom_call_target="tpu_custom_call", output_to_operand_aliasing={{}: (3, {})} | custom-call | flops 943718400 | bytes 9000000 | tf_op jit(solution)/shard_map/pallas_call | solution.py:220
  257.5 3.6 %shard_map.104 = f32[10,320,320]{2,1,0:T(8,128)} custom-call(s32[4]{0:T(128)S(1)} %pad_add_fusion.place_ref, bf16[2,320,256]{2,1,0:T(8,128)(2,1)S(1)} %copy-done.2, f32[16,5,2,8,128]{4,3,2,1,0:T(8,128)} %all-to-all-done.refs_0_, f32[10,320,320]{2,1,0:T(8,128)} %shard_map.103.refs_1_), custom_call_target="tpu_custom_call", output_to_operand_aliasing={{}: (3, {})} | custom-call | flops 629145600 | bytes 6000000 | tf_op jit(solution)/shard_map/pallas_call | solution.py:220
  (36 shorter events, 0.1 us)
Async XLA Ops:
  0.1 1.1 copy-start
  8.3 8.9 %copy-start.8 = (bf16[2,2,2,2,160,128]{5,4,3,2,1,0:T(8,128)(2,1)S(1)}, bf16[2,2,2,2,160,128]{5,4,3,2,1,0:T(8,128)(2,1)}, u32[]{:S(2)}) copy-start(bf16[2,2,2,2,160,128]{5,4,3,2,1,0:T(8,128)(2,1)} %constant.33.clone.table_ref) | copy-start | bytes 1966084
  8.3 7.7 %collective-permute-start = (f32[8,128,384]{2,1,0:T(8,128)S(1)}, f32[8,128,384]{2,1,0:T(8,128)S(1)}, u32[]{:S(2)}, u32[]{:S(2)}) collective-permute-start(f32[8,128,384]{2,1,0:T(8,128)S(1)} %get-tuple-element.20), channel_id=1, source_target_pairs={{0,32},{32,0},{1,33},{33,1},{2,34},{34,2},{3,35},{35,3},{4,36},{36... | collective-permute-start | bytes 4718600 | tf_op jit(solution)/shard_map/ppermute | solution.py:258
  15.5 9.2 %collective-permute-start.2 = (f32[8,128,384]{2,1,0:T(8,128)S(1)}, f32[8,128,384]{2,1,0:T(8,128)S(1)}, u32[]{:S(2)}, u32[]{:S(2)}) collective-permute-start(f32[8,128,384]{2,1,0:T(8,128)S(1)} %get-tuple-element.23), channel_id=1, source_target_pairs={{0,32},{32,0},{1,33},{33,1},{2,34},{34,2},{3,35},{35,3},{4,36},{36... | collective-permute-start | bytes 4718600 | tf_op jit(solution)/shard_map/ppermute | solution.py:258
  16.0 1.2 copy-start.14
  23.8 24.6 %collective-permute-start.4 = (f32[16,5,3,8,128]{4,3,2,1,0:T(8,128)S(1)}, f32[16,5,3,8,128]{4,3,2,1,0:T(8,128)S(1)}, u32[]{:S(2)}, u32[]{:S(2)}) collective-permute-start(f32[16,5,3,8,128]{4,3,2,1,0:T(8,128)S(1)} %bitcast.15), channel_id=1, source_target_pairs={{0,16},{16,0},{64,80},{80,64},{1,17},{17,1},{65,81},{81,65},{2,18}... | collective-permute-start | bytes 2949128 | tf_op jit(solution)/shard_map/ppermute | solution.py:238
  24.7 1.2 copy-start.13
  25.8 7.9 %copy-start.1 = (bf16[2,512,384]{2,1,0:T(8,128)(2,1)S(1)}, bf16[2,512,384]{2,1,0:T(8,128)(2,1)}, u32[]{:S(2)}) copy-start(bf16[2,512,384]{2,1,0:T(8,128)(2,1)} %constant.34.clone.table_ref) | copy-start | bytes 2359300
  32.6 7.2 %copy-start.7 = (f32[1280,128]{1,0:T(8,128)}, f32[1280,128]{1,0:T(8,128)S(1)}, u32[]{:S(2)}) copy-start(f32[1280,128]{1,0:T(8,128)S(1)} %get-tuple-element.24) | copy-start | bytes 1966084
  32.6 59.8 %collective-permute-start.5 = (f32[16,5,3,8,128]{4,3,2,1,0:T(8,128)S(1)}, f32[16,5,3,8,128]{4,3,2,1,0:T(8,128)S(1)}, u32[]{:S(2)}, u32[]{:S(2)}) collective-permute-start(f32[16,5,3,8,128]{4,3,2,1,0:T(8,128)S(1)} %bitcast.16), channel_id=1, source_target_pairs={{0,80},{16,64},{64,16},{80,0},{1,81},{17,65},{65,17},{81,1},{2,82}... | collective-permute-start | bytes 2949128 | tf_op jit(solution)/shard_map/ppermute | solution.py:238
  39.7 75.7 %collective-permute-start.8 = (f32[8,128,384]{2,1,0:T(8,128)}, f32[8,128,384]{2,1,0:T(8,128)}, u32[]{:S(2)}, u32[]{:S(2)}) collective-permute-start(f32[8,128,384]{2,1,0:T(8,128)} %shard_map.98), channel_id=1, source_target_pairs={{0,32},{32,0},{1,33},{33,1},{2,34},{34,2},{3,35},{35,3},{4,36},{36... | collective-permute-start | bytes 4718600 | tf_op jit(solution)/shard_map/ppermute | solution.py:258
  39.8 81.8 %collective-permute-start.6 = (f32[16,5,5,8,128]{4,3,2,1,0:T(8,128)}, f32[16,5,5,8,128]{4,3,2,1,0:T(8,128)}, u32[]{:S(2)}, u32[]{:S(2)}) collective-permute-start(f32[16,5,5,8,128]{4,3,2,1,0:T(8,128)} %bitcast.9), channel_id=1, source_target_pairs={{0,64},{16,80},{64,0},{80,16},{1,65},{17,81},{65,1},{81,17},{2,66}... | collective-permute-start | bytes 4915208 | tf_op jit(solution)/shard_map/ppermute | solution.py:238
  93.5 30.9 %all-to-all-start.1 = ((f32[16,5,3,8,128]{4,3,2,1,0:T(8,128)}), f32[16,5,3,8,128]{4,3,2,1,0:T(8,128)S(1)}, u32[]{:S(2)}, u32[]{:S(2)}) async-start(f32[16,5,3,8,128]{4,3,2,1,0:T(8,128)} %add.16), calls=%async_computation.1 | async-start | bytes 1966080 | tf_op jit(solution)/shard_map/all_to_all | solution.py:242
  109.6 5.8 %copy-start.5 = (f32[8,128,384]{2,1,0:T(8,128)}, f32[8,128,384]{2,1,0:T(8,128)S(1)}, u32[]{:S(2)}) copy-start(f32[8,128,384]{2,1,0:T(8,128)S(1)} %get-tuple-element.29.own_ref) | copy-start | bytes 4718596
  109.6 22.0 %collective-permute-start.7 = (f32[8,128,384]{2,1,0:T(8,128)}, f32[8,128,384]{2,1,0:T(8,128)}, u32[]{:S(2)}, u32[]{:S(2)}) collective-permute-start(f32[8,128,384]{2,1,0:T(8,128)} %get-tuple-element.30), channel_id=1, source_target_pairs={{0,32},{32,0},{1,33},{33,1},{2,34},{34,2},{3,35},{35,3},{4,36},{36... | collective-permute-start | bytes 4718600 | tf_op jit(solution)/shard_map/ppermute | solution.py:258
  115.4 5.8 %copy-start.3 = (f32[8,128,384]{2,1,0:T(8,128)}, f32[8,128,384]{2,1,0:T(8,128)S(1)}, u32[]{:S(2)}) copy-start(f32[8,128,384]{2,1,0:T(8,128)S(1)} %shard_map.97.own_ref) | copy-start | bytes 4718596
  115.4 6.1 %copy-start.11 = (f32[3200,128]{1,0:T(8,128)S(1)}, f32[3200,128]{1,0:T(8,128)}, u32[]{:S(2)}) copy-start(f32[3200,128]{1,0:T(8,128)} %get-tuple-element.27) | copy-start | bytes 4915204
  121.2 40.5 %collective-permute-start.9 = (f32[16,5,5,8,128]{4,3,2,1,0:T(8,128)}, f32[16,5,5,8,128]{4,3,2,1,0:T(8,128)}, u32[]{:S(2)}, u32[]{:S(2)}) collective-permute-start(f32[16,5,5,8,128]{4,3,2,1,0:T(8,128)} %bitcast.21), channel_id=1, source_target_pairs={{0,64},{16,80},{64,0},{80,16},{1,65},{17,81},{65,1},{81,17},{2,66}... | collective-permute-start | bytes 4915208 | tf_op jit(solution)/shard_map/ppermute | solution.py:238
  124.4 40.3 %all-to-all-start.2 = ((f32[16,5,5,8,128]{4,3,2,1,0:T(8,128)}), f32[16,5,5,8,128]{4,3,2,1,0:T(8,128)S(1)}, u32[]{:S(2)}, u32[]{:S(2)}) async-start(f32[16,5,5,8,128]{4,3,2,1,0:T(8,128)} %add.17), calls=%async_computation.2 | async-start | bytes 3276800 | tf_op jit(solution)/shard_map/all_to_all | solution.py:242
  131.6 1.4 copy-start.6
  133.0 1.1 copy-start.9
  134.1 8.9 %copy-start.4 = (f32[8,128,384]{2,1,0:T(8,128)S(1)}, f32[8,128,384]{2,1,0:T(8,128)}, u32[]{:S(2)}) copy-start(f32[8,128,384]{2,1,0:T(8,128)} %copy-done.3) | copy-start | bytes 4718596
  141.3 20.5 %copy-start.12 = (f32[3200,128]{1,0:T(8,128)S(1)}, f32[3200,128]{1,0:T(8,128)}, u32[]{:S(2)}) copy-start(f32[3200,128]{1,0:T(8,128)} %get-tuple-element.31) | copy-start | bytes 4915204
  141.3 53.0 %collective-permute-start.10 = (f32[16,5,5,8,128]{4,3,2,1,0:T(8,128)}, f32[16,5,5,8,128]{4,3,2,1,0:T(8,128)}, u32[]{:S(2)}, u32[]{:S(2)}) collective-permute-start(f32[16,5,5,8,128]{4,3,2,1,0:T(8,128)} %bitcast.22), channel_id=1, source_target_pairs={{0,16},{16,0},{64,80},{80,64},{1,17},{17,1},{65,81},{81,65},{2,18}... | collective-permute-start | bytes 4915208 | tf_op jit(solution)/shard_map/ppermute | solution.py:238
  148.3 47.5 %collective-permute-start.11 = (f32[16,5,5,8,128]{4,3,2,1,0:T(8,128)}, f32[16,5,5,8,128]{4,3,2,1,0:T(8,128)}, u32[]{:S(2)}, u32[]{:S(2)}) collective-permute-start(f32[16,5,5,8,128]{4,3,2,1,0:T(8,128)} %bitcast.23), channel_id=1, source_target_pairs={{0,80},{16,64},{64,16},{80,0},{1,81},{17,65},{65,17},{81,1},{2,82}... | collective-permute-start | bytes 4915208 | tf_op jit(solution)/shard_map/ppermute | solution.py:238
  164.7 34.4 %all-to-all-start.3 = ((f32[16,5,5,8,128]{4,3,2,1,0:T(8,128)}), f32[16,5,5,8,128]{4,3,2,1,0:T(8,128)}, u32[]{:S(2)}, u32[]{:S(2)}) async-start(f32[16,5,5,8,128]{4,3,2,1,0:T(8,128)} %add.18), calls=%async_computation.3 | async-start | bytes 3276800 | tf_op jit(solution)/shard_map/all_to_all | solution.py:242
  199.1 29.2 %all-to-all-start.4 = ((f32[16,5,5,8,128]{4,3,2,1,0:T(8,128)}), f32[16,5,5,8,128]{4,3,2,1,0:T(8,128)}, u32[]{:S(2)}, u32[]{:S(2)}) async-start(f32[16,5,5,8,128]{4,3,2,1,0:T(8,128)} %add.19), calls=%async_computation.4 | async-start | bytes 3276800 | tf_op jit(solution)/shard_map/all_to_all | solution.py:242
  206.3 16.1 %collective-permute-start.1 = (f32[16,5,2,8,128]{4,3,2,1,0:T(8,128)S(1)}, f32[16,5,2,8,128]{4,3,2,1,0:T(8,128)S(1)}, u32[]{:S(2)}, u32[]{:S(2)}) collective-permute-start(f32[16,5,2,8,128]{4,3,2,1,0:T(8,128)S(1)} %bitcast.17), channel_id=1, source_target_pairs={{0,16},{16,0},{64,80},{80,64},{1,17},{17,1},{65,81},{81,65},{2,18}... | collective-permute-start | bytes 1966088 | tf_op jit(solution)/shard_map/ppermute | solution.py:238
  206.3 17.6 %collective-permute-start.3 = (f32[16,5,2,8,128]{4,3,2,1,0:T(8,128)}, f32[16,5,2,8,128]{4,3,2,1,0:T(8,128)S(1)}, u32[]{:S(2)}, u32[]{:S(2)}) collective-permute-start(f32[16,5,2,8,128]{4,3,2,1,0:T(8,128)} %bitcast.18), channel_id=1, source_target_pairs={{0,80},{16,64},{64,16},{80,0},{1,81},{17,65},{65,17},{81,1},{2,82}... | collective-permute-start | bytes 1966088 | tf_op jit(solution)/shard_map/ppermute | solution.py:238
  228.2 29.3 %all-to-all-start = ((f32[16,5,2,8,128]{4,3,2,1,0:T(8,128)}), f32[16,5,2,8,128]{4,3,2,1,0:T(8,128)}, u32[]{:S(2)}, u32[]{:S(2)}) async-start(f32[16,5,2,8,128]{4,3,2,1,0:T(8,128)} %add.15), calls=%async_computation | async-start | bytes 1310720 | tf_op jit(solution)/shard_map/all_to_all | solution.py:242
  236.2 1.0 copy-start.10
  237.2 8.1 %copy-start.2 = (bf16[2,320,256]{2,1,0:T(8,128)(2,1)S(1)}, bf16[2,320,256]{2,1,0:T(8,128)(2,1)}, u32[]{:S(2)}) copy-start(bf16[2,320,256]{2,1,0:T(8,128)(2,1)} %constant.36.clone.table_ref) | copy-start | bytes 983044

commit v3 on v2

--- a/solution.py
+++ b/solution.py
@@ -18,8 +18,9 @@
 YC = 8
 DESTS = 16
 PAIRS = 5
-LAST = (3, 2)
-VMEM_LIMIT = 50 * 1024 * 1024
+EARLY = (3, 2)
+VMEM_LIMIT = 24 * 1024 * 1024
+DEPTH_LIMIT = 50 * 1024 * 1024
 
 
 def split_table(table):
@@ -71,8 +72,8 @@
     return jnp.where(lane % 64 < 32, pltpu.roll(tail, 96, 1), -pltpu.roll(tail, 32, 1))
 
 
-def params():
-    return pltpu.CompilerParams(vmem_limit_bytes=VMEM_LIMIT)
+def params(limit=VMEM_LIMIT):
+    return pltpu.CompilerParams(vmem_limit_bytes=limit)
 
 
 def depth_kernel(group, keeps, place_ref, u_ref, v_ref, t_ref, table_ref, *out_refs):
@@ -112,7 +113,7 @@
         ],
         out_specs=[out] * len(keeps),
         out_shape=[shape] * len(keeps),
-        compiler_params=params(),
+        compiler_params=params(DEPTH_LIMIT),
         cost_estimate=pl.CostEstimate(
             flops=len(keeps) * XB * YC * N * 384 * 6, bytes_accessed=9_000_000, transcendentals=0
         ),
@@ -171,17 +172,20 @@
         ],
         out_specs=[pl.BlockSpec(shape, lambda i: (0, 0)) for shape in outs],
         out_shape=[jax.ShapeDtypeStruct(shape, jnp.float32) for shape in outs],
-        compiler_params=params(),
+        compiler_params=params(DEPTH_LIMIT),
         cost_estimate=pl.CostEstimate(flops=YC * len(blocks) * 160 * 512 * 384 * 6, bytes_accessed=7_000_000, transcendentals=0),
     )(place, own, recv, table)
     return [r.reshape(DESTS, 5, pairs, YC, LANES) for r, pairs in zip(results, sizes)]
 
 
-def second_kernel(count, fresh, base, place_ref, table_ref, *refs):
+def second_kernel(count, fresh, parts, base, place_ref, table_ref, *refs):
     out_ref = refs[-1]
     left, right = [], []
-    for side in range(count):
-        t = [refs[side][:, i, 0].reshape(DESTS * YC, LANES) for i in range(5)]
+    at = 0
+    for side in range(len(fresh)):
+        group = refs[at : at + parts[side]]
+        at += parts[side]
+        t = [sum(ref[:, i, 0].reshape(DESTS * YC, LANES) for ref in group) for i in range(5)]
         values = jnp.concatenate(t, axis=1)
         turned = jnp.concatenate([t[1], -t[0], t[3], -t[2], turn_tail(t[4])], axis=1)
         high, low = halves(jnp.concatenate([values, turned], axis=0))
@@ -212,13 +216,14 @@
 
 
 def second_stage(place, table, sides, base, before):
-    pairs = sides[0][1].shape[2]
+    values = [value for side in sides for value in side[1:]]
+    pairs = values[0].shape[2]
     block = pl.BlockSpec((DESTS, 5, 1, YC, LANES), lambda k: (0, 0, k, 0, 0))
     out = pl.BlockSpec((2, 2 * KEEP, 2 * KEEP), lambda k: (k + base, 0, 0))
     extra = [] if before is None else [before]
-    count = len(sides)
+    count = len(values)
     return pl.pallas_call(
-        functools.partial(second_kernel, count, [s[0] for s in sides], base),
+        functools.partial(second_kernel, count, [s[0] for s in sides], [len(s) - 1 for s in sides], base),
         grid=(pairs,),
         in_specs=[pl.BlockSpec(memory_space=pltpu.SMEM), pl.BlockSpec(table.shape, lambda k: (0,) * 3)]
         + [block] * count
@@ -228,9 +233,9 @@
         input_output_aliases={2 + count: 0} if extra else {},
         compiler_params=params(),
         cost_estimate=pl.CostEstimate(
-            flops=pairs * count * 320 * 256 * 640 * 6, bytes_accessed=3_000_000 * pairs, transcendentals=0
+            flops=pairs * len(sides) * 320 * 256 * 640 * 6, bytes_accessed=3_000_000 * pairs, transcendentals=0
         ),
-    )(place, table, *[s[1] for s in sides], *extra)
+    )(place, table, *values, *extra)
 
 
 def ring(value, flip_high, flip_low):
@@ -276,30 +281,36 @@
     recv = swap(send)
     (own,) = depth("01", (1,))
     near = near_ring(first(own, recv, (0,), ((PAIRS,),)))
-    far = far_ring("01", first(own, recv, (1,), ((PAIRS,),)))
+    far, far_early = first(own, recv, (1,), (EARLY,))
+    far = far_ring("01", [far])
 
     send, own = depth("00", (0, 1))
-    kept, across = first(own, swap(send), (0, 1), ((PAIRS,), (PAIRS,)))
+    kept, across, across_early = first(own, swap(send), (0, 1), ((PAIRS,), EARLY))
     across = far_ring("00", [across])
 
+    early = spread(jnp.stack([across_early, far_early], axis=1))
+    across_early = ring(early[:, 0], 0, 1)
+    far_early = ring(early[:, 1], 1, 1)
+
     send, own = depth("11", (0, 1))
-    near_last, *far_last = first(own, swap(send), (0, 1), ((PAIRS,), LAST))
+    near_last, far_last = first(own, swap(send), (0, 1), ((PAIRS,), (PAIRS,)))
     near_last = near_ring([near_last])
-    far_last = far_ring("11", far_last)
+    far_last = far_ring("11", [far_last])
 
     send, own = depth("10", (0, 1))
-    kept_last, *across_last = first(own, swap(send), (0, 1), ((PAIRS,), LAST))
-    across_last = far_ring("10", across_last)
+    kept_last, across_last = first(own, swap(send), (0, 1), ((PAIRS,), (PAIRS,)))
+    across_last = far_ring("10", [across_last])
 
     mine = gather(kept, near[0])
     other = gather(across[0], far[0])
     mine_last = gather(kept_last, near_last[0])
-    other_last = [gather(a, b) for a, b in zip(across_last, far_last)]
-
-    result = second(0, [(0, mine), (1, other)], 0, None)
+    other_last = gather(across_last[0], far_last[0])
+
+    result = second(0, [(0, mine)], 0, None)
+    result = second(0, [(1, other)], 0, result)
     result = second(1, [(0, mine_last)], 0, result)
-    result = second(1, [(1, other_last[0])], 0, result)
-    result = second(1, [(1, other_last[1])], LAST[0], result)
+    result = second(0, [(1, across_early, far_early)], EARLY[0], result)
+    result = second(1, [(1, other_last)], 0, result)
     return result[None]
 
 

time: 263 us -> 231 us (0.88); the launches traced: 261 us -> 226 us
  waiting for transfers between devices: 106 us -> 65.7 us
  local copies, waits for them, and re-layouts: 6.98 us -> 11.5 us
    ppermute x8, waiting for transfers between devices: 102 us -> 65.7 us  [ring(): return lax.ppermute(value, ('xh', 'xl'), moves)]
    pallas_call x4 -> x5, Pallas kernels: 23.9 us -> 28.5 us  [second_stage(): pl.pallas_call(functools.partial(second_kernel, count, [s[0] for s in sid...]
    all_to_all x5, waiting for transfers between devices: 3.41 us -> 0.01 us  [spread(): lax.all_to_all(value, ('z', 'y'), split_axis=0, concat_axis=0, tiled=True)]
    unnamed x30 -> x44, local copies, waits for them, and re-layouts: 6.98 us -> 10 us
    add x5 -> x4, other arithmetic: 11 us -> 10.5 us  [gather(): return spread(jnp.add(a, b))]
  transfers between devices with their start and end apart: 17 -> 17, of which waited for: 8 -> 4; matrix products, arithmetic and copies ran while one was open for 4% -> 5% of each run, Pallas kernels for 30% -> 32%
where the time goes in v3:
time: 231 us; the launch traced here: 226 us
  Pallas kernels  91.2 us (39%)
  waiting for transfers between devices  65.7 us (28%)
  starting transfers between devices  46.1 us (20%)
  other arithmetic  11.7 us (5%)
  local copies, waits for them, and re-layouts  11.5 us (5%)
    ppermute x8, waiting for transfers between devices, ring(): return lax.ppermute(value, ('xh', 'xl'), moves)  65.7 us
    all_to_all x5, starting transfers between devices, spread(): lax.all_to_all(value, ('z', 'y'), split_axis=0, concat_axis=0, tiled=True)  37.4 us
    pallas_call x5, Pallas kernels, depth_stage(): pl.pallas_call(functools.partial(depth_kernel, group, keeps), grid=(XB //...  33.1 us
    pallas_call x5, Pallas kernels, first_stage(): pl.pallas_call(functools.partial(first_kernel, blocks, splits), grid=(YC...  29.6 us
    pallas_call x5, Pallas kernels, second_stage(): pl.pallas_call(functools.partial(second_kernel, count, [s[0] for s in sid...  28.5 us
    add x4, other arithmetic, gather(): return spread(jnp.add(a, b))  10.5 us
    unnamed x44, local copies, waits for them, and re-layouts  10 us
    ppermute x8, starting transfers between devices, ring(): return lax.ppermute(value, ('xh', 'xl'), moves)  8.03 us
  transfers between devices with their start and end apart: 17, of which 4 were waited for; matrix products, arithmetic and copies ran while one was open for 5% of the time, Pallas kernels for 32%

profile of v3, /device:TPU:22, one launch (start us, length us, event | category | flops | bytes accessed | tf_op | source)
XLA Modules:
  0.0 226.5 jit_solution(13605622357549886382)
XLA Ops:
  0.0 0.1 pad_add_fusion.place_ref
  0.1 1.1 copy-done
  1.2 5.2 %shard_map.107 = f32[8,128,384]{2,1,0:T(8,128)S(1)} custom-call(s32[4]{0:T(128)S(1)} %pad_add_fusion.place_ref, f32[128,16,512]{2,1,0:T(8,128)} %u_ref.9, f32[128,16,512]{2,1,0:T(8,128)} %v_ref.9, f32[128,16,512]{2,1,0:T(8,128)} %t_ref.9, bf16[2,512,384]{2,1,0:T(8,128)(2,1)S(1)} %copy-done), custom_call_target="tpu_custom_call" | custom-call | flops 1207959552 | bytes 9000000 | tf_op jit(solution)/shard_map/pallas_call | solution.py:104
  6.4 0.1 collective-permute-start.5
  6.5 6.9 %shard_map.104 = (f32[8,128,384]{2,1,0:T(8,128)S(1)}, f32[8,128,384]{2,1,0:T(8,128)S(1)}) custom-call(s32[4]{0:T(128)S(1)} %pad_add_fusion.place_ref, f32[128,16,512]{2,1,0:T(8,128)} %u_ref.9, f32[128,16,512]{2,1,0:T(8,128)} %v_ref.9, f32[128,16,512]{2,1,0:T(8,128)} %t_ref.9, bf16[2,512,384]{2,1,0:T(8,128)(2,1)S(1)} %copy-done), custom_call_target="tpu_custom_call" | custom-call | flops 2415919104 | bytes 9000000 | tf_op jit(solution)/shard_map/pallas_call | solution.py:104
  13.4 0.6 collective-permute-start.4
  14.0 5.2 %shard_map.106.own_ref = f32[8,128,384]{2,1,0:T(8,128)S(1)} custom-call(s32[4]{0:T(128)S(1)} %pad_add_fusion.place_ref, f32[128,16,512]{2,1,0:T(8,128)} %u_ref.9, f32[128,16,512]{2,1,0:T(8,128)} %v_ref.9, f32[128,16,512]{2,1,0:T(8,128)} %t_ref.9, bf16[2,512,384]{2,1,0:T(8,128)(2,1)S(1)} %copy-done), custom_call_target="tpu_custom_call" | custom-call | flops 1207959552 | bytes 9000000 | tf_op jit(solution)/shard_map/pallas_call | solution.py:104
  19.2 1.2 copy-done.10
  20.3 4.2 %shard_map.108 = (f32[1920,128]{1,0:T(8,128)S(1)}, f32[1280,128]{1,0:T(8,128)S(1)}) custom-call(s32[4]{0:T(128)S(1)} %pad_add_fusion.place_ref, f32[8,128,384]{2,1,0:T(8,128)S(1)} %shard_map.106.own_ref, f32[8,128,384]{2,1,0:T(8,128)} %copy-done.10, bf16[2,2,2,2,160,128]{5,4,3,2,1,0:T(8,128)(2,1)S(1)} %copy-done.18), custom_call_target="tpu_custom_call" | custom-call | flops 1509949440 | bytes 7000000 | tf_op jit(solution)/shard_map/pallas_call | solution.py:164
  24.6 1.2 copy-done.21
  25.8 6.6 %shard_map.105 = (f32[3200,128]{1,0:T(8,128)}, f32[1920,128]{1,0:T(8,128)S(1)}, f32[1280,128]{1,0:T(8,128)S(1)}) custom-call(s32[4]{0:T(128)S(1)} %pad_add_fusion.place_ref, f32[8,128,384]{2,1,0:T(8,128)S(1)} %get-tuple-element.26.own_ref, f32[8,128,384]{2,1,0:T(8,128)} %copy-done.21, bf16[2,2,2,2,160,128]{5,4,3,2,1,0:T(8,128)(2,1)S(1)} %copy-done.18), custom_call_target="tpu_custom_call" | custom-call | flops 3019898880 | bytes 7000000 | tf_op jit(solution)/shard_map/pallas_call | solution.py:164
  32.4 0.9 copy-done.16
  33.3 1.2 pad_maximum_fusion
  34.5 8.4 %all-to-all-start.1 = ((f32[16,2,5,2,8,128]{5,4,3,2,1,0:T(8,128)}), f32[16,2,5,2,8,128]{5,4,3,2,1,0:T(8,128)}, u32[]{:S(2)}, u32[]{:S(2)}) async-start(f32[16,2,5,2,8,128]{5,4,3,2,1,0:T(8,128)} %pad_maximum_fusion), calls=%async_computation.1 | async-start | bytes 2621440 | tf_op jit(solution)/shard_map/all_to_all | solution.py:247
  43.0 8.0 %shard_map.102 = (f32[8,128,384]{2,1,0:T(8,128)}, f32[8,128,384]{2,1,0:T(8,128)S(1)}) custom-call(s32[4]{0:T(128)S(1)} %pad_add_fusion.place_ref, f32[128,16,512]{2,1,0:T(8,128)} %u_ref.9, f32[128,16,512]{2,1,0:T(8,128)} %v_ref.9, f32[128,16,512]{2,1,0:T(8,128)} %t_ref.9, bf16[2,512,384]{2,1,0:T(8,128)(2,1)S(1)} %copy-done.1), custom_call_target="tpu_custom_call" | custom-call | flops 2415919104 | bytes 9000000 | tf_op jit(solution)/shard_map/pallas_call | solution.py:104
  51.0 1.1 copy-done.8
  52.1 0.5 collective-permute-start.10
  52.6 0.9 collective-permute-start.9
  53.5 4.6 %shard_map.109 = f32[3200,128]{1,0:T(8,128)} custom-call(s32[4]{0:T(128)S(1)} %pad_add_fusion.place_ref, f32[8,128,384]{2,1,0:T(8,128)S(1)} %shard_map.106.own_ref, f32[8,128,384]{2,1,0:T(8,128)S(1)} %copy-done.11, bf16[2,2,2,2,160,128]{5,4,3,2,1,0:T(8,128)(2,1)S(1)} %copy-done.18), custom_call_target="tpu_custom_call" | custom-call | flops 1509949440 | bytes 7000000 | tf_op jit(solution)/shard_map/pallas_call | solution.py:164
  58.1 3.3 %collective-permute-start.11 = (f32[16,5,5,8,128]{4,3,2,1,0:T(8,128)}, f32[16,5,5,8,128]{4,3,2,1,0:T(8,128)}, u32[]{:S(2)}, u32[]{:S(2)}) collective-permute-start(f32[16,5,5,8,128]{4,3,2,1,0:T(8,128)} %bitcast.34), channel_id=1, source_target_pairs={{0,64},{16,80},{64,0},{80,16},{1,65},{17,81},{65,1},{81,17},{2,66}... | collective-permute-start | bytes 4915208 | tf_op jit(solution)/shard_map/ppermute | solution.py:243
  61.4 16.1 %collective-permute-done.10 = f32[16,5,3,8,128]{4,3,2,1,0:T(8,128)S(1)} collective-permute-done((f32[16,5,3,8,128]{4,3,2,1,0:T(8,128)S(1)}, f32[16,5,3,8,128]{4,3,2,1,0:T(8,128)S(1)}, u32[]{:S(2)}, u32[]{:S(2)}) %collective-permute-start.10) | collective-permute-done | bytes 983072 | tf_op jit(solution)/shard_map/ppermute | solution.py:243
  77.5 1.1 add.14
  78.6 7.2 %all-to-all-start.3 = ((f32[16,5,3,8,128]{4,3,2,1,0:T(8,128)}), f32[16,5,3,8,128]{4,3,2,1,0:T(8,128)S(1)}, u32[]{:S(2)}, u32[]{:S(2)}) async-start(f32[16,5,3,8,128]{4,3,2,1,0:T(8,128)} %add.14), calls=%async_computation.3 | async-start | bytes 1966080 | tf_op jit(solution)/shard_map/all_to_all | solution.py:247
  85.8 7.9 %shard_map.100 = (f32[8,128,384]{2,1,0:T(8,128)}, f32[8,128,384]{2,1,0:T(8,128)S(1)}) custom-call(s32[4]{0:T(128)S(1)} %pad_add_fusion.place_ref, f32[128,16,512]{2,1,0:T(8,128)} %u_ref.9, f32[128,16,512]{2,1,0:T(8,128)} %v_ref.9, f32[128,16,512]{2,1,0:T(8,128)} %t_ref.9, bf16[2,512,384]{2,1,0:T(8,128)(2,1)S(1)} %copy-done.1), custom_call_target="tpu_custom_call" | custom-call | flops 2415919104 | bytes 9000000 | tf_op jit(solution)/shard_map/pallas_call | solution.py:104
  93.7 1.2 copy-done.12
  95.0 7.2 %shard_map.103 = (f32[3200,128]{1,0:T(8,128)}, f32[3200,128]{1,0:T(8,128)}) custom-call(s32[4]{0:T(128)S(1)} %pad_add_fusion.place_ref, f32[8,128,384]{2,1,0:T(8,128)S(1)} %copy-done.9, f32[8,128,384]{2,1,0:T(8,128)} %collective-permute-done.2.recv_ref, bf16[2,2,2,2,160,128]{5,4,3,2,1,0:T(8,128)(2,1)S(1)} %copy-done.18), custom_call_target="tpu_custom_call" | custom-call | flops 3019898880 | bytes 7000000 | tf_op jit(solution)/shard_map/pallas_call | solution.py:164
  102.1 2.2 collective-permute-start.8
  104.3 10.4 %collective-permute-done.11 = f32[16,5,5,8,128]{4,3,2,1,0:T(8,128)} collective-permute-done((f32[16,5,5,8,128]{4,3,2,1,0:T(8,128)}, f32[16,5,5,8,128]{4,3,2,1,0:T(8,128)}, u32[]{:S(2)}, u32[]{:S(2)}) %collective-permute-start.11) | collective-permute-done | bytes 1638432 | tf_op jit(solution)/shard_map/ppermute | solution.py:243
  114.7 2.9 %add.15 = f32[16,5,5,8,128]{4,3,2,1,0:T(8,128)} add(f32[16,5,5,8,128]{4,3,2,1,0:T(8,128)S(1)} %bitcast.31, f32[16,5,5,8,128]{4,3,2,1,0:T(8,128)} %collective-permute-done.11) | non-fusion elementwise | flops 409600 | bytes 4915200 | tf_op jit(solution)/shard_map/add | solution.py:275
  117.5 1.0 copy-done.4
  118.5 7.4 %all-to-all-start.4 = ((f32[16,5,5,8,128]{4,3,2,1,0:T(8,128)}), f32[16,5,5,8,128]{4,3,2,1,0:T(8,128)S(1)}, u32[]{:S(2)}, u32[]{:S(2)}) async-start(f32[16,5,5,8,128]{4,3,2,1,0:T(8,128)} %add.15), calls=%async_computation.4 | async-start | bytes 3276800 | tf_op jit(solution)/shard_map/all_to_all | solution.py:247
  125.8 0.5 collective-permute-start.3
  126.3 1.1 copy-done.19
  127.4 7.0 %shard_map.101 = (f32[3200,128]{1,0:T(8,128)}, f32[3200,128]{1,0:T(8,128)}) custom-call(s32[4]{0:T(128)S(1)} %pad_add_fusion.place_ref, f32[8,128,384]{2,1,0:T(8,128)S(1)} %copy-done.13, f32[8,128,384]{2,1,0:T(8,128)} %collective-permute-done.recv_ref, bf16[2,2,2,2,160,128]{5,4,3,2,1,0:T(8,128)(2,1)S(1)} %copy-done.19), custom_call_target="tpu_custom_call" | custom-call | flops 3019898880 | bytes 7000000 | tf_op jit(solution)/shard_map/pallas_call | solution.py:164
  134.4 15.4 %collective-permute-done.8 = f32[16,5,5,8,128]{4,3,2,1,0:T(8,128)} collective-permute-done((f32[16,5,5,8,128]{4,3,2,1,0:T(8,128)}, f32[16,5,5,8,128]{4,3,2,1,0:T(8,128)}, u32[]{:S(2)}, u32[]{:S(2)}) %collective-permute-start.8) | collective-permute-done | bytes 1638432 | tf_op jit(solution)/shard_map/ppermute | solution.py:243
  149.8 3.3 %add.13 = f32[16,5,5,8,128]{4,3,2,1,0:T(8,128)} add(f32[16,5,5,8,128]{4,3,2,1,0:T(8,128)} %bitcast.32, f32[16,5,5,8,128]{4,3,2,1,0:T(8,128)} %collective-permute-done.8) | non-fusion elementwise | flops 409600 | bytes 4915200 | tf_op jit(solution)/shard_map/add | solution.py:275
  153.1 7.2 %all-to-all-start.2 = ((f32[16,5,5,8,128]{4,3,2,1,0:T(8,128)}), f32[16,5,5,8,128]{4,3,2,1,0:T(8,128)S(1)}, u32[]{:S(2)}, u32[]{:S(2)}) async-start(f32[16,5,5,8,128]{4,3,2,1,0:T(8,128)} %add.13), calls=%async_computation.2 | async-start | bytes 3276800 | tf_op jit(solution)/shard_map/all_to_all | solution.py:247
  160.3 23.8 %collective-permute-done.3 = f32[16,5,5,8,128]{4,3,2,1,0:T(8,128)} collective-permute-done((f32[16,5,5,8,128]{4,3,2,1,0:T(8,128)}, f32[16,5,5,8,128]{4,3,2,1,0:T(8,128)}, u32[]{:S(2)}, u32[]{:S(2)}) %collective-permute-start.3) | collective-permute-done | bytes 1638432 | tf_op jit(solution)/shard_map/ppermute | solution.py:243
  184.1 3.3 %add.12 = f32[16,5,5,8,128]{4,3,2,1,0:T(8,128)} add(f32[16,5,5,8,128]{4,3,2,1,0:T(8,128)} %collective-permute-done.1, f32[16,5,5,8,128]{4,3,2,1,0:T(8,128)} %collective-permute-done.3) | non-fusion elementwise | flops 409600 | bytes 4915200 | tf_op jit(solution)/shard_map/add | solution.py:275
  187.4 1.1 copy-done.2
  188.6 7.2 %all-to-all-start = ((f32[16,5,5,8,128]{4,3,2,1,0:T(8,128)}), f32[16,5,5,8,128]{4,3,2,1,0:T(8,128)S(1)}, u32[]{:S(2)}, u32[]{:S(2)}) async-start(f32[16,5,5,8,128]{4,3,2,1,0:T(8,128)} %add.12), calls=%async_computation | async-start | bytes 3276800 | tf_op jit(solution)/shard_map/all_to_all | solution.py:247
  195.8 1.4 slice_bitcast_fusion
  197.2 0.7 collective-permute-start.7
  197.9 5.3 %shard_map.110.refs_1_ = f32[10,320,320]{2,1,0:T(8,128)} custom-call(s32[4]{0:T(128)S(1)} %pad_add_fusion.place_ref, bf16[2,320,256]{2,1,0:T(8,128)(2,1)S(1)} %copy-done.6, f32[16,5,5,8,128]{4,3,2,1,0:T(8,128)S(1)} %all-to-all-done.4.refs_0_), custom_call_target="tpu_custom_call" | custom-call | flops 1572864000 | bytes 15000000 | tf_op jit(solution)/shard_map/pallas_call | solution.py:225
  203.3 5.2 %shard_map.111.refs_1_ = f32[10,320,320]{2,1,0:T(8,128)} custom-call(s32[4]{0:T(128)S(1)} %pad_add_fusion.place_ref, bf16[2,320,256]{2,1,0:T(8,128)(2,1)S(1)} %copy-done.6, f32[16,5,3,8,128]{4,3,2,1,0:T(8,128)S(1)} %copy-done.5, f32[10,320,320]{2,1,0:T(8,128)} %shard_map.110.refs_1_), custom_call_target="tpu_custom_call", output_to_operand_aliasing={{}: (3, {})} | custom-call | flops 943718400 | bytes 9000000 | tf_op jit(solution)/shard_map/pallas_call | solution.py:225
  208.4 7.2 %shard_map.112.refs_2_ = f32[10,320,320]{2,1,0:T(8,128)} custom-call(s32[4]{0:T(128)S(1)} %pad_add_fusion.place_ref, bf16[2,320,256]{2,1,0:T(8,128)(2,1)S(1)} %copy-done.7, f32[16,5,5,8,128]{4,3,2,1,0:T(8,128)S(1)} %copy-done.3, f32[10,320,320]{2,1,0:T(8,128)} %shard_map.111.refs_1_), custom_call_target="tpu_custom_call", output_to_operand_aliasing={{}: (3, {})} | custom-call | flops 1572864000 | bytes 15000000 | tf_op jit(solution)/shard_map/pallas_call | solution.py:225
  215.7 3.5 %shard_map.113.refs_1_ = f32[10,320,320]{2,1,0:T(8,128)} custom-call(s32[4]{0:T(128)S(1)} %pad_add_fusion.place_ref, bf16[2,320,256]{2,1,0:T(8,128)(2,1)S(1)} %copy-done.6, f32[16,5,2,8,128]{4,3,2,1,0:T(8,128)S(1)} %collective-permute-done.6.refs_0_, f32[16,5,2,8,128]{4,3,2,1,0:T(8,128)S(1)} %collective-permute-done.7.refs_1_, ...), custom_call_target="tpu_custom_call", output_to_operand_aliasing={{}: (4, {})} | custom-call | flops 629145600 | bytes 6000000 | tf_op jit(solution)/shard_map/pallas_call | solution.py:225
  219.2 7.2 %shard_map.114 = f32[10,320,320]{2,1,0:T(8,128)} custom-call(s32[4]{0:T(128)S(1)} %pad_add_fusion.place_ref, bf16[2,320,256]{2,1,0:T(8,128)(2,1)S(1)} %copy-done.7, f32[16,5,5,8,128]{4,3,2,1,0:T(8,128)S(1)} %all-to-all-done.refs_0_, f32[10,320,320]{2,1,0:T(8,128)} %shard_map.113.refs_1_), custom_call_target="tpu_custom_call", output_to_operand_aliasing={{}: (3, {})} | custom-call | flops 1572864000 | bytes 15000000 | tf_op jit(solution)/shard_map/pallas_call | solution.py:225
  (52 shorter events, 0.1 us)
Async XLA Ops:
  0.1 1.1 copy-start
  6.4 12.8 %collective-permute-start.5 = (f32[8,128,384]{2,1,0:T(8,128)S(1)}, f32[8,128,384]{2,1,0:T(8,128)S(1)}, u32[]{:S(2)}, u32[]{:S(2)}) collective-permute-start(f32[8,128,384]{2,1,0:T(8,128)S(1)} %shard_map.107), channel_id=1, source_target_pairs={{0,32},{32,0},{1,33},{33,1},{2,34},{34,2},{3,35},{35,3},{4,36},{36... | collective-permute-start | bytes 4718600 | tf_op jit(solution)/shard_map/ppermute | solution.py:263
  13.4 6.9 %copy-start.18 = (bf16[2,2,2,2,160,128]{5,4,3,2,1,0:T(8,128)(2,1)S(1)}, bf16[2,2,2,2,160,128]{5,4,3,2,1,0:T(8,128)(2,1)}, u32[]{:S(2)}) copy-start(bf16[2,2,2,2,160,128]{5,4,3,2,1,0:T(8,128)(2,1)} %constant.33.clone.table_ref) | copy-start | bytes 1966084
  13.4 11.1 %collective-permute-start.4 = (f32[8,128,384]{2,1,0:T(8,128)S(1)}, f32[8,128,384]{2,1,0:T(8,128)S(1)}, u32[]{:S(2)}, u32[]{:S(2)}) collective-permute-start(f32[8,128,384]{2,1,0:T(8,128)S(1)} %get-tuple-element.27), channel_id=1, source_target_pairs={{0,32},{32,0},{1,33},{33,1},{2,34},{34,2},{3,35},{35,3},{4,36},{36... | collective-permute-start | bytes 4718600 | tf_op jit(solution)/shard_map/ppermute | solution.py:263
  19.1 1.2 copy-start.10
  24.5 7.9 %copy-start.14 = (f32[1920,128]{1,0:T(8,128)}, f32[1920,128]{1,0:T(8,128)S(1)}, u32[]{:S(2)}) copy-start(f32[1920,128]{1,0:T(8,128)S(1)} %get-tuple-element.33) | copy-start | bytes 2949124
  24.6 1.2 copy-start.21
  32.4 0.9 copy-start.16
  34.5 8.4 %copy-start.1 = (bf16[2,512,384]{2,1,0:T(8,128)(2,1)S(1)}, bf16[2,512,384]{2,1,0:T(8,128)(2,1)}, u32[]{:S(2)}) copy-start(bf16[2,512,384]{2,1,0:T(8,128)(2,1)} %constant.34.clone.table_ref) | copy-start | bytes 2359300
  34.5 44.0 %all-to-all-start.1 = ((f32[16,2,5,2,8,128]{5,4,3,2,1,0:T(8,128)}), f32[16,2,5,2,8,128]{5,4,3,2,1,0:T(8,128)}, u32[]{:S(2)}, u32[]{:S(2)}) async-start(f32[16,2,5,2,8,128]{5,4,3,2,1,0:T(8,128)} %pad_maximum_fusion), calls=%async_computation.1 | async-start | bytes 2621440 | tf_op jit(solution)/shard_map/all_to_all | solution.py:247
  43.0 9.2 %copy-start.15 = (f32[1920,128]{1,0:T(8,128)S(1)}, f32[1920,128]{1,0:T(8,128)}, u32[]{:S(2)}) copy-start(f32[1920,128]{1,0:T(8,128)} %copy-done.14) | copy-start | bytes 2949124
  43.0 9.7 %copy-start.17 = (f32[1920,128]{1,0:T(8,128)S(1)}, f32[1920,128]{1,0:T(8,128)}, u32[]{:S(2)}) copy-start(f32[1920,128]{1,0:T(8,128)} %copy-done.16) | copy-start | bytes 2949124
  43.0 10.5 %copy-start.11 = (f32[8,128,384]{2,1,0:T(8,128)S(1)}, f32[8,128,384]{2,1,0:T(8,128)}, u32[]{:S(2)}) copy-start(f32[8,128,384]{2,1,0:T(8,128)} %copy-done.10) | copy-start | bytes 4718596
  51.0 1.1 copy-start.8
  52.1 42.8 %collective-permute-start.2 = (f32[8,128,384]{2,1,0:T(8,128)}, f32[8,128,384]{2,1,0:T(8,128)}, u32[]{:S(2)}, u32[]{:S(2)}) collective-permute-start(f32[8,128,384]{2,1,0:T(8,128)} %get-tuple-element.24), channel_id=1, source_target_pairs={{0,32},{32,0},{1,33},{33,1},{2,34},{34,2},{3,35},{35,3},{4,36},{36... | collective-permute-start | bytes 4718600 | tf_op jit(solution)/shard_map/ppermute | solution.py:263
  52.1 25.4 %collective-permute-start.10 = (f32[16,5,3,8,128]{4,3,2,1,0:T(8,128)S(1)}, f32[16,5,3,8,128]{4,3,2,1,0:T(8,128)S(1)}, u32[]{:S(2)}, u32[]{:S(2)}) collective-permute-start(f32[16,5,3,8,128]{4,3,2,1,0:T(8,128)S(1)} %bitcast.29), channel_id=1, source_target_pairs={{0,80},{16,64},{64,16},{80,0},{1,81},{17,65},{65,17},{81,1},{2,82}... | collective-permute-start | bytes 2949128 | tf_op jit(solution)/shard_map/ppermute | solution.py:243
  52.6 24.9 %collective-permute-start.9 = (f32[16,5,3,8,128]{4,3,2,1,0:T(8,128)S(1)}, f32[16,5,3,8,128]{4,3,2,1,0:T(8,128)S(1)}, u32[]{:S(2)}, u32[]{:S(2)}) collective-permute-start(f32[16,5,3,8,128]{4,3,2,1,0:T(8,128)S(1)} %bitcast.30), channel_id=1, source_target_pairs={{0,16},{16,0},{64,80},{80,64},{1,17},{17,1},{65,81},{81,65},{2,18}... | collective-permute-start | bytes 2949128 | tf_op jit(solution)/shard_map/ppermute | solution.py:243
  58.1 56.6 %collective-permute-start.11 = (f32[16,5,5,8,128]{4,3,2,1,0:T(8,128)}, f32[16,5,5,8,128]{4,3,2,1,0:T(8,128)}, u32[]{:S(2)}, u32[]{:S(2)}) collective-permute-start(f32[16,5,5,8,128]{4,3,2,1,0:T(8,128)} %bitcast.34), channel_id=1, source_target_pairs={{0,64},{16,80},{64,0},{80,16},{1,65},{17,81},{65,1},{81,17},{2,66}... | collective-permute-start | bytes 4915208 | tf_op jit(solution)/shard_map/ppermute | solution.py:243
  78.6 38.9 %all-to-all-start.3 = ((f32[16,5,3,8,128]{4,3,2,1,0:T(8,128)}), f32[16,5,3,8,128]{4,3,2,1,0:T(8,128)S(1)}, u32[]{:S(2)}, u32[]{:S(2)}) async-start(f32[16,5,3,8,128]{4,3,2,1,0:T(8,128)} %add.14), calls=%async_computation.3 | async-start | bytes 1966080 | tf_op jit(solution)/shard_map/all_to_all | solution.py:247
  85.8 9.1 %copy-start.9 = (f32[8,128,384]{2,1,0:T(8,128)S(1)}, f32[8,128,384]{2,1,0:T(8,128)}, u32[]{:S(2)}) copy-start(f32[8,128,384]{2,1,0:T(8,128)} %copy-done.8) | copy-start | bytes 4718596
  93.7 1.2 copy-start.12
  94.9 31.4 %collective-permute-start = (f32[8,128,384]{2,1,0:T(8,128)}, f32[8,128,384]{2,1,0:T(8,128)}, u32[]{:S(2)}, u32[]{:S(2)}) collective-permute-start(f32[8,128,384]{2,1,0:T(8,128)} %get-tuple-element.21), channel_id=1, source_target_pairs={{0,32},{32,0},{1,33},{33,1},{2,34},{34,2},{3,35},{35,3},{4,36},{36... | collective-permute-start | bytes 4718600 | tf_op jit(solution)/shard_map/ppermute | solution.py:263
  95.0 19.7 %copy-start.20 = (f32[3200,128]{1,0:T(8,128)S(1)}, f32[3200,128]{1,0:T(8,128)}, u32[]{:S(2)}) copy-start(f32[3200,128]{1,0:T(8,128)} %get-tuple-element.34) | copy-start | bytes 4915204
  102.1 47.7 %collective-permute-start.8 = (f32[16,5,5,8,128]{4,3,2,1,0:T(8,128)}, f32[16,5,5,8,128]{4,3,2,1,0:T(8,128)}, u32[]{:S(2)}, u32[]{:S(2)}) collective-permute-start(f32[16,5,5,8,128]{4,3,2,1,0:T(8,128)} %bitcast.35), channel_id=1, source_target_pairs={{0,64},{16,80},{64,0},{80,16},{1,65},{17,81},{65,1},{81,17},{2,66}... | collective-permute-start | bytes 4915208 | tf_op jit(solution)/shard_map/ppermute | solution.py:243
  117.5 1.0 copy-start.4
  118.5 7.8 %copy-start.13 = (f32[8,128,384]{2,1,0:T(8,128)S(1)}, f32[8,128,384]{2,1,0:T(8,128)}, u32[]{:S(2)}) copy-start(f32[8,128,384]{2,1,0:T(8,128)} %copy-done.12) | copy-start | bytes 4718596
  118.5 34.6 %all-to-all-start.4 = ((f32[16,5,5,8,128]{4,3,2,1,0:T(8,128)}), f32[16,5,5,8,128]{4,3,2,1,0:T(8,128)S(1)}, u32[]{:S(2)}, u32[]{:S(2)}) async-start(f32[16,5,5,8,128]{4,3,2,1,0:T(8,128)} %add.15), calls=%async_computation.4 | async-start | bytes 3276800 | tf_op jit(solution)/shard_map/all_to_all | solution.py:247
  125.8 58.3 %collective-permute-start.3 = (f32[16,5,5,8,128]{4,3,2,1,0:T(8,128)}, f32[16,5,5,8,128]{4,3,2,1,0:T(8,128)}, u32[]{:S(2)}, u32[]{:S(2)}) collective-permute-start(f32[16,5,5,8,128]{4,3,2,1,0:T(8,128)} %bitcast.33), channel_id=1, source_target_pairs={{0,80},{16,64},{64,16},{80,0},{1,81},{17,65},{65,17},{81,1},{2,82}... | collective-permute-start | bytes 4915208 | tf_op jit(solution)/shard_map/ppermute | solution.py:243
  126.3 1.1 copy-start.19
  134.4 49.7 %collective-permute-start.1 = (f32[16,5,5,8,128]{4,3,2,1,0:T(8,128)}, f32[16,5,5,8,128]{4,3,2,1,0:T(8,128)}, u32[]{:S(2)}, u32[]{:S(2)}) collective-permute-start(f32[16,5,5,8,128]{4,3,2,1,0:T(8,128)} %bitcast.36), channel_id=1, source_target_pairs={{0,16},{16,0},{64,80},{80,64},{1,17},{17,1},{65,81},{81,65},{2,18}... | collective-permute-start | bytes 4915208 | tf_op jit(solution)/shard_map/ppermute | solution.py:243
  153.1 34.4 %all-to-all-start.2 = ((f32[16,5,5,8,128]{4,3,2,1,0:T(8,128)}), f32[16,5,5,8,128]{4,3,2,1,0:T(8,128)S(1)}, u32[]{:S(2)}, u32[]{:S(2)}) async-start(f32[16,5,5,8,128]{4,3,2,1,0:T(8,128)} %add.13), calls=%async_computation.2 | async-start | bytes 3276800 | tf_op jit(solution)/shard_map/all_to_all | solution.py:247
  187.4 1.2 copy-start.2
  188.6 30.6 %all-to-all-start = ((f32[16,5,5,8,128]{4,3,2,1,0:T(8,128)}), f32[16,5,5,8,128]{4,3,2,1,0:T(8,128)S(1)}, u32[]{:S(2)}, u32[]{:S(2)}) async-start(f32[16,5,5,8,128]{4,3,2,1,0:T(8,128)} %add.12), calls=%async_computation | async-start | bytes 3276800 | tf_op jit(solution)/shard_map/all_to_all | solution.py:247
  195.8 2.1 copy-start.6
  197.2 18.4 %collective-permute-start.7 = (f32[16,5,2,8,128]{4,3,2,1,0:T(8,128)S(1)}, f32[16,5,2,8,128]{4,3,2,1,0:T(8,128)S(1)}, u32[]{:S(2)}, u32[]{:S(2)}) collective-permute-start(f32[16,5,2,8,128]{4,3,2,1,0:T(8,128)S(1)} %get-tuple-element.35), channel_id=1, source_target_pairs={{0,80},{16,64},{64,16},{80,0},{1,81},{17,65},{65,17},{81,1},{2,82}... | collective-permute-start | bytes 1966088 | tf_op jit(solution)/shard_map/ppermute | solution.py:243
  197.9 5.3 %copy-start.5 = (f32[16,5,3,8,128]{4,3,2,1,0:T(8,128)S(1)}, f32[16,5,3,8,128]{4,3,2,1,0:T(8,128)}, u32[]{:S(2)}) copy-start(f32[16,5,3,8,128]{4,3,2,1,0:T(8,128)} %copy-done.4) | copy-start | bytes 2949124
  197.9 17.8 %collective-permute-start.6 = (f32[16,5,2,8,128]{4,3,2,1,0:T(8,128)S(1)}, f32[16,5,2,8,128]{4,3,2,1,0:T(8,128)S(1)}, u32[]{:S(2)}, u32[]{:S(2)}) collective-permute-start(f32[16,5,2,8,128]{4,3,2,1,0:T(8,128)S(1)} %get-tuple-element.36), channel_id=1, source_target_pairs={{0,16},{16,0},{64,80},{80,64},{1,17},{17,1},{65,81},{81,65},{2,18}... | collective-permute-start | bytes 1966088 | tf_op jit(solution)/shard_map/ppermute | solution.py:243
  203.3 5.2 %copy-start.3 = (f32[16,5,5,8,128]{4,3,2,1,0:T(8,128)S(1)}, f32[16,5,5,8,128]{4,3,2,1,0:T(8,128)}, u32[]{:S(2)}) copy-start(f32[16,5,5,8,128]{4,3,2,1,0:T(8,128)} %copy-done.2) | copy-start | bytes 4915204
  203.3 5.2 %copy-start.7 = (bf16[2,320,256]{2,1,0:T(8,128)(2,1)S(1)}, bf16[2,320,256]{2,1,0:T(8,128)(2,1)}, u32[]{:S(2)}) copy-start(bf16[2,320,256]{2,1,0:T(8,128)(2,1)} %constant.36.clone.table_ref) | copy-start | bytes 983044

commit v4 on v3

--- a/solution.py
+++ b/solution.py
@@ -15,6 +15,7 @@
 KEEP = 160
 LANES = 128
 XB = 128
+XSTEP = 32
 YC = 8
 DESTS = 16
 PAIRS = 5
@@ -44,8 +45,8 @@
 def first_table():
     half, e, pair, dest = np.meshgrid(np.arange(2), np.arange(2), np.arange(5), np.arange(16), indexing="ij")
     waves = (half * 160 + dest * 10 + 2 * pair + e - KEEP).reshape(2, KEEP)
-    angle = angles(np.arange(2 * XB)[None, None, :], waves[:, :, None]).reshape(2, KEEP, 2, XB)
-    table = np.stack([np.cos(angle), np.sin(angle)], axis=1).transpose(0, 1, 3, 2, 4)
+    angle = angles(np.arange(XB)[None, None, :], waves[:, :, None])
+    table = np.stack([np.cos(angle), np.sin(angle)], axis=1)
     return split_table(table / np.sqrt(N))
 
 
@@ -76,48 +77,70 @@
     return pltpu.CompilerParams(vmem_limit_bytes=limit)
 
 
-def depth_kernel(group, keeps, place_ref, u_ref, v_ref, t_ref, table_ref, *out_refs):
+def depth_kernel(chunk, group, keeps, place_ref, table_ref, *refs):
+    count = len(keeps)
+    fields, outs = refs[:3], refs[3 : 3 + count]
+    held, made, in_sems, out_sems = refs[3 + count :]
     first = place_ref[0] == 0
     squares = place_ref[1] == group
-    u, v, t = u_ref[...], v_ref[...], t_ref[...]
-    rows = YC * u.shape[0]
-    highs, lows = [], []
-    for keep in keeps:
-        swap = first if keep == 0 else ~first
-        a = jnp.where(squares & swap, v, u)
-        product = a * jnp.where(squares, a, jnp.where(swap, t, v))
-        high, low = halves(jnp.swapaxes(product, 0, 1).reshape(rows, N))
-        highs.append(high)
-        lows.append(low)
-    high, low = jnp.concatenate(highs, axis=0), jnp.concatenate(lows, axis=0)
-    table = jnp.concatenate([table_ref[0], table_ref[0], table_ref[1]], axis=0)
-    out = dot(jnp.concatenate([high, low, high], axis=1), table)
-    for i, ref in enumerate(out_refs):
-        ref[...] = out[i * rows : (i + 1) * rows].reshape(YC, rows // YC, 384)
+    rows = YC * XSTEP
+
+    def load(f, i):
+        source = fields[f].at[pl.ds(i * XSTEP, XSTEP), pl.ds(chunk * YC, YC)]
+        return pltpu.make_async_copy(source, held.at[f, i], in_sems.at[f, i])
+
+    def save(k, i):
+        target = outs[k].at[:, pl.ds(i * XSTEP, XSTEP)]
+        return pltpu.make_async_copy(made.at[k, i], target, out_sems.at[k, i])
+
+    for i in range(XB // XSTEP):
+        for f in range(3):
+            load(f, i).start()
+
+    def step(i, carry):
+        for f in range(3):
+            load(f, i).wait()
+        u, v, t = held[0, i], held[1, i], held[2, i]
+        highs, lows = [], []
+        for keep in keeps:
+            swap = first if keep == 0 else ~first
+            a = jnp.where(squares & swap, v, u)
+            product = a * jnp.where(squares, a, jnp.where(swap, t, v))
+            high, low = halves(jnp.swapaxes(product, 0, 1).reshape(rows, N))
+            highs.append(high)
+            lows.append(low)
+        high, low = jnp.concatenate(highs, axis=0), jnp.concatenate(lows, axis=0)
+        table = jnp.concatenate([table_ref[0], table_ref[0], table_ref[1]], axis=0)
+        out = dot(jnp.concatenate([high, low, high], axis=1), table)
+        for k in range(count):
+            made[k, i] = out[k * rows : (k + 1) * rows].reshape(YC, XSTEP, 384)
+            save(k, i).start()
+        return carry
+
+    lax.fori_loop(0, XB // XSTEP, step, 0)
+    for i in range(XB // XSTEP):
+        for k in range(count):
+            save(k, i).wait()
 
 
 def depth_stage(place, u, v, t, table, chunk, group, keeps):
-    xb = 32
-    block = pl.BlockSpec((xb, YC, N), lambda i: (i, chunk, 0))
-    out = pl.BlockSpec((YC, xb, 384), lambda i: (0, i, 0))
+    steps, count = XB // XSTEP, len(keeps)
     shape = jax.ShapeDtypeStruct((YC, XB, 384), jnp.float32)
+    far = pl.BlockSpec(memory_space=pltpu.HBM)
     return pl.pallas_call(
-        functools.partial(depth_kernel, group, keeps),
-        grid=(XB // xb,),
-        in_specs=[
-            pl.BlockSpec(memory_space=pltpu.SMEM),
-            block,
-            block,
-            block,
-            pl.BlockSpec((2, N, 384), lambda i: (0, 0, 0)),
+        functools.partial(depth_kernel, chunk, group, keeps),
+        in_specs=[pl.BlockSpec(memory_space=pltpu.SMEM), pl.BlockSpec(memory_space=pltpu.VMEM), far, far, far],
+        out_specs=[far] * count,
+        out_shape=[shape] * count,
+        scratch_shapes=[
+            pltpu.VMEM((3, steps, XSTEP, YC, N), jnp.float32),
+            pltpu.VMEM((count, steps, YC, XSTEP, 384), jnp.float32),
+            pltpu.SemaphoreType.DMA((3, steps)),
+            pltpu.SemaphoreType.DMA((count, steps)),
         ],
-        out_specs=[out] * len(keeps),
-        out_shape=[shape] * len(keeps),
         compiler_params=params(DEPTH_LIMIT),
-        cost_estimate=pl.CostEstimate(
-            flops=len(keeps) * XB * YC * N * 384 * 6, bytes_accessed=9_000_000, transcendentals=0
-        ),
-    )(place, u, v, t, table)
+        cost_estimate=pl.CostEstimate(flops=count * XB * YC * N * 384 * 6, bytes_accessed=9_000_000, transcendentals=0),
+    )(place, table, u, v, t)
 
 
 def first_kernel(blocks, splits, place_ref, own_ref, recv_ref, table_ref, *refs):
@@ -131,8 +154,17 @@
     high, low = halves(jnp.concatenate(sides, axis=1))
     data = jnp.concatenate([high, low, high], axis=0)
 
+    row = lax.broadcasted_iota(jnp.int32, (KEEP, 1), 0)
+    e = row // 80
+    q = (row // 16 + row + e) & 1
+    turns = [jnp.where(flip == 1, -1.0, 1.0).astype(jnp.bfloat16) for flip in (q ^ e, q)]
+
     def rows_of(half):
-        parts = [[table_ref[part, half, cs, core ^ j] for cs in range(2) for j in range(2)] for part in range(2)]
+        parts = []
+        for part in range(2):
+            plain = [table_ref[part, half, cs] for cs in range(2)]
+            moved = [jnp.concatenate([plain[cs][:80], plain[1 - cs][80:]], axis=0) * turns[cs] for cs in range(2)]
+            parts.append([jnp.where(core == j, plain[cs], moved[cs]) for cs in range(2) for j in range(2)])
         return jnp.concatenate(parts[0] + parts[0] + parts[1], axis=1)
 
     out = dot(jnp.concatenate([rows_of(low_half ^ b) for b in blocks], axis=0), data)
@@ -168,7 +200,7 @@
             pl.BlockSpec(memory_space=pltpu.SMEM),
             block,
             block,
-            pl.BlockSpec(table.shape, lambda i: (0,) * 6),
+            pl.BlockSpec(table.shape, lambda i: (0,) * 5),
         ],
         out_specs=[pl.BlockSpec(shape, lambda i: (0, 0)) for shape in outs],
         out_shape=[jax.ShapeDtypeStruct(shape, jnp.float32) for shape in outs],
@@ -178,58 +210,91 @@
     return [r.reshape(DESTS, 5, pairs, YC, LANES) for r, pairs in zip(results, sizes)]
 
 
-def second_kernel(count, fresh, parts, base, place_ref, table_ref, *refs):
-    out_ref = refs[-1]
-    left, right = [], []
-    at = 0
-    for side in range(len(fresh)):
-        group = refs[at : at + parts[side]]
-        at += parts[side]
-        t = [sum(ref[:, i, 0].reshape(DESTS * YC, LANES) for ref in group) for i in range(5)]
-        values = jnp.concatenate(t, axis=1)
-        turned = jnp.concatenate([t[1], -t[0], t[3], -t[2], turn_tail(t[4])], axis=1)
-        high, low = halves(jnp.concatenate([values, turned], axis=0))
-        odd = lax.broadcasted_iota(jnp.int32, (2 * KEEP, 1), 0) % 2 == 1
-        flip = odd & ((place_ref[3] ^ fresh[side]) == 1)
-        sign = jnp.where(flip, -1.0, 1.0).astype(jnp.bfloat16)
-        left += [table_ref[0] * sign, table_ref[0] * sign, table_ref[1] * sign]
-        right += [high, low, high]
-    out = dot(jnp.concatenate(left, axis=1), jnp.concatenate(right, axis=0))
-    tail = out[:, 512:]
-    lane = lax.broadcasted_iota(jnp.int32, tail.shape, 1)
-    for e in range(2):
-        re, im = out[:, 256 * e : 256 * e + 128], out[:, 256 * e + 128 : 256 * e + 256]
-        moved = pltpu.roll(im, 32, 1)
-        ends = tail if e == 0 else pltpu.roll(tail, 64, 1)
-        pieces = [re, jnp.where(lane < 32, ends, moved), jnp.where(lane < 32, moved, ends)[:, :64]]
-        for i, piece in enumerate(pieces):
-            span = slice(128 * i, min(128 * (i + 1), 320))
-            if len(refs) > count + 1:
-                piece = piece + refs[count][e, :, span]
-            out_ref[e, :, span] = piece
-
-    @pl.when((place_ref[2] == 1) & (pl.program_id(0) + base == 0))
-    def _():
-        row = out_ref[0, KEEP : KEEP + 1, 0:128]
-        first = lax.broadcasted_iota(jnp.int32, row.shape, 1) == 0
-        out_ref[0, KEEP : KEEP + 1, 0:128] = jnp.where(first, 0.0, row)
+def second_kernel(fresh, parts, base, pairs, adds, place_ref, table_ref, *refs):
+    count = sum(parts)
+    sides, past, out_ref = refs[:count], refs[count], refs[count + adds]
+    held, total, in_sems, past_sems, out_sems = refs[count + adds + 1 :]
+
+    def load(s, p):
+        return pltpu.make_async_copy(sides[s].at[:, :, p], held.at[s, p], in_sems.at[s, p])
+
+    def recall(p):
+        return pltpu.make_async_copy(past.at[pl.ds(2 * (p + base), 2)], total.at[p], past_sems.at[p])
+
+    def save(p):
+        return pltpu.make_async_copy(total.at[p], out_ref.at[pl.ds(2 * (p + base), 2)], out_sems.at[p])
+
+    for p in range(pairs):
+        for s in range(count):
+            load(s, p).start()
+        if adds:
+            recall(p).start()
+
+    def step(p, carry):
+        left, right = [], []
+        at = 0
+        for s in range(count):
+            load(s, p).wait()
+        for side in range(len(fresh)):
+            group = range(at, at + parts[side])
+            at += parts[side]
+            t = [sum(held[s, p, :, i].reshape(DESTS * YC, LANES) for s in group) for i in range(5)]
+            values = jnp.concatenate(t, axis=1)
+            turned = jnp.concatenate([t[1], -t[0], t[3], -t[2], turn_tail(t[4])], axis=1)
+            high, low = halves(jnp.concatenate([values, turned], axis=0))
+            odd = lax.broadcasted_iota(jnp.int32, (2 * KEEP, 1), 0) % 2 == 1
+            flip = odd & ((place_ref[3] ^ fresh[side]) == 1)
+            sign = jnp.where(flip, -1.0, 1.0).astype(jnp.bfloat16)
+            left += [table_ref[0] * sign, table_ref[0] * sign, table_ref[1] * sign]
+            right += [high, low, high]
+        out = dot(jnp.concatenate(left, axis=1), jnp.concatenate(right, axis=0))
+        tail = out[:, 512:]
+        lane = lax.broadcasted_iota(jnp.int32, tail.shape, 1)
+        if adds:
+            recall(p).wait()
+        for e in range(2):
+            re, im = out[:, 256 * e : 256 * e + 128], out[:, 256 * e + 128 : 256 * e + 256]
+            moved = pltpu.roll(im, 32, 1)
+            ends = tail if e == 0 else pltpu.roll(tail, 64, 1)
+            pieces = [re, jnp.where(lane < 32, ends, moved), jnp.where(lane < 32, moved, ends)[:, :64]]
+            for i, piece in enumerate(pieces):
+                span = slice(128 * i, min(128 * (i + 1), 320))
+                total[p, e, :, span] = piece + total[p, e, :, span] if adds else piece
+
+        @pl.when((place_ref[2] == 1) & (p + base == 0))
+        def _():
+            row = total[0, 0, KEEP : KEEP + 1, 0:128]
+            first = lax.broadcasted_iota(jnp.int32, row.shape, 1) == 0
+            total[0, 0, KEEP : KEEP + 1, 0:128] = jnp.where(first, 0.0, row)
+
+        save(p).start()
+        return carry
+
+    lax.fori_loop(0, pairs, step, 0)
+    for p in range(pairs):
+        save(p).wait()
 
 
 def second_stage(place, table, sides, base, before):
     values = [value for side in sides for value in side[1:]]
     pairs = values[0].shape[2]
-    block = pl.BlockSpec((DESTS, 5, 1, YC, LANES), lambda k: (0, 0, k, 0, 0))
-    out = pl.BlockSpec((2, 2 * KEEP, 2 * KEEP), lambda k: (k + base, 0, 0))
     extra = [] if before is None else [before]
     count = len(values)
+    far = pl.BlockSpec(memory_space=pltpu.HBM)
+    parts = [len(s) - 1 for s in sides]
     return pl.pallas_call(
-        functools.partial(second_kernel, count, [s[0] for s in sides], [len(s) - 1 for s in sides], base),
-        grid=(pairs,),
-        in_specs=[pl.BlockSpec(memory_space=pltpu.SMEM), pl.BlockSpec(table.shape, lambda k: (0,) * 3)]
-        + [block] * count
-        + [out] * len(extra),
-        out_specs=out,
+        functools.partial(second_kernel, [s[0] for s in sides], parts, base, pairs, len(extra)),
+        in_specs=[pl.BlockSpec(memory_space=pltpu.SMEM), pl.BlockSpec(memory_space=pltpu.VMEM)]
+        + [far] * (count + len(extra)),
+        out_specs=far,
         out_shape=jax.ShapeDtypeStruct((2 * PAIRS, 2 * KEEP, 2 * KEEP), jnp.float32),
+        scratch_shapes=[
+            pltpu.VMEM((count, pairs, DESTS, 5, YC, LANES), jnp.float32),
+            pltpu.VMEM((pairs, 2, 2 * KEEP, 2 * KEEP), jnp.float32),
+            pltpu.SemaphoreType.DMA((count, pairs)),
+            pltpu.SemaphoreType.DMA((pairs,)),
+            pltpu.SemaphoreType.DMA((pairs,)),
+        ],
         input_output_aliases={2 + count: 0} if extra else {},
         compiler_params=params(),
         cost_estimate=pl.CostEstimate(

time: 231 us -> 231 us (level)
  transfers between devices with their start and end apart: 17 -> 17, of which waited for: 4 -> 5; matrix products, arithmetic and copies ran while one was open for 5% -> 5% of each run, Pallas kernels for 32% -> 32%
where the time goes in v4:
time: 231 us; the launch traced here: 227 us
  Pallas kernels  91.3 us (40%)
  waiting for transfers between devices  66.2 us (29%)
  starting transfers between devices  46.1 us (20%)
  other arithmetic  11.7 us (5%)
  local copies, waits for them, and re-layouts  11.3 us (5%)
    ppermute x8, waiting for transfers between devices, ring(): return lax.ppermute(value, ('xh', 'xl'), moves)  66.2 us
    all_to_all x5, starting transfers between devices, spread(): lax.all_to_all(value, ('z', 'y'), split_axis=0, concat_axis=0, tiled=True)  37.5 us
    pallas_call x5, Pallas kernels, depth_stage(): pl.pallas_call(functools.partial(depth_kernel, chunk, group, keeps), in_s...  36.1 us
    pallas_call x5, Pallas kernels, first_stage(): pl.pallas_call(functools.partial(first_kernel, blocks, splits), grid=(YC...  29.8 us
    pallas_call x5, Pallas kernels, second_stage(): pl.pallas_call(functools.partial(second_kernel, [s[0] for s in sides], pa...  25.4 us
    add x4, other arithmetic, gather(): return spread(jnp.add(a, b))  10.5 us
    unnamed x44, local copies, waits for them, and re-layouts  9.91 us
    ppermute x8, starting transfers between devices, ring(): return lax.ppermute(value, ('xh', 'xl'), moves)  8.02 us
  transfers between devices with their start and end apart: 17, of which 5 were waited for; matrix products, arithmetic and copies ran while one was open for 5% of the time, Pallas kernels for 32%

profile of v4, /device:TPU:22, one launch (start us, length us, event | category | flops | bytes accessed | tf_op | source)
XLA Modules:
  0.0 227.2 jit_solution(708269392109438611)
XLA Ops:
  0.1 1.1 copy-done
  1.2 5.4 %shard_map.107 = f32[8,128,384]{2,1,0:T(8,128)S(1)} custom-call(s32[4]{0:T(128)S(1)} %pad_add_fusion.place_ref, bf16[2,512,384]{2,1,0:T(8,128)(2,1)S(1)} %copy-done, f32[128,16,512]{2,1,0:T(8,128)} %refs_0_.9, f32[128,16,512]{2,1,0:T(8,128)} %refs_1_.9, f32[128,16,512]{2,1,0:T(8,128)} %refs_2_.9), custom_call_target="tpu_custom_call" | custom-call | flops 1207959552 | bytes 9000000 | tf_op jit(solution)/shard_map/pallas_call | solution.py:130
  6.6 0.1 collective-permute-start.5
  6.7 8.0 %shard_map.104 = (f32[8,128,384]{2,1,0:T(8,128)S(1)}, f32[8,128,384]{2,1,0:T(8,128)S(1)}) custom-call(s32[4]{0:T(128)S(1)} %pad_add_fusion.place_ref, bf16[2,512,384]{2,1,0:T(8,128)(2,1)S(1)} %copy-done, f32[128,16,512]{2,1,0:T(8,128)} %refs_0_.9, f32[128,16,512]{2,1,0:T(8,128)} %refs_1_.9, f32[128,16,512]{2,1,0:T(8,128)} %refs_2_.9), custom_call_target="tpu_custom_call" | custom-call | flops 2415919104 | bytes 9000000 | tf_op jit(solution)/shard_map/pallas_call | solution.py:130
  14.7 0.6 collective-permute-start.4
  15.3 5.4 %shard_map.106.own_ref = f32[8,128,384]{2,1,0:T(8,128)S(1)} custom-call(s32[4]{0:T(128)S(1)} %pad_add_fusion.place_ref, bf16[2,512,384]{2,1,0:T(8,128)(2,1)S(1)} %copy-done, f32[128,16,512]{2,1,0:T(8,128)} %refs_0_.9, f32[128,16,512]{2,1,0:T(8,128)} %refs_1_.9, f32[128,16,512]{2,1,0:T(8,128)} %refs_2_.9), custom_call_target="tpu_custom_call" | custom-call | flops 1207959552 | bytes 9000000 | tf_op jit(solution)/shard_map/pallas_call | solution.py:130
  20.7 1.2 copy-done.10
  21.9 4.3 %shard_map.108 = (f32[1920,128]{1,0:T(8,128)S(1)}, f32[1280,128]{1,0:T(8,128)S(1)}) custom-call(s32[4]{0:T(128)S(1)} %pad_add_fusion.place_ref, f32[8,128,384]{2,1,0:T(8,128)S(1)} %shard_map.106.own_ref, f32[8,128,384]{2,1,0:T(8,128)} %copy-done.10, bf16[2,2,2,160,128]{4,3,2,1,0:T(8,128)(2,1)S(1)} %copy-done.18), custom_call_target="tpu_custom_call" | custom-call | flops 1509949440 | bytes 7000000 | tf_op jit(solution)/shard_map/pallas_call | solution.py:196
  26.2 1.2 copy-done.21
  27.4 6.7 %shard_map.105 = (f32[3200,128]{1,0:T(8,128)}, f32[1920,128]{1,0:T(8,128)S(1)}, f32[1280,128]{1,0:T(8,128)S(1)}) custom-call(s32[4]{0:T(128)S(1)} %pad_add_fusion.place_ref, f32[8,128,384]{2,1,0:T(8,128)S(1)} %get-tuple-element.26.own_ref, f32[8,128,384]{2,1,0:T(8,128)} %copy-done.21, bf16[2,2,2,160,128]{4,3,2,1,0:T(8,128)(2,1)S(1)} %copy-done.18), custom_call_target="tpu_custom_call" | custom-call | flops 3019898880 | bytes 7000000 | tf_op jit(solution)/shard_map/pallas_call | solution.py:196
  34.0 0.9 copy-done.16
  35.0 1.2 pad_maximum_fusion
  36.2 8.4 %all-to-all-start.1 = ((f32[16,2,5,2,8,128]{5,4,3,2,1,0:T(8,128)}), f32[16,2,5,2,8,128]{5,4,3,2,1,0:T(8,128)}, u32[]{:S(2)}, u32[]{:S(2)}) async-start(f32[16,2,5,2,8,128]{5,4,3,2,1,0:T(8,128)} %pad_maximum_fusion), calls=%async_computation.1 | async-start | bytes 2621440 | tf_op jit(solution)/shard_map/all_to_all | solution.py:312
  44.6 8.8 %shard_map.102 = (f32[8,128,384]{2,1,0:T(8,128)}, f32[8,128,384]{2,1,0:T(8,128)S(1)}) custom-call(s32[4]{0:T(128)S(1)} %pad_add_fusion.place_ref, bf16[2,512,384]{2,1,0:T(8,128)(2,1)S(1)} %copy-done.1, f32[128,16,512]{2,1,0:T(8,128)} %refs_0_.9, f32[128,16,512]{2,1,0:T(8,128)} %refs_1_.9, f32[128,16,512]{2,1,0:T(8,128)} %refs_2_.9), custom_call_target="tpu_custom_call" | custom-call | flops 2415919104 | bytes 9000000 | tf_op jit(solution)/shard_map/pallas_call | solution.py:130
  53.4 1.1 copy-done.8
  54.6 0.5 collective-permute-start.10
  55.1 0.9 collective-permute-start.9
  56.0 4.6 %shard_map.109 = f32[3200,128]{1,0:T(8,128)} custom-call(s32[4]{0:T(128)S(1)} %pad_add_fusion.place_ref, f32[8,128,384]{2,1,0:T(8,128)S(1)} %shard_map.106.own_ref, f32[8,128,384]{2,1,0:T(8,128)S(1)} %copy-done.11, bf16[2,2,2,160,128]{4,3,2,1,0:T(8,128)(2,1)S(1)} %copy-done.18), custom_call_target="tpu_custom_call" | custom-call | flops 1509949440 | bytes 7000000 | tf_op jit(solution)/shard_map/pallas_call | solution.py:196
  60.6 3.3 %collective-permute-start.11 = (f32[16,5,5,8,128]{4,3,2,1,0:T(8,128)}, f32[16,5,5,8,128]{4,3,2,1,0:T(8,128)}, u32[]{:S(2)}, u32[]{:S(2)}) collective-permute-start(f32[16,5,5,8,128]{4,3,2,1,0:T(8,128)} %bitcast.34), channel_id=1, source_target_pairs={{0,64},{16,80},{64,0},{80,16},{1,65},{17,81},{65,1},{81,17},{2,66}... | collective-permute-start | bytes 4915208 | tf_op jit(solution)/shard_map/ppermute | solution.py:308
  63.9 16.1 %collective-permute-done.10 = f32[16,5,3,8,128]{4,3,2,1,0:T(8,128)S(1)} collective-permute-done((f32[16,5,3,8,128]{4,3,2,1,0:T(8,128)S(1)}, f32[16,5,3,8,128]{4,3,2,1,0:T(8,128)S(1)}, u32[]{:S(2)}, u32[]{:S(2)}) %collective-permute-start.10) | collective-permute-done | bytes 983072 | tf_op jit(solution)/shard_map/ppermute | solution.py:308
  80.0 1.1 add.14
  81.0 7.2 %all-to-all-start.3 = ((f32[16,5,3,8,128]{4,3,2,1,0:T(8,128)}), f32[16,5,3,8,128]{4,3,2,1,0:T(8,128)S(1)}, u32[]{:S(2)}, u32[]{:S(2)}) async-start(f32[16,5,3,8,128]{4,3,2,1,0:T(8,128)} %add.14), calls=%async_computation.3 | async-start | bytes 1966080 | tf_op jit(solution)/shard_map/all_to_all | solution.py:312
  88.3 8.5 %shard_map.100 = (f32[8,128,384]{2,1,0:T(8,128)}, f32[8,128,384]{2,1,0:T(8,128)S(1)}) custom-call(s32[4]{0:T(128)S(1)} %pad_add_fusion.place_ref, bf16[2,512,384]{2,1,0:T(8,128)(2,1)S(1)} %copy-done.1, f32[128,16,512]{2,1,0:T(8,128)} %refs_0_.9, f32[128,16,512]{2,1,0:T(8,128)} %refs_1_.9, f32[128,16,512]{2,1,0:T(8,128)} %refs_2_.9), custom_call_target="tpu_custom_call" | custom-call | flops 2415919104 | bytes 9000000 | tf_op jit(solution)/shard_map/pallas_call | solution.py:130
  96.8 1.2 copy-done.12
  98.0 7.2 %shard_map.103 = (f32[3200,128]{1,0:T(8,128)}, f32[3200,128]{1,0:T(8,128)}) custom-call(s32[4]{0:T(128)S(1)} %pad_add_fusion.place_ref, f32[8,128,384]{2,1,0:T(8,128)S(1)} %copy-done.9, f32[8,128,384]{2,1,0:T(8,128)} %collective-permute-done.2.recv_ref, bf16[2,2,2,160,128]{4,3,2,1,0:T(8,128)(2,1)S(1)} %copy-done.18), custom_call_target="tpu_custom_call" | custom-call | flops 3019898880 | bytes 7000000 | tf_op jit(solution)/shard_map/pallas_call | solution.py:196
  105.2 2.2 collective-permute-start.8
  107.3 9.8 %collective-permute-done.11 = f32[16,5,5,8,128]{4,3,2,1,0:T(8,128)} collective-permute-done((f32[16,5,5,8,128]{4,3,2,1,0:T(8,128)}, f32[16,5,5,8,128]{4,3,2,1,0:T(8,128)}, u32[]{:S(2)}, u32[]{:S(2)}) %collective-permute-start.11) | collective-permute-done | bytes 1638432 | tf_op jit(solution)/shard_map/ppermute | solution.py:308
  117.1 2.9 %add.15 = f32[16,5,5,8,128]{4,3,2,1,0:T(8,128)} add(f32[16,5,5,8,128]{4,3,2,1,0:T(8,128)S(1)} %bitcast.31, f32[16,5,5,8,128]{4,3,2,1,0:T(8,128)} %collective-permute-done.11) | non-fusion elementwise | flops 409600 | bytes 4915200 | tf_op jit(solution)/shard_map/add | solution.py:340
  120.0 1.0 copy-done.4
  120.9 7.4 %all-to-all-start.4 = ((f32[16,5,5,8,128]{4,3,2,1,0:T(8,128)}), f32[16,5,5,8,128]{4,3,2,1,0:T(8,128)S(1)}, u32[]{:S(2)}, u32[]{:S(2)}) async-start(f32[16,5,5,8,128]{4,3,2,1,0:T(8,128)} %add.15), calls=%async_computation.4 | async-start | bytes 3276800 | tf_op jit(solution)/shard_map/all_to_all | solution.py:312
  128.3 0.5 collective-permute-start.3
  128.8 1.0 copy-done.19
  129.8 7.1 %shard_map.101 = (f32[3200,128]{1,0:T(8,128)}, f32[3200,128]{1,0:T(8,128)}) custom-call(s32[4]{0:T(128)S(1)} %pad_add_fusion.place_ref, f32[8,128,384]{2,1,0:T(8,128)S(1)} %copy-done.13, f32[8,128,384]{2,1,0:T(8,128)} %collective-permute-done.recv_ref, bf16[2,2,2,160,128]{4,3,2,1,0:T(8,128)(2,1)S(1)} %copy-done.19), custom_call_target="tpu_custom_call" | custom-call | flops 3019898880 | bytes 7000000 | tf_op jit(solution)/shard_map/pallas_call | solution.py:196
  136.8 15.4 %collective-permute-done.8 = f32[16,5,5,8,128]{4,3,2,1,0:T(8,128)} collective-permute-done((f32[16,5,5,8,128]{4,3,2,1,0:T(8,128)}, f32[16,5,5,8,128]{4,3,2,1,0:T(8,128)}, u32[]{:S(2)}, u32[]{:S(2)}) %collective-permute-start.8) | collective-permute-done | bytes 1638432 | tf_op jit(solution)/shard_map/ppermute | solution.py:308
  152.3 3.3 %add.13 = f32[16,5,5,8,128]{4,3,2,1,0:T(8,128)} add(f32[16,5,5,8,128]{4,3,2,1,0:T(8,128)} %bitcast.32, f32[16,5,5,8,128]{4,3,2,1,0:T(8,128)} %collective-permute-done.8) | non-fusion elementwise | flops 409600 | bytes 4915200 | tf_op jit(solution)/shard_map/add | solution.py:340
  155.5 7.2 %all-to-all-start.2 = ((f32[16,5,5,8,128]{4,3,2,1,0:T(8,128)}), f32[16,5,5,8,128]{4,3,2,1,0:T(8,128)S(1)}, u32[]{:S(2)}, u32[]{:S(2)}) async-start(f32[16,5,5,8,128]{4,3,2,1,0:T(8,128)} %add.13), calls=%async_computation.2 | async-start | bytes 3276800 | tf_op jit(solution)/shard_map/all_to_all | solution.py:312
  162.7 23.8 %collective-permute-done.3 = f32[16,5,5,8,128]{4,3,2,1,0:T(8,128)} collective-permute-done((f32[16,5,5,8,128]{4,3,2,1,0:T(8,128)}, f32[16,5,5,8,128]{4,3,2,1,0:T(8,128)}, u32[]{:S(2)}, u32[]{:S(2)}) %collective-permute-start.3) | collective-permute-done | bytes 1638432 | tf_op jit(solution)/shard_map/ppermute | solution.py:308
  186.6 3.3 %add.12 = f32[16,5,5,8,128]{4,3,2,1,0:T(8,128)} add(f32[16,5,5,8,128]{4,3,2,1,0:T(8,128)} %collective-permute-done.1, f32[16,5,5,8,128]{4,3,2,1,0:T(8,128)} %collective-permute-done.3) | non-fusion elementwise | flops 409600 | bytes 4915200 | tf_op jit(solution)/shard_map/add | solution.py:340
  189.9 1.1 copy-done.2
  191.0 7.2 %all-to-all-start = ((f32[16,5,5,8,128]{4,3,2,1,0:T(8,128)}), f32[16,5,5,8,128]{4,3,2,1,0:T(8,128)S(1)}, u32[]{:S(2)}, u32[]{:S(2)}) async-start(f32[16,5,5,8,128]{4,3,2,1,0:T(8,128)} %add.12), calls=%async_computation | async-start | bytes 3276800 | tf_op jit(solution)/shard_map/all_to_all | solution.py:312
  198.3 1.4 slice_bitcast_fusion
  199.7 0.7 collective-permute-start.7
  200.4 4.9 %shard_map.110.refs_1_ = f32[10,320,320]{2,1,0:T(8,128)} custom-call(s32[4]{0:T(128)S(1)} %pad_add_fusion.place_ref, bf16[2,320,256]{2,1,0:T(8,128)(2,1)S(1)} %copy-done.6, f32[16,5,5,8,128]{4,3,2,1,0:T(8,128)S(1)} %all-to-all-done.4.refs_0_), custom_call_target="tpu_custom_call" | custom-call | flops 1572864000 | bytes 15000000 | tf_op jit(solution)/shard_map/pallas_call | solution.py:285
  205.3 4.6 %shard_map.111.refs_1_ = f32[10,320,320]{2,1,0:T(8,128)} custom-call(s32[4]{0:T(128)S(1)} %pad_add_fusion.place_ref, bf16[2,320,256]{2,1,0:T(8,128)(2,1)S(1)} %copy-done.6, f32[16,5,3,8,128]{4,3,2,1,0:T(8,128)S(1)} %copy-done.5, f32[10,320,320]{2,1,0:T(8,128)} %shard_map.110.refs_1_), custom_call_target="tpu_custom_call", output_to_operand_aliasing={{}: (3, {})} | custom-call | flops 943718400 | bytes 9000000 | tf_op jit(solution)/shard_map/pallas_call | solution.py:285
  209.9 6.1 %shard_map.112.refs_2_ = f32[10,320,320]{2,1,0:T(8,128)} custom-call(s32[4]{0:T(128)S(1)} %pad_add_fusion.place_ref, bf16[2,320,256]{2,1,0:T(8,128)(2,1)S(1)} %copy-done.7, f32[16,5,5,8,128]{4,3,2,1,0:T(8,128)S(1)} %copy-done.3, f32[10,320,320]{2,1,0:T(8,128)} %shard_map.111.refs_1_), custom_call_target="tpu_custom_call", output_to_operand_aliasing={{}: (3, {})} | custom-call | flops 1572864000 | bytes 15000000 | tf_op jit(solution)/shard_map/pallas_call | solution.py:285
  216.0 1.1 collective-permute-done.7.refs_1_
  217.1 3.8 %shard_map.113.refs_1_ = f32[10,320,320]{2,1,0:T(8,128)} custom-call(s32[4]{0:T(128)S(1)} %pad_add_fusion.place_ref, bf16[2,320,256]{2,1,0:T(8,128)(2,1)S(1)} %copy-done.6, f32[16,5,2,8,128]{4,3,2,1,0:T(8,128)S(1)} %collective-permute-done.6.refs_0_, f32[16,5,2,8,128]{4,3,2,1,0:T(8,128)S(1)} %collective-permute-done.7.refs_1_, ...), custom_call_target="tpu_custom_call", output_to_operand_aliasing={{}: (4, {})} | custom-call | flops 629145600 | bytes 6000000 | tf_op jit(solution)/shard_map/pallas_call | solution.py:285
  220.9 6.1 %shard_map.114 = f32[10,320,320]{2,1,0:T(8,128)} custom-call(s32[4]{0:T(128)S(1)} %pad_add_fusion.place_ref, bf16[2,320,256]{2,1,0:T(8,128)(2,1)S(1)} %copy-done.7, f32[16,5,5,8,128]{4,3,2,1,0:T(8,128)S(1)} %all-to-all-done.refs_0_, f32[10,320,320]{2,1,0:T(8,128)} %shard_map.113.refs_1_), custom_call_target="tpu_custom_call", output_to_operand_aliasing={{}: (3, {})} | custom-call | flops 1572864000 | bytes 15000000 | tf_op jit(solution)/shard_map/pallas_call | solution.py:285
  (52 shorter events, 0.2 us)
Async XLA Ops:
  0.1 1.1 copy-start
  6.6 14.1 %collective-permute-start.5 = (f32[8,128,384]{2,1,0:T(8,128)S(1)}, f32[8,128,384]{2,1,0:T(8,128)S(1)}, u32[]{:S(2)}, u32[]{:S(2)}) collective-permute-start(f32[8,128,384]{2,1,0:T(8,128)S(1)} %shard_map.107), channel_id=1, source_target_pairs={{0,32},{32,0},{1,33},{33,1},{2,34},{34,2},{3,35},{35,3},{4,36},{36... | collective-permute-start | bytes 4718600 | tf_op jit(solution)/shard_map/ppermute | solution.py:328
  14.7 7.2 %copy-start.18 = (bf16[2,2,2,160,128]{4,3,2,1,0:T(8,128)(2,1)S(1)}, bf16[2,2,2,160,128]{4,3,2,1,0:T(8,128)(2,1)}, u32[]{:S(2)}) copy-start(bf16[2,2,2,160,128]{4,3,2,1,0:T(8,128)(2,1)} %constant.33.clone.table_ref) | copy-start | bytes 983044
  14.7 11.4 %collective-permute-start.4 = (f32[8,128,384]{2,1,0:T(8,128)S(1)}, f32[8,128,384]{2,1,0:T(8,128)S(1)}, u32[]{:S(2)}, u32[]{:S(2)}) collective-permute-start(f32[8,128,384]{2,1,0:T(8,128)S(1)} %get-tuple-element.27), channel_id=1, source_target_pairs={{0,32},{32,0},{1,33},{33,1},{2,34},{34,2},{3,35},{35,3},{4,36},{36... | collective-permute-start | bytes 4718600 | tf_op jit(solution)/shard_map/ppermute | solution.py:328
  20.7 1.2 copy-start.10
  26.2 7.9 %copy-start.14 = (f32[1920,128]{1,0:T(8,128)}, f32[1920,128]{1,0:T(8,128)S(1)}, u32[]{:S(2)}) copy-start(f32[1920,128]{1,0:T(8,128)S(1)} %get-tuple-element.33) | copy-start | bytes 2949124
  26.2 1.2 copy-start.21
  34.0 0.9 copy-start.16
  36.2 8.4 %copy-start.1 = (bf16[2,512,384]{2,1,0:T(8,128)(2,1)S(1)}, bf16[2,512,384]{2,1,0:T(8,128)(2,1)}, u32[]{:S(2)}) copy-start(bf16[2,512,384]{2,1,0:T(8,128)(2,1)} %constant.34.clone.table_ref) | copy-start | bytes 2359300
  36.2 44.9 %all-to-all-start.1 = ((f32[16,2,5,2,8,128]{5,4,3,2,1,0:T(8,128)}), f32[16,2,5,2,8,128]{5,4,3,2,1,0:T(8,128)}, u32[]{:S(2)}, u32[]{:S(2)}) async-start(f32[16,2,5,2,8,128]{5,4,3,2,1,0:T(8,128)} %pad_maximum_fusion), calls=%async_computation.1 | async-start | bytes 2621440 | tf_op jit(solution)/shard_map/all_to_all | solution.py:312
  44.6 10.0 %copy-start.15 = (f32[1920,128]{1,0:T(8,128)S(1)}, f32[1920,128]{1,0:T(8,128)}, u32[]{:S(2)}) copy-start(f32[1920,128]{1,0:T(8,128)} %copy-done.14) | copy-start | bytes 2949124
  44.6 10.5 %copy-start.17 = (f32[1920,128]{1,0:T(8,128)S(1)}, f32[1920,128]{1,0:T(8,128)}, u32[]{:S(2)}) copy-start(f32[1920,128]{1,0:T(8,128)} %copy-done.16) | copy-start | bytes 2949124
  44.6 11.3 %copy-start.11 = (f32[8,128,384]{2,1,0:T(8,128)S(1)}, f32[8,128,384]{2,1,0:T(8,128)}, u32[]{:S(2)}) copy-start(f32[8,128,384]{2,1,0:T(8,128)} %copy-done.10) | copy-start | bytes 4718596
  53.4 1.1 copy-start.8
  54.6 43.4 %collective-permute-start.2 = (f32[8,128,384]{2,1,0:T(8,128)}, f32[8,128,384]{2,1,0:T(8,128)}, u32[]{:S(2)}, u32[]{:S(2)}) collective-permute-start(f32[8,128,384]{2,1,0:T(8,128)} %get-tuple-element.24), channel_id=1, source_target_pairs={{0,32},{32,0},{1,33},{33,1},{2,34},{34,2},{3,35},{35,3},{4,36},{36... | collective-permute-start | bytes 4718600 | tf_op jit(solution)/shard_map/ppermute | solution.py:328
  54.6 25.4 %collective-permute-start.10 = (f32[16,5,3,8,128]{4,3,2,1,0:T(8,128)S(1)}, f32[16,5,3,8,128]{4,3,2,1,0:T(8,128)S(1)}, u32[]{:S(2)}, u32[]{:S(2)}) collective-permute-start(f32[16,5,3,8,128]{4,3,2,1,0:T(8,128)S(1)} %bitcast.29), channel_id=1, source_target_pairs={{0,80},{16,64},{64,16},{80,0},{1,81},{17,65},{65,17},{81,1},{2,82}... | collective-permute-start | bytes 2949128 | tf_op jit(solution)/shard_map/ppermute | solution.py:308
  55.1 24.9 %collective-permute-start.9 = (f32[16,5,3,8,128]{4,3,2,1,0:T(8,128)S(1)}, f32[16,5,3,8,128]{4,3,2,1,0:T(8,128)S(1)}, u32[]{:S(2)}, u32[]{:S(2)}) collective-permute-start(f32[16,5,3,8,128]{4,3,2,1,0:T(8,128)S(1)} %bitcast.30), channel_id=1, source_target_pairs={{0,16},{16,0},{64,80},{80,64},{1,17},{17,1},{65,81},{81,65},{2,18}... | collective-permute-start | bytes 2949128 | tf_op jit(solution)/shard_map/ppermute | solution.py:308
  60.6 56.5 %collective-permute-start.11 = (f32[16,5,5,8,128]{4,3,2,1,0:T(8,128)}, f32[16,5,5,8,128]{4,3,2,1,0:T(8,128)}, u32[]{:S(2)}, u32[]{:S(2)}) collective-permute-start(f32[16,5,5,8,128]{4,3,2,1,0:T(8,128)} %bitcast.34), channel_id=1, source_target_pairs={{0,64},{16,80},{64,0},{80,16},{1,65},{17,81},{65,1},{81,17},{2,66}... | collective-permute-start | bytes 4915208 | tf_op jit(solution)/shard_map/ppermute | solution.py:308
  81.0 38.9 %all-to-all-start.3 = ((f32[16,5,3,8,128]{4,3,2,1,0:T(8,128)}), f32[16,5,3,8,128]{4,3,2,1,0:T(8,128)S(1)}, u32[]{:S(2)}, u32[]{:S(2)}) async-start(f32[16,5,3,8,128]{4,3,2,1,0:T(8,128)} %add.14), calls=%async_computation.3 | async-start | bytes 1966080 | tf_op jit(solution)/shard_map/all_to_all | solution.py:312
  88.3 9.7 %copy-start.9 = (f32[8,128,384]{2,1,0:T(8,128)S(1)}, f32[8,128,384]{2,1,0:T(8,128)}, u32[]{:S(2)}) copy-start(f32[8,128,384]{2,1,0:T(8,128)} %copy-done.8) | copy-start | bytes 4718596
  96.7 1.2 copy-start.12
  98.0 30.8 %collective-permute-start = (f32[8,128,384]{2,1,0:T(8,128)}, f32[8,128,384]{2,1,0:T(8,128)}, u32[]{:S(2)}, u32[]{:S(2)}) collective-permute-start(f32[8,128,384]{2,1,0:T(8,128)} %get-tuple-element.21), channel_id=1, source_target_pairs={{0,32},{32,0},{1,33},{33,1},{2,34},{34,2},{3,35},{35,3},{4,36},{36... | collective-permute-start | bytes 4718600 | tf_op jit(solution)/shard_map/ppermute | solution.py:328
  98.0 19.1 %copy-start.20 = (f32[3200,128]{1,0:T(8,128)S(1)}, f32[3200,128]{1,0:T(8,128)}, u32[]{:S(2)}) copy-start(f32[3200,128]{1,0:T(8,128)} %get-tuple-element.34) | copy-start | bytes 4915204
  105.2 47.1 %collective-permute-start.8 = (f32[16,5,5,8,128]{4,3,2,1,0:T(8,128)}, f32[16,5,5,8,128]{4,3,2,1,0:T(8,128)}, u32[]{:S(2)}, u32[]{:S(2)}) collective-permute-start(f32[16,5,5,8,128]{4,3,2,1,0:T(8,128)} %bitcast.35), channel_id=1, source_target_pairs={{0,64},{16,80},{64,0},{80,16},{1,65},{17,81},{65,1},{81,17},{2,66}... | collective-permute-start | bytes 4915208 | tf_op jit(solution)/shard_map/ppermute | solution.py:308
  120.0 1.0 copy-start.4
  120.9 7.8 %copy-start.13 = (f32[8,128,384]{2,1,0:T(8,128)S(1)}, f32[8,128,384]{2,1,0:T(8,128)}, u32[]{:S(2)}) copy-start(f32[8,128,384]{2,1,0:T(8,128)} %copy-done.12) | copy-start | bytes 4718596
  120.9 34.6 %all-to-all-start.4 = ((f32[16,5,5,8,128]{4,3,2,1,0:T(8,128)}), f32[16,5,5,8,128]{4,3,2,1,0:T(8,128)S(1)}, u32[]{:S(2)}, u32[]{:S(2)}) async-start(f32[16,5,5,8,128]{4,3,2,1,0:T(8,128)} %add.15), calls=%async_computation.4 | async-start | bytes 3276800 | tf_op jit(solution)/shard_map/all_to_all | solution.py:312
  128.3 58.3 %collective-permute-start.3 = (f32[16,5,5,8,128]{4,3,2,1,0:T(8,128)}, f32[16,5,5,8,128]{4,3,2,1,0:T(8,128)}, u32[]{:S(2)}, u32[]{:S(2)}) collective-permute-start(f32[16,5,5,8,128]{4,3,2,1,0:T(8,128)} %bitcast.33), channel_id=1, source_target_pairs={{0,80},{16,64},{64,16},{80,0},{1,81},{17,65},{65,17},{81,1},{2,82}... | collective-permute-start | bytes 4915208 | tf_op jit(solution)/shard_map/ppermute | solution.py:308
  128.8 1.0 copy-start.19
  136.8 49.8 %collective-permute-start.1 = (f32[16,5,5,8,128]{4,3,2,1,0:T(8,128)}, f32[16,5,5,8,128]{4,3,2,1,0:T(8,128)}, u32[]{:S(2)}, u32[]{:S(2)}) collective-permute-start(f32[16,5,5,8,128]{4,3,2,1,0:T(8,128)} %bitcast.36), channel_id=1, source_target_pairs={{0,16},{16,0},{64,80},{80,64},{1,17},{17,1},{65,81},{81,65},{2,18}... | collective-permute-start | bytes 4915208 | tf_op jit(solution)/shard_map/ppermute | solution.py:308
  155.5 34.4 %all-to-all-start.2 = ((f32[16,5,5,8,128]{4,3,2,1,0:T(8,128)}), f32[16,5,5,8,128]{4,3,2,1,0:T(8,128)S(1)}, u32[]{:S(2)}, u32[]{:S(2)}) async-start(f32[16,5,5,8,128]{4,3,2,1,0:T(8,128)} %add.13), calls=%async_computation.2 | async-start | bytes 3276800 | tf_op jit(solution)/shard_map/all_to_all | solution.py:312
  189.9 1.2 copy-start.2
  191.0 29.8 %all-to-all-start = ((f32[16,5,5,8,128]{4,3,2,1,0:T(8,128)}), f32[16,5,5,8,128]{4,3,2,1,0:T(8,128)S(1)}, u32[]{:S(2)}, u32[]{:S(2)}) async-start(f32[16,5,5,8,128]{4,3,2,1,0:T(8,128)} %add.12), calls=%async_computation | async-start | bytes 3276800 | tf_op jit(solution)/shard_map/all_to_all | solution.py:312
  198.2 2.1 copy-start.6
  199.7 17.4 %collective-permute-start.7 = (f32[16,5,2,8,128]{4,3,2,1,0:T(8,128)S(1)}, f32[16,5,2,8,128]{4,3,2,1,0:T(8,128)S(1)}, u32[]{:S(2)}, u32[]{:S(2)}) collective-permute-start(f32[16,5,2,8,128]{4,3,2,1,0:T(8,128)S(1)} %get-tuple-element.35), channel_id=1, source_target_pairs={{0,80},{16,64},{64,16},{80,0},{1,81},{17,65},{65,17},{81,1},{2,82}... | collective-permute-start | bytes 1966088 | tf_op jit(solution)/shard_map/ppermute | solution.py:308
  200.4 4.9 %copy-start.5 = (f32[16,5,3,8,128]{4,3,2,1,0:T(8,128)S(1)}, f32[16,5,3,8,128]{4,3,2,1,0:T(8,128)}, u32[]{:S(2)}) copy-start(f32[16,5,3,8,128]{4,3,2,1,0:T(8,128)} %copy-done.4) | copy-start | bytes 2949124
  200.4 16.7 %collective-permute-start.6 = (f32[16,5,2,8,128]{4,3,2,1,0:T(8,128)S(1)}, f32[16,5,2,8,128]{4,3,2,1,0:T(8,128)S(1)}, u32[]{:S(2)}, u32[]{:S(2)}) collective-permute-start(f32[16,5,2,8,128]{4,3,2,1,0:T(8,128)S(1)} %get-tuple-element.36), channel_id=1, source_target_pairs={{0,16},{16,0},{64,80},{80,64},{1,17},{17,1},{65,81},{81,65},{2,18}... | collective-permute-start | bytes 1966088 | tf_op jit(solution)/shard_map/ppermute | solution.py:308
  205.3 4.6 %copy-start.3 = (f32[16,5,5,8,128]{4,3,2,1,0:T(8,128)S(1)}, f32[16,5,5,8,128]{4,3,2,1,0:T(8,128)}, u32[]{:S(2)}) copy-start(f32[16,5,5,8,128]{4,3,2,1,0:T(8,128)} %copy-done.2) | copy-start | bytes 4915204
  205.3 4.6 %copy-start.7 = (bf16[2,320,256]{2,1,0:T(8,128)(2,1)S(1)}, bf16[2,320,256]{2,1,0:T(8,128)(2,1)}, u32[]{:S(2)}) copy-start(bf16[2,320,256]{2,1,0:T(8,128)(2,1)} %constant.36.clone.table_ref) | copy-start | bytes 983044
